TPU v7x, 32 devices: a whole 2x2x4 slice. The times are simulated.
32 devices in a mesh: tm: 4 (over x, core), space: 8 (over z, y).
Axes of the slice: x: 2, y: 2, z: 4, core: 2. Of those that a mesh axis runs over, the one named last changes fastest.
Arguments:
- iterate: float32 [64, 16, 3, 4096], P('space', 'tm'), may hold values from -6 to 6
- forcing: float32 [64, 16, 3, 4096], P('space', 'tm'), may hold values from -6 to 6
- initial_velocity: float32 [64, 3, 4096], P('space'), may hold values from -6 to 6
- viscosity: float32 [64, 4096], P('space'), may hold values from 0.1 to 1
- peclet: float32 [64, 3, 4096], P('space'), may hold values from -0.9 to 0.9
- live_patch_mask: int32 [64], P('space'), may hold values from 0 to 1, as said below
- neighbour_holder: int32 [64, 6], P('space'), may hold values from -1 to 7, as said below
- neighbour_slot: int32 [64, 6], P('space'), may hold values from -1 to 7, as said below
Outputs:
- corrected_velocity: float32 [64, 16, 3, 4096], P('space', 'tm')
- corrected_residual: float32 [64, 16, 3, 4096], P('space', 'tm')
Inputs may be any that keep to these rules, and one draw needn't show every extreme that they name: `live_patch_mask`: on each index of space the live slots (1) come first; their count is 2 to 8, and in every draw some two indices j and j + 4 have all 8 slots live. `neighbour_holder`: the patches of one index s of space are the blocks of one aligned 2x2x2 octant; the octant's position is read from the bits of s: bit b of s is bit b div 3 of coordinate b mod 3, except that where a coordinate has two bits its lower bit is complemented when its higher bit is 1; slot p lies at offsets (p mod 2, p div 2 mod 2, p div 4); the entry is -1 where no live patch lies across the face or the slot is dead; the relation is symmetric across opposite faces; the live patches of one index face those of another given index across at most 4 faces, exactly 4 for some pair in every draw. `neighbour_slot`: -1 exactly where neighbour_holder is -1.
All inputs are finite; a program needn't handle non-finite values.
Results may differ from a plain program's by a relative error of at most 0.0003.
Values sent between devices are 32-bit elements; how exact they have to be, the bound alone decides.
No kernel may reach another device: no remote copies, remote signals or barrier semaphores. Data moves between devices by JAX's collectives and lax.ppermute only.
A program may use at most 192 MiB of HBM per device.

v0:
```python
import jax
import jax.numpy as jnp
from jax import lax
from jax.sharding import PartitionSpec as P

WINDOW_SLICES = 16
BLOCK_EDGE = 16
SWEEPS = 5
FCAP = 4


STEP_DURATION = 0.5
ALPHA_SCALE = 0.1
HIGHEST_PRECISION = lax.Precision.HIGHEST


def shifted(value, axis, steps):
    count = lax.axis_size(axis)
    initial, last = (max(0, -steps), min(count, count - steps))
    return lax.ppermute(value, axis, [(source, source + steps) for source in range(initial, last)])


def face_masks(place_count):
    levels = place_count.bit_length() - 1
    return [[bit_index] for bit_index in range(levels)]


def face_routes(neighbour_holder, neighbour_slot, peer_ids, own_index):
    owners = neighbour_holder.reshape(-1)
    slot_numbers = neighbour_slot.reshape(-1)
    face_total = owners.shape[0]
    block_count = peer_ids.shape[0]
    face_codes = jnp.arange(face_total, dtype=jnp.int32)
    face_side = face_codes % 6
    across = jnp.maximum(slot_numbers, 0) * 6 + face_side + 1 - 2 * (face_side % 2)
    remote = (owners >= 0) & (owners != own_index)
    same_peer = remote[:, None] & remote[None, :] & (owners[:, None] == owners[None, :])
    send_rank = jnp.sum(same_peer & (across[None, :] < across[:, None]), axis=1)
    arrive_rank = jnp.sum(same_peer & (face_codes[None, :] < face_codes[:, None]), axis=1)
    matched = remote[:, None] & (owners[:, None] == peer_ids[None, :])
    block_ids = jnp.arange(block_count, dtype=jnp.int32)
    block_of = jnp.sum(jnp.where(matched, block_ids[None, :], 0), axis=1)
    covered = jnp.any(matched, axis=1)
    targets = jnp.arange(block_count * FCAP, dtype=jnp.int32)
    send_pick = (
        covered[None, :] & (block_of[None, :] * FCAP + send_rank[None, :] == targets[:, None])
    ).astype(jnp.float32)
    column = jnp.where(remote, block_of * FCAP + arrive_rank, block_count * FCAP + across)
    present = owners >= 0
    columns = jnp.arange(block_count * FCAP + face_total, dtype=jnp.int32)
    collect_pick = (present[:, None] & (column[:, None] == columns[None, :])).astype(jnp.float32)
    return (send_pick, collect_pick)


def neighbour_faces(flat_field, exchange_paths):
    send_pick, collect_pick, mask_list = exchange_paths
    slot_count, channels, cell_count = flat_field.shape
    width = channels * BLOCK_EDGE * BLOCK_EDGE
    cube_view = flat_field.reshape(slot_count, channels, BLOCK_EDGE, BLOCK_EDGE, BLOCK_EDGE)
    layers = jnp.stack(
        [
            cube_view[:, :, 0],
            cube_view[:, :, -1],
            cube_view[:, :, :, 0],
            cube_view[:, :, :, -1],
            cube_view[:, :, :, :, 0],
            cube_view[:, :, :, :, -1],
        ],
        axis=1,
    )
    layers = layers.reshape(slot_count * 6, width)
    outgoing = jnp.dot(send_pick, layers, precision=HIGHEST_PRECISION).reshape(-1, FCAP, width)
    incoming = lax.all_to_all(outgoing, "space", split_axis=0, concat_axis=0, tiled=True)
    sources = jnp.concatenate([incoming.reshape(-1, width), layers], axis=0)
    ghost_faces = jnp.dot(collect_pick, sources, precision=HIGHEST_PRECISION)
    return ghost_faces.reshape(slot_count, 6, channels, BLOCK_EDGE * BLOCK_EDGE)


def neighbour_sum(flat_field, ghost_faces, peclet):
    slot_count, channels, cell_count = flat_field.shape
    face_cells = BLOCK_EDGE * BLOCK_EDGE
    cell_index = jnp.arange(cell_count, dtype=jnp.int32)
    second_coord = cell_index // BLOCK_EDGE % BLOCK_EDGE
    third_coord = cell_index % BLOCK_EDGE

    def spread_second(layer):
        return jnp.broadcast_to(
            layer.reshape(slot_count, channels, BLOCK_EDGE, 1, BLOCK_EDGE),
            (slot_count, channels, BLOCK_EDGE, BLOCK_EDGE, BLOCK_EDGE),
        ).reshape(slot_count, channels, cell_count)

    def spread_third(layer):
        return jnp.broadcast_to(
            layer.reshape(slot_count, channels, face_cells, 1),
            (slot_count, channels, face_cells, BLOCK_EDGE),
        ).reshape(slot_count, channels, cell_count)

    x_upper = jnp.concatenate([flat_field[:, :, face_cells:], ghost_faces[:, 1]], axis=2)
    x_lower = jnp.concatenate([ghost_faces[:, 0], flat_field[:, :, :-face_cells]], axis=2)
    y_upper = jnp.where(
        second_coord == BLOCK_EDGE - 1,
        spread_second(ghost_faces[:, 3]),
        jnp.roll(flat_field, -BLOCK_EDGE, axis=2),
    )
    y_lower = jnp.where(
        second_coord == 0,
        spread_second(ghost_faces[:, 2]),
        jnp.roll(flat_field, BLOCK_EDGE, axis=2),
    )
    z_upper = jnp.where(
        third_coord == BLOCK_EDGE - 1,
        spread_third(ghost_faces[:, 5]),
        jnp.roll(flat_field, -1, axis=2),
    )
    z_lower = jnp.where(
        third_coord == 0, spread_third(ghost_faces[:, 4]), jnp.roll(flat_field, 1, axis=2)
    )
    x_peclet = peclet[:, 0:1]
    y_peclet = peclet[:, 1:2]
    z_peclet = peclet[:, 2:3]
    summed = (1.0 - x_peclet) * x_upper + (1.0 + x_peclet) * x_lower
    summed = summed + (1.0 - y_peclet) * y_upper + (1.0 + y_peclet) * y_lower
    summed = summed + (1.0 - z_peclet) * z_upper + (1.0 + z_peclet) * z_lower
    return summed


def compute_residual(
    velocity_state, forcing, initial_velocity, viscosity, peclet, live_indicator, exchange_paths
):
    slot_count, local_slices, components, cell_count = velocity_state.shape
    final_slice = velocity_state[:, -1]
    earlier = shifted(final_slice, "tm", 1)
    earlier = jnp.where(lax.axis_index("tm") == 0, initial_velocity, earlier)
    prior_slice = jnp.concatenate([earlier[:, None], velocity_state[:, :-1]], axis=1)
    flat_field = velocity_state.reshape(slot_count, local_slices * components, cell_count)
    ghost_faces = neighbour_faces(flat_field, exchange_paths)
    adjacent_sum = neighbour_sum(flat_field, ghost_faces, peclet).reshape(velocity_state.shape)
    operator_result = viscosity[:, None, None, :] * (6.0 * velocity_state - adjacent_sum)
    return (
        forcing - (velocity_state - prior_slice) / STEP_DURATION - operator_result
    ) * live_indicator[:, None, None, None]


def spectral_tables():
    times = jnp.arange(WINDOW_SLICES, dtype=jnp.int32)
    groups = WINDOW_SLICES // 2
    modes = jnp.arange(groups, dtype=jnp.int32)
    product = modes[:, None] * times[None, :] % WINDOW_SLICES
    angles = 2.0 * jnp.pi * product.astype(jnp.float32) / WINDOW_SLICES
    ramp = times.astype(jnp.float32) / WINDOW_SLICES
    twisted = jnp.power(ALPHA_SCALE, ramp)
    untwisted = jnp.power(ALPHA_SCALE, -ramp) / WINDOW_SLICES
    cosine = jnp.cos(angles)
    sine = jnp.sin(angles)
    root = ALPHA_SCALE ** (1.0 / WINDOW_SLICES)
    mode_angle = 2.0 * jnp.pi * modes.astype(jnp.float32) / WINDOW_SLICES
    shift_a = (1.0 - root * jnp.cos(mode_angle)) / STEP_DURATION
    shift_imag = root * jnp.sin(mode_angle) / STEP_DURATION
    alternating = (1 - 2 * (times % 2)).astype(jnp.float32)
    first_mode = (modes == 0)[:, None]
    second_row = jnp.where(first_mode, alternating[None, :], -sine)
    forward = jnp.stack([cosine, second_row], axis=1) * twisted[None, None, :]
    doubled = jnp.where(first_mode, 1.0, 2.0)
    back_second = jnp.where(first_mode, alternating[None, :], -2.0 * sine)
    inverse = jnp.stack([(doubled * cosine).T, back_second.T], axis=2) * untwisted[:, None, None]
    shift_b = jnp.where(modes == 0, (1.0 + root) / STEP_DURATION, shift_a)
    shift_imag = jnp.where(modes == 0, 0.0, shift_imag)
    return (forward, inverse, shift_a, shift_b, shift_imag)


def time_blocks(values):
    return lax.all_to_all(values, "tm", split_axis=0, concat_axis=0, tiled=True)


def spectral_blocks(values):
    return lax.all_to_all(values, "tm", split_axis=0, concat_axis=0, tiled=True)


def body(
    iterate,
    forcing,
    initial_velocity,
    viscosity,
    peclet,
    live_patch_mask,
    neighbour_holder,
    neighbour_slot,
):
    time_devices = lax.axis_size("tm")
    place_count = lax.axis_size("space")
    own_place = lax.axis_index("space")
    mask_list = face_masks(place_count)
    peer_ids = jnp.arange(place_count, dtype=jnp.int32)
    send_pick, collect_pick = face_routes(neighbour_holder, neighbour_slot, peer_ids, own_place)
    exchange_paths = (send_pick, collect_pick, mask_list)
    live_indicator = live_patch_mask.astype(jnp.float32)
    slot_count, local_slices, components, cell_count = iterate.shape
    slot_lead = slot_count // time_devices
    residual_value = compute_residual(
        iterate, forcing, initial_velocity, viscosity, peclet, live_indicator, exchange_paths
    )
    forward, inverse, shift_a, shift_b, shift_imag = spectral_tables()
    per_device = forward.shape[0] // time_devices
    regrouped = time_blocks(
        residual_value.reshape(time_devices, slot_lead, local_slices, components, cell_count)
    )
    forward_table = forward.reshape(time_devices, per_device, 2, time_devices, local_slices)
    spectrum = jnp.einsum(
        "agrtj,tsjcx->asgrcx", forward_table, regrouped, precision=HIGHEST_PRECISION
    )
    spectrum = spectral_blocks(spectrum).reshape(slot_count, per_device, 2, components, cell_count)
    first_group = lax.axis_index("tm") * per_device

    def own_modes(values):
        return lax.dynamic_slice_in_dim(values, first_group, per_device).reshape(
            1, per_device, 1, 1
        )

    diffusion = 6.0 * viscosity[:, None, None, :]
    diag_a = own_modes(shift_a) + diffusion
    diag_b = own_modes(shift_b) + diffusion
    coupling = own_modes(shift_imag)
    determinant = diag_a * diag_b + coupling * coupling
    source_real = spectrum[:, :, 0]
    source_imag = spectrum[:, :, 1]
    total_real = source_real
    total_imag = source_imag
    correction = spectrum
    for sweep_index in range(SWEEPS):
        if sweep_index > 0:
            flat_field = correction.reshape(slot_count, per_device * 2 * components, cell_count)
            ghost_faces = neighbour_faces(flat_field, exchange_paths)
            adjacent_sum = neighbour_sum(flat_field, ghost_faces, peclet).reshape(correction.shape)
            total_real = source_real + viscosity[:, None, None, :] * adjacent_sum[:, :, 0]
            total_imag = source_imag + viscosity[:, None, None, :] * adjacent_sum[:, :, 1]
        real_component = (diag_b * total_real + coupling * total_imag) / determinant
        imaginary_component = (diag_a * total_imag - coupling * total_real) / determinant
        correction = jnp.stack([real_component, imaginary_component], axis=2)
    returned = spectral_blocks(
        correction.reshape(time_devices, slot_lead, per_device, 2, components, cell_count)
    )
    inverse_table = inverse.reshape(time_devices, local_slices, time_devices, per_device, 2)
    update = jnp.einsum("tjagr,asgrcx->tsjcx", inverse_table, returned, precision=HIGHEST_PRECISION)
    update = time_blocks(update).reshape(iterate.shape)
    corrected_velocity = iterate + update
    corrected_residual = compute_residual(
        corrected_velocity,
        forcing,
        initial_velocity,
        viscosity,
        peclet,
        live_indicator,
        exchange_paths,
    )
    return (corrected_velocity, corrected_residual)


def solution(mesh):
    return jax.shard_map(
        body,
        mesh=mesh,
        in_specs=(
            P("space", "tm", None, None),
            P("space", "tm", None, None),
            P("space", None, None),
            P("space", None),
            P("space", None, None),
            P("space"),
            P("space", None),
            P("space", None),
        ),
        out_specs=(P("space", "tm", None, None), P("space", "tm", None, None)),
        check_vma=False,
    )
```

profile of v0, /device:TPU:0, one launch (start us, length us, event | category | flops | bytes accessed | tf_op | source)
XLA Modules:
  0.0 1305.8 jit_solution(7236250363456896547)
XLA Ops:
  20.6 21.4 %fusion.194 = (f32[8,12,16,16,1]{4,3,2,0,1:T(8,128)}, f32[8,12,16,16,1]{4,3,2,0,1:T(8,128)}) fusion(f32[8,12,16,16,16]{4,3,2,0,1:T(8,128)} %reshape_reshape.18), kind=kLoop, calls=%fused_computation.363 | loop fusion | bytes 393216 | tf_op jit(solution)/shard_map/slice | solution.py:67
  137.8 12.0 reshape.821
  157.2 12.0 reshape.822
  176.5 12.4 reshape.823
  204.0 18.9 %all-to-all-done.1 = f32[4,2,4,3,4096]{4,2,3,1,0:T(4,128)S(1)} async-done(((f32[4,2,4,3,4096]{4,2,3,1,0:T(4,128)}), f32[4,2,4,3,4096]{4,2,3,1,0:T(4,128)S(1)}, u32[]{:S(2)}, u32[]{:S(2)}) %all-to-all-start.1) | async-done | bytes 1572896 | tf_op jit(solution)/shard_map/all_to_all | solution.py:172
  233.4 19.0 %all-to-all-done.2 = f32[4,2,2,2,3,4096]{5,3,2,4,1,0:T(2,128)S(1)} async-done(((f32[4,2,2,2,3,4096]{5,3,2,4,1,0:T(2,128)}), f32[4,2,2,2,3,4096]{5,3,2,4,1,0:T(2,128)S(1)}, u32[]{:S(2)}, u32[]{:S(2)}) %all-to-all-start.2) | async-done | bytes 1572896 | tf_op jit(solution)/shard_map/all_to_all | solution.py:176
  265.4 21.5 %fusion.191 = (f32[8,12,16,16,1]{4,3,2,0,1:T(8,128)}, f32[8,12,16,16,1]{4,3,2,0,1:T(8,128)}) fusion(f32[8,12,16,16,16]{4,3,2,0,1:T(8,128)} %reshape_reshape.19), kind=kLoop, calls=%fused_computation.360 | loop fusion | bytes 393216 | tf_op jit(solution)/shard_map/slice | solution.py:67
  398.6 12.0 reshape.831
  437.3 12.1 reshape.833
  465.2 21.5 %fusion.188 = (f32[8,12,16,16,1]{4,3,2,0,1:T(8,128)}, f32[8,12,16,16,1]{4,3,2,0,1:T(8,128)}) fusion(f32[8,12,16,16,16]{4,3,2,0,1:T(8,128)} %reshape_reshape.20), kind=kLoop, calls=%fused_computation.357 | loop fusion | bytes 393216 | tf_op jit(solution)/shard_map/slice | solution.py:67
  596.6 12.0 reshape.839
  635.3 12.1 reshape.841
  663.2 21.5 %fusion.185 = (f32[8,12,16,16,1]{4,3,2,0,1:T(8,128)}, f32[8,12,16,16,1]{4,3,2,0,1:T(8,128)}) fusion(f32[8,12,16,16,16]{4,3,2,0,1:T(8,128)} %reshape_reshape.21), kind=kLoop, calls=%fused_computation.354 | loop fusion | bytes 393216 | tf_op jit(solution)/shard_map/slice | solution.py:67
  794.5 12.0 reshape.847
  813.8 12.0 reshape.848
  833.2 12.1 reshape.849
  861.1 21.5 %fusion.182 = (f32[8,12,16,16,1]{4,3,2,0,1:T(8,128)}, f32[8,12,16,16,1]{4,3,2,0,1:T(8,128)}) fusion(f32[8,12,16,16,16]{4,3,2,0,1:T(8,128)} %reshape_reshape.22), kind=kLoop, calls=%fused_computation.351 | loop fusion | bytes 393216 | tf_op jit(solution)/shard_map/slice | solution.py:67
  992.4 12.0 reshape.855
  1031.1 12.1 reshape.857
  1061.2 19.3 %all-to-all-done.7 = f32[4,2,2,2,3,4096]{5,3,2,4,1,0:T(2,128)S(1)} async-done(((f32[4,2,2,2,3,4096]{5,3,2,4,1,0:T(2,128)}), f32[4,2,2,2,3,4096]{5,3,2,4,1,0:T(2,128)S(1)}, u32[]{:S(2)}, u32[]{:S(2)}) %all-to-all-start.7) | async-done | bytes 1572896 | tf_op jit(solution)/shard_map/all_to_all | solution.py:176
  1085.7 23.0 %all_to_all.50 = f32[4,2,4,3,4096]{4,2,3,1,0:T(4,128)S(1)} all-to-all(f32[4,2,4,3,4096]{4,2,3,1,0:T(4,128)S(1)} %bitcast.467), channel_id=1, replica_groups=mesh['tm'=4,'space'=8] {'tm'}, dimensions={0} | all-to-all | bytes 3145728 | tf_op jit(solution)/shard_map/all_to_all | solution.py:172
  1127.2 21.4 %fusion.179 = (f32[8,12,16,16,1]{4,3,2,0,1:T(8,128)}, f32[8,12,16,16,1]{4,3,2,0,1:T(8,128)}) fusion(f32[8,12,16,16,16]{4,3,2,0,1:T(8,128)} %reshape_reshape.23), kind=kLoop, calls=%fused_computation.348 | loop fusion | bytes 393216 | tf_op jit(solution)/shard_map/slice | solution.py:67
  1264.2 12.0 reshape.865
  1283.6 12.1 reshape.866
  (571 shorter events, 925.3 us)
Async XLA Ops:
  1.4 111.7 %copy-start.109 = (pred[48]{0:T(512)(128)(4,1)}, pred[48]{0:T(512)(128)(4,1)S(1)}, u32[]{:S(2)}) copy-start(pred[48]{0:T(512)(128)(4,1)S(1)} %get-tuple-element.175) | copy-start | bytes 148
  20.6 21.4 %copy-start.122 = (s32[8,6]{1,0:T(8,128)S(1)}, s32[8,6]{1,0:T(8,128)}, u32[]{:S(2)}) copy-start(s32[8,6]{1,0:T(8,128)} %param.15) | copy-start | bytes 580
  81.8 31.4 %copy-start.107 = (s32[48]{0:T(128)}, s32[48]{0:T(128)S(1)}, u32[]{:S(2)}) copy-start(s32[48]{0:T(128)S(1)} %get-tuple-element.177) | copy-start | bytes 580
  83.0 30.0 %all-to-all-start = ((f32[8,4,3072]{2,1,0:T(4,128)}), f32[8,4,3072]{2,1,0:T(4,128)S(1)}, u32[]{:S(2)}, u32[]{:S(2)}) async-start(f32[8,4,3072]{2,1,0:T(4,128)} %fusion.176), calls=%async_computation | async-start | bytes 786432 | tf_op jit(solution)/shard_map/all_to_all | solution.py:73
  91.1 20.1 %collective-permute-start = (f32[8,3,4096]{2,0,1:T(8,128)}, f32[8,3,4096]{2,0,1:T(8,128)}, u32[]{:S(2)}, u32[]{:S(2)}) collective-permute-start(f32[8,3,4096]{2,0,1:T(8,128)} %slice_bitcast_fusion.1), channel_id=1, source_target_pairs={{0,8},{8,16},{16,24},{1,9},{9,17},{17,25},{2,10},{10,18},{18,26},{... | collective-permute-start | bytes 1179656 | tf_op jit(solution)/shard_map/ppermute | solution.py:20
  102.1 86.9 %copy-start.12 = (f32[8,4096]{1,0:T(8,128)}, f32[8,4096]{1,0:T(8,128)S(1)}, u32[]{:S(2)}) copy-start(f32[8,4096]{1,0:T(8,128)S(1)} %get-tuple-element.163) | copy-start | bytes 393220
  102.1 86.9 %copy-start.18 = (f32[8,4096]{1,0:T(8,128)}, f32[8,4096]{1,0:T(8,128)S(1)}, u32[]{:S(2)}) copy-start(f32[8,4096]{1,0:T(8,128)S(1)} %get-tuple-element.164) | copy-start | bytes 393220
  102.1 86.9 %copy-start.24 = (f32[8,4096]{1,0:T(8,128)}, f32[8,4096]{1,0:T(8,128)S(1)}, u32[]{:S(2)}) copy-start(f32[8,4096]{1,0:T(8,128)S(1)} %get-tuple-element.165) | copy-start | bytes 393220
  102.1 86.9 %copy-start.30 = (f32[8,4096]{1,0:T(8,128)}, f32[8,4096]{1,0:T(8,128)S(1)}, u32[]{:S(2)}) copy-start(f32[8,4096]{1,0:T(8,128)S(1)} %get-tuple-element.166) | copy-start | bytes 393220
  102.2 86.9 %copy-start.36 = (f32[8,4096]{1,0:T(8,128)}, f32[8,4096]{1,0:T(8,128)S(1)}, u32[]{:S(2)}) copy-start(f32[8,4096]{1,0:T(8,128)S(1)} %get-tuple-element.167) | copy-start | bytes 393220
  199.3 23.6 %copy-start.125 = (f32[4,4]{1,0:T(4,128)S(1)}, f32[4,4]{1,0:T(4,128)}, u32[]{:S(2)}) copy-start(f32[4,4]{1,0:T(4,128)} %fusion.153) | copy-start | bytes 196
  199.3 23.6 %all-to-all-start.1 = ((f32[4,2,4,3,4096]{4,2,3,1,0:T(4,128)}), f32[4,2,4,3,4096]{4,2,3,1,0:T(4,128)S(1)}, u32[]{:S(2)}, u32[]{:S(2)}) async-start(f32[4,2,4,3,4096]{4,2,3,1,0:T(4,128)} %bitcast.29), calls=%async_computation.1 | async-start | bytes 3145728 | tf_op jit(solution)/shard_map/all_to_all | solution.py:172
  228.2 24.1 %all-to-all-start.2 = ((f32[4,2,2,2,3,4096]{5,3,2,4,1,0:T(2,128)}), f32[4,2,2,2,3,4096]{5,3,2,4,1,0:T(2,128)S(1)}, u32[]{:S(2)}, u32[]{:S(2)}) async-start(f32[4,2,2,2,3,4096]{5,3,2,4,1,0:T(2,128)} %copy.1023), calls=%async_computation.2 | async-start | bytes 3145728 | tf_op jit(solution)/shard_map/all_to_all | solution.py:176
  233.3 23.7 %copy-start.2 = (f32[8,2,4096]{2,0,1:T(8,128)}, f32[8,2,4096]{2,0,1:T(8,128)S(1)}, u32[]{:S(2)}) copy-start(f32[8,2,4096]{2,0,1:T(8,128)S(1)} %get-tuple-element.169) | copy-start | bytes 786436
  233.4 23.7 %copy-start.7 = (f32[8,2,4096]{2,0,1:T(8,128)}, f32[8,2,4096]{2,0,1:T(8,128)S(1)}, u32[]{:S(2)}) copy-start(f32[8,2,4096]{2,0,1:T(8,128)S(1)} %get-tuple-element.170) | copy-start | bytes 786436
  352.6 17.5 %all-to-all-start.3 = ((f32[8,4,3072]{2,1,0:T(4,128)}), f32[8,4,3072]{2,1,0:T(4,128)}, u32[]{:S(2)}, u32[]{:S(2)}) async-start(f32[8,4,3072]{2,1,0:T(4,128)} %fusion.174), calls=%async_computation.3 | async-start | bytes 786432 | tf_op jit(solution)/shard_map/all_to_all | solution.py:73
  552.4 15.7 %all-to-all-start.4 = ((f32[8,4,3072]{2,1,0:T(4,128)}), f32[8,4,3072]{2,1,0:T(4,128)}, u32[]{:S(2)}, u32[]{:S(2)}) async-start(f32[8,4,3072]{2,1,0:T(4,128)} %fusion.172), calls=%async_computation.4 | async-start | bytes 786432 | tf_op jit(solution)/shard_map/all_to_all | solution.py:73
  750.4 15.6 %all-to-all-start.5 = ((f32[8,4,3072]{2,1,0:T(4,128)}), f32[8,4,3072]{2,1,0:T(4,128)}, u32[]{:S(2)}, u32[]{:S(2)}) async-start(f32[8,4,3072]{2,1,0:T(4,128)} %fusion.170), calls=%async_computation.5 | async-start | bytes 786432 | tf_op jit(solution)/shard_map/all_to_all | solution.py:73
  948.3 15.7 %all-to-all-start.6 = ((f32[8,4,3072]{2,1,0:T(4,128)}), f32[8,4,3072]{2,1,0:T(4,128)}, u32[]{:S(2)}, u32[]{:S(2)}) async-start(f32[8,4,3072]{2,1,0:T(4,128)} %fusion.168), calls=%async_computation.6 | async-start | bytes 786432 | tf_op jit(solution)/shard_map/all_to_all | solution.py:73
  1057.0 23.6 %all-to-all-start.7 = ((f32[4,2,2,2,3,4096]{5,3,2,4,1,0:T(2,128)}), f32[4,2,2,2,3,4096]{5,3,2,4,1,0:T(2,128)S(1)}, u32[]{:S(2)}, u32[]{:S(2)}) async-start(f32[4,2,2,2,3,4096]{5,3,2,4,1,0:T(2,128)} %copy.1093), calls=%async_computation.7 | async-start | bytes 3145728 | tf_op jit(solution)/shard_map/all_to_all | solution.py:176
  1085.6 23.0 %copy-start.1 = (f32[8,4,3,4096]{3,1,2,0:T(4,128)S(1)}, f32[8,4,3,4096]{3,1,2,0:T(4,128)}, u32[]{:S(2)}) copy-start(f32[8,4,3,4096]{3,1,2,0:T(4,128)} %param.8) | copy-start | bytes 4718596
  1204.9 15.3 %copy-start.110 = (pred[48]{0:T(512)(128)(4,1)S(1)}, pred[48]{0:T(512)(128)(4,1)}, u32[]{:S(2)}) copy-start(pred[48]{0:T(512)(128)(4,1)} %copy-done.109) | copy-start | bytes 148
  1204.9 15.1 %all-to-all-start.9 = ((f32[8,4,3072]{2,1,0:T(4,128)}), f32[8,4,3072]{2,1,0:T(4,128)S(1)}, u32[]{:S(2)}, u32[]{:S(2)}) async-start(f32[8,4,3072]{2,1,0:T(4,128)} %fusion.166), calls=%async_computation.9 | async-start | bytes 786432 | tf_op jit(solution)/shard_map/all_to_all | solution.py:73
  1208.7 2.8 collective-permute-start.1
  (116 other events, 997.4 us)
where the time goes:
time: 1320 us; the launch traced here: 1310 us
  local copies, waits for them, and re-layouts  1050 us (80%)
  waiting for transfers between devices  102 us (8%)
  other arithmetic  62.8 us (5%)
  starting transfers between devices  45.5 us (3%)
  blocking collectives  23 us (2%)
  matrix products  22.5 us (2%)
    slice x12, local copies, waits for them, and re-layouts, neighbour_faces(): cube_view[:, :, :, :, -1]  198 us
    reshape x12, local copies, waits for them, and re-layouts, spread_third(): return jnp.broadcast_to(layer.reshape(slot_count, channels, face_cells, 1...  145 us
    reshape x12, local copies, waits for them, and re-layouts, spread_second(): return jnp.broadcast_to(layer.reshape(slot_count, channels, BLOCK_EDGE, 1...  144 us
    broadcast_in_dim x30, local copies, waits for them, and re-layouts, spread_third(): jnp.broadcast_to(layer.reshape(slot_count, channels, face_cells, 1), (slo...  88.4 us
    broadcast_in_dim x24, local copies, waits for them, and re-layouts, spread_second(): jnp.broadcast_to(layer.reshape(slot_count, channels, BLOCK_EDGE, 1, BLOCK...  74.2 us
    slice x6, local copies, waits for them, and re-layouts, neighbour_faces(): cube_view[:, :, :, :, 0]  69.2 us
    reshape x12, local copies, waits for them, and re-layouts, neighbour_faces(): layers = layers.reshape(slot_count * 6, width)  69 us
    unnamed x291, local copies, waits for them, and re-layouts  49.4 us
  transfers between devices with their start and end apart: 11, of which 9 were waited for; matrix products, arithmetic and copies ran while one was open for 3% of the time, Pallas kernels for 0%

commit v1 on v0

v1 whole, which is shorter than its diff:
```python
import jax
import jax.numpy as jnp
from jax import lax
from jax.experimental import pallas as pl
from jax.experimental.pallas import tpu as pltpu
from jax.sharding import PartitionSpec as P

EDGE = 16
LANES = 128
CHUNKS = 32
COMPONENTS = 3
ALPHA_SCALE = 0.1
WINDOW_SLICES = 16
SWEEPS = 5
XP, XM, YP, YM, ZP, ZM, XG, YG, ZG, Q, INV, K0 = range(12)
CORE, CHIP, SIDE_X, SIDE_Y, HOLD = range(5)
F32 = jnp.float32


def iota(shape, axis):
    return lax.broadcasted_iota(jnp.int32, shape, axis)


def tile_shape(*lead):
    return lead + (2, EDGE, LANES)


def call(kernel, flags, ins, outs, scratch=(), flops=2_000_000, name=None):
    vmem = pl.BlockSpec(memory_space=pltpu.VMEM)
    return pl.pallas_call(
        kernel,
        in_specs=[pl.BlockSpec(memory_space=pltpu.SMEM)] + [vmem] * len(ins),
        out_specs=[vmem] * len(outs),
        out_shape=[jax.ShapeDtypeStruct(s, F32) for s in outs],
        scratch_shapes=list(scratch),
        compiler_params=pltpu.CompilerParams(vmem_limit_bytes=24 * 1024 * 1024),
        cost_estimate=pl.CostEstimate(flops=flops, bytes_accessed=1_000_000, transcendentals=0),
        name=name,
    )(flags, *ins)


class Shape:
    def __init__(self, slots, local, n_time, places):
        self.slots = slots
        self.half = slots // 2
        self.local = local
        self.span = 2 * local
        self.chips = n_time // 2
        levels = places.bit_length() - 1
        self.bits = [[b for b in range(levels) if b % 3 == d] for d in range(3)]
        self.y_per = max(1, 8 // self.span)
        self.z_per = max(1, 16 // self.span)
        self.x_shape = (2 * COMPONENTS, self.span * 2, LANES)
        self.y_shape = (-(-2 // self.y_per) * COMPONENTS, EDGE, LANES)
        self.z_shape = tile_shape(-(-self.half // self.z_per) * COMPONENTS)
        self.x_count = len(self.bits[0])
        self.field = tile_shape(self.half, COMPONENTS, self.span)
        self.slice = tile_shape(self.half, COMPONENTS)


def position(place, bits):
    if len(bits) == 1:
        return place >> bits[0] & 1
    low, high = place >> bits[0] & 1, place >> bits[1] & 1
    return 2 * high + (low ^ high)


def exchange(sh, messages, n_time, places):
    axes = ("tm", "space")
    received = []
    x_out, y_out, inner_out, z_out = messages[:-3], messages[-3], messages[-2], messages[-1]

    def pairs(bit, bits, crossed):
        table = []
        for t in range(n_time):
            for s in range(places):
                here, there = position(s, bits), position(s ^ (1 << bit), bits)
                if abs(here - there) != 1:
                    continue
                if crossed and (there > here) != (t % 2 == 1):
                    continue
                target = t ^ 1 if crossed else t
                table.append((t * places + s, target * places + (s ^ (1 << bit))))
        return table

    z_in = lax.ppermute(z_out, axes, pairs(sh.bits[2][0], sh.bits[2], True))
    x_in = [
        lax.ppermute(x_out[i], axes, pairs(bit, sh.bits[0], False))
        for i, bit in enumerate(sh.bits[0])
    ]
    y_in = lax.ppermute(y_out, axes, pairs(sh.bits[1][0], sh.bits[1], False))
    inner_in = swap_cores(inner_out, n_time)
    return x_in + [y_in, inner_in, z_in]


def swap_cores(value, n_time):
    return lax.ppermute(value, "tm", [(t, t ^ 1) for t in range(n_time)])


def emit_messages(sh, flags, src, outs):
    core = flags[CORE]
    lane = iota((EDGE, LANES), 1)
    x_outs, y_out, inner_out, z_out = outs[:-3], outs[-3], outs[-2], outs[-1]
    side_y = flags[SIDE_Y]

    def comp_step(comp, _):
        for number, x_out in enumerate(x_outs):
            side = flags[SIDE_X] if number == 0 else 1 - flags[SIDE_X]
            for jj in range(2):
                for l in range(sh.span):
                    for h in range(2):
                        upper = src[2 * jj + 1, comp, l, h, EDGE - 1 : EDGE, :]
                        lower = src[2 * jj, comp, l, h, 0:1, :]
                        x_out[jj * COMPONENTS + comp, 2 * l + h : 2 * l + h + 1, :] = jnp.where(
                            side == 1, upper, lower
                        )
        group_of_lane = lane // EDGE
        for g in range(-(-2 // sh.y_per)):
            packed = jnp.zeros((EDGE, LANES), F32)
            for jj in range(g * sh.y_per, min(2, (g + 1) * sh.y_per)):
                for l in range(sh.span):
                    index = (jj % sh.y_per) * sh.span + l
                    layer = src[2 * side_y + jj, comp, l, side_y]
                    if index:
                        layer = pltpu.roll(layer, EDGE * index, 1)
                    packed = jnp.where(group_of_lane == (index + 7 * side_y) % 8, layer, packed)
            y_out[g * COMPONENTS + comp] = jnp.where(
                side_y == 1, pltpu.roll(packed, EDGE, 1), packed
            )
        within = lane % EDGE
        for g in range(-(-sh.half // sh.z_per)):
            for h in range(2):
                low = jnp.zeros((EDGE, LANES), F32)
                high = jnp.zeros((EDGE, LANES), F32)
                for j in range(g * sh.z_per, min(sh.half, (g + 1) * sh.z_per)):
                    for l in range(sh.span):
                        index = (j % sh.z_per) * sh.span + l
                        tile = src[j, comp, l, h]
                        here = within == index
                        shifted = pltpu.roll(tile, index, 1) if index else tile
                        low = jnp.where(here, shifted, low)
                        back = (index - EDGE + 1) % LANES
                        shifted = pltpu.roll(tile, back, 1) if back else tile
                        high = jnp.where(here, shifted, high)
                inner_out[g * COMPONENTS + comp, h] = jnp.where(core == 1, low, high)
                z_out[g * COMPONENTS + comp, h] = jnp.where(core == 1, high, low)
        return 0

    lax.fori_loop(0, COMPONENTS, comp_step, 0)


def neighbour_sum(sh, flags, coef, src, faces, z_ghost, j, comp, l):
    xs, y_in = faces[:-1], faces[-1]
    lane = iota((EDGE, LANES), 1)
    tiles = [src[j, comp, l, h] for h in range(2)]
    up = [pltpu.roll(v, LANES - EDGE, 1) for v in tiles]
    down = [pltpu.roll(v, EDGE, 1) for v in tiles]
    y_upper = [jnp.where(lane < LANES - EDGE, up[0], up[1]), up[1]]
    y_lower = [down[0], jnp.where(lane >= EDGE, down[1], down[0])]
    x_side, x_row = j % 2, j // 2
    y_side, y_row = j // 2, j % 2
    y_index = (y_row % sh.y_per) * sh.span + l
    y_group = y_in[(y_row // sh.y_per) * COMPONENTS + comp]
    if y_side == 1:
        y_ghost = [
            pltpu.roll(src[j ^ 2, comp, l, 1], EDGE, 1),
            pltpu.roll(y_group, (LANES - EDGE - EDGE * y_index) % LANES, 1)
            if (LANES - EDGE - EDGE * y_index) % LANES
            else y_group,
        ]
    else:
        y_ghost = [
            pltpu.roll(y_group, (-EDGE * y_index) % LANES, 1) if y_index else y_group,
            pltpu.roll(src[j ^ 2, comp, l, 0], LANES - EDGE, 1),
        ]
    z_index = (j % sh.z_per) * sh.span + l
    z_group = (j // sh.z_per) * COMPONENTS + comp
    result = []
    for h in range(2):
        v = tiles[h]
        total = coef[j, XP, h] * pltpu.roll(v, EDGE - 1, 0)
        total += coef[j, XM, h] * pltpu.roll(v, 1, 0)
        total += coef[j, YP, h] * y_upper[h]
        total += coef[j, YM, h] * y_lower[h]
        total += coef[j, ZP, h] * pltpu.roll(v, LANES - 1, 1)
        total += coef[j, ZM, h] * pltpu.roll(v, 1, 1)
        total += coef[j, YG, h] * y_ghost[h]
        low = z_ghost[0, z_group, h]
        low = pltpu.roll(low, LANES - z_index, 1) if z_index else low
        high = z_ghost[1, z_group, h]
        high = pltpu.roll(high, EDGE - 1 - z_index, 1) if z_index != EDGE - 1 else high
        total += coef[j, ZG, h] * jnp.where(lane % EDGE == 0, low, high)
        outer = x_row * COMPONENTS + comp
        row = slice(2 * l + h, 2 * l + h + 1)
        if len(xs) == 1:
            crossed = xs[0][outer, row, :]
        else:
            wanted = flags[SIDE_X] if x_side == 1 else 1 - flags[SIDE_X]
            crossed = jnp.where(wanted == 1, xs[0][outer, row, :], xs[1][outer, row, :])
        inside = EDGE - 1 if x_side == 1 else 0
        own = src[j ^ 1, comp, l, h, inside : inside + 1, :]
        first, last = (own, crossed) if x_side == 1 else (crossed, own)
        ghost = jnp.concatenate(
            [jnp.broadcast_to(first, (8, LANES)), jnp.broadcast_to(last, (8, LANES))], axis=0
        )
        total += coef[j, XG, h] * ghost
        result.append(total)
    return result


def place_z_ghost(flags, inner_in, z_in, z_ghost):
    core = flags[CORE]

    def step(g, _):
        inner, outer = inner_in[g], z_in[g]
        z_ghost[0, g] = jnp.where(core == 1, inner, outer)
        z_ghost[1, g] = jnp.where(core == 1, outer, inner)
        return 0

    lax.fori_loop(0, inner_in.shape[0], step, 0)


def rows_to_tiles(read, count, rows, write):
    for chunk in range(CHUNKS):
        rows[chunk * count : (chunk + 1) * count, :] = read(chunk)
    for i in range(count):
        for h in range(2):
            write(i, h, rows[pl.ds(h * count + i, EDGE, 2 * count), :])


def tiles_to_rows(tile, count, rows, write):
    for i in range(count):
        for h in range(2):
            rows[pl.ds(h * count + i, EDGE, 2 * count), :] = tile(i, h)
    for chunk in range(CHUNKS):
        write(chunk, rows[chunk * count : (chunk + 1) * count, :])


def coefficient_kernel(sh, flags, viscosity, peclet, initial, coef, first, rows, tiles):
    core = flags[CORE]
    chip = flags[CHIP]
    slots = sh.slots

    def unpack(source, kind):
        def write(i, h, value):
            tiles[kind, i, h] = value

        rows_to_tiles(lambda c: source(c), slots, rows, write)

    unpack(lambda c: viscosity[:, c * LANES : (c + 1) * LANES], 0)
    for d in range(3):
        unpack(lambda c, d=d: peclet[d, :, c * LANES : (c + 1) * LANES], 1 + d)
    for d in range(3):
        unpack(lambda c, d=d: initial[d, :, c * LANES : (c + 1) * LANES], 4 + d)

    lane = iota((EDGE, LANES), 1)
    row = iota((EDGE, LANES), 0)
    zero = jnp.zeros((EDGE, LANES), F32)

    def step(j, _):
        slot = core * sh.half + j
        hold = [flags[HOLD + j * 6 + face].astype(F32) for face in range(6)]
        for h in range(2):
            nu = tiles[0, slot, h]
            inverse = 2.0 + 6.0 * nu
            q = 2.0 / inverse
            scale = nu / inverse
            plus = [scale * (1.0 - tiles[1 + d, slot, h]) for d in range(3)]
            minus = [scale * (1.0 + tiles[1 + d, slot, h]) for d in range(3)]
            coef[j, XP, h] = jnp.where(row < EDGE - 1, plus[0], zero)
            coef[j, XM, h] = jnp.where(row > 0, minus[0], zero)
            coef[j, XG, h] = jnp.where(
                row == 0,
                minus[0] * hold[0],
                jnp.where(row == EDGE - 1, plus[0] * hold[1], zero),
            )
            if h == 0:
                coef[j, YP, h] = plus[1]
                coef[j, YM, h] = jnp.where(lane >= EDGE, minus[1], zero)
                coef[j, YG, h] = jnp.where(lane < EDGE, minus[1] * hold[2], zero)
            else:
                coef[j, YP, h] = jnp.where(lane < LANES - EDGE, plus[1], zero)
                coef[j, YM, h] = minus[1]
                coef[j, YG, h] = jnp.where(lane >= LANES - EDGE, plus[1] * hold[3], zero)
            within = lane % EDGE
            coef[j, ZP, h] = jnp.where(within < EDGE - 1, plus[2], zero)
            coef[j, ZM, h] = jnp.where(within > 0, minus[2], zero)
            coef[j, ZG, h] = jnp.where(
                within == 0,
                minus[2] * hold[4],
                jnp.where(within == EDGE - 1, plus[2] * hold[5], zero),
            )
            coef[j, Q, h] = q
            coef[j, INV, h] = inverse
            power = q
            for _ in range(sh.span.bit_length() - 1):
                power = power * power
            whole = power
            for _ in range(sh.chips.bit_length() - 1):
                whole = whole * whole
            weight = 1.0 / (1.0 - ALPHA_SCALE * whole)
            for back in range(1, sh.chips + 1):
                wrapped = jnp.where(chip < back, ALPHA_SCALE, 1.0)
                coef[j, K0 + back - 1, h] = weight * wrapped
                weight = weight * power
            for d in range(COMPONENTS):
                first[j, d, h] = tiles[4 + d, slot, h]
        return 0

    lax.fori_loop(0, sh.half, step, 0)


def gather_kernel(sh, flags, whole, other, field, last, *rest):
    rows = rest[-1]
    core = flags[CORE]

    def step(k, _):
        j, comp = k // COMPONENTS, k % COMPONENTS

        def own(i, h, value):
            field[j, comp, core * sh.local + i, h] = value

        def partner(i, h, value):
            field[j, comp, (1 - core) * sh.local + i, h] = value

        slot = core * sh.half + j
        rows_to_tiles(
            lambda c: whole[slot, comp, :, c * LANES : (c + 1) * LANES], sh.local, rows.at[0], own
        )
        rows_to_tiles(
            lambda c: other[j, comp, :, c * LANES : (c + 1) * LANES], sh.local, rows.at[1], partner
        )
        last[j, comp] = field[j, comp, sh.span - 1]
        return 0

    lax.fori_loop(0, sh.half * COMPONENTS, step, 0)
    emit_messages(sh, flags, field, rest[:-1])


def force_kernel(sh, flags, whole, other, field, rows):
    core = flags[CORE]

    def step(k, _):
        j, comp = k // COMPONENTS, k % COMPONENTS

        def own(i, h, value):
            field[j, comp, core * sh.local + i, h] = value

        def partner(i, h, value):
            field[j, comp, (1 - core) * sh.local + i, h] = value

        slot = core * sh.half + j
        rows_to_tiles(
            lambda c: whole[slot, comp, :, c * LANES : (c + 1) * LANES], sh.local, rows.at[0], own
        )
        rows_to_tiles(
            lambda c: other[j, comp, :, c * LANES : (c + 1) * LANES], sh.local, rows.at[1], partner
        )
        return 0

    lax.fori_loop(0, sh.half * COMPONENTS, step, 0)


def residual_kernel(sh, flags, coef, field, force, before, first, *rest):
    faces = rest[: sh.x_count + 1]
    inner_in, z_in, scaled, partial, last, z_ghost = rest[sh.x_count + 1 :]
    place_z_ghost(flags, inner_in, z_in, z_ghost)
    chip = flags[CHIP]
    for j in range(sh.half):
        live = flags[HOLD + 6 * sh.half + j].astype(F32)

        def comp_step(comp, _, j=j, live=live):
            prior = [jnp.where(chip == 0, first[j, comp, h], before[j, comp, h]) for h in range(2)]
            carry = [jnp.zeros((EDGE, LANES), F32)] * 2
            for l in range(sh.span):
                total = neighbour_sum(sh, flags, coef, field, faces, z_ghost, j, comp, l)
                for h in range(2):
                    q = coef[j, Q, h]
                    now = field[j, comp, l, h]
                    value = total[h] + (0.5 * q) * force[j, comp, l, h] - now + q * prior[h]
                    value = value * live
                    prior[h] = now
                    scaled[j, comp, l, h] = value
                    carry[h] = value + q * carry[h]
                    partial[j, comp, l, h] = carry[h]
            for h in range(2):
                last[j, comp, h] = carry[h]
            return 0

        lax.fori_loop(0, COMPONENTS, comp_step, 0)


def sweep_kernel(sh, flags, coef, field, scaled, *rest):
    faces = rest[: sh.x_count + 1]
    inner_in, z_in, partial, last, z_ghost = rest[sh.x_count + 1 :]
    place_z_ghost(flags, inner_in, z_in, z_ghost)
    for j in range(sh.half):

        def comp_step(comp, _, j=j):
            carry = [jnp.zeros((EDGE, LANES), F32)] * 2
            for l in range(sh.span):
                total = neighbour_sum(sh, flags, coef, field, faces, z_ghost, j, comp, l)
                for h in range(2):
                    carry[h] = scaled[j, comp, l, h] + total[h] + coef[j, Q, h] * carry[h]
                    partial[j, comp, l, h] = carry[h]
            for h in range(2):
                last[j, comp, h] = carry[h]
            return 0

        lax.fori_loop(0, COMPONENTS, comp_step, 0)


def incoming_slice(sh, coef, lasts, j, comp, h):
    total = coef[j, K0, h] * lasts[0][j, comp, h]
    for back in range(1, sh.chips):
        total += coef[j, K0 + back, h] * lasts[back][j, comp, h]
    return total


def close_kernel(sh, flags, coef, partial, *rest):
    lasts, (field, *messages) = rest[: sh.chips], rest[sh.chips :]

    def step(k, _):
        j, comp = k // COMPONENTS, k % COMPONENTS
        for h in range(2):
            q = coef[j, Q, h]
            term = incoming_slice(sh, coef, lasts, j, comp, h)
            for l in range(sh.span):
                term = q * term
                field[j, comp, l, h] = partial[j, comp, l, h] + term
        return 0

    lax.fori_loop(0, sh.half * COMPONENTS, step, 0)
    emit_messages(sh, flags, field, messages)


def velocity_kernel(sh, flags, velocity, field, keep, send, rows):
    core = flags[CORE]

    def step(k, _):
        j, comp = k // COMPONENTS, k % COMPONENTS
        for which, out in ((core, keep), (1 - core, send)):

            def tile(i, h, which=which):
                l = which * sh.local + i
                return velocity[j, comp, l, h] + field[j, comp, l, h]

            def write(c, value, out=out):
                out[j, comp, :, c * LANES : (c + 1) * LANES] = value

            tiles_to_rows(tile, sh.local, rows.at[0 if out is keep else 1], write)
        return 0

    lax.fori_loop(0, sh.half * COMPONENTS, step, 0)


def final_kernel(sh, flags, coef, field, scaled, *rest):
    lasts, rest = rest[: sh.chips], rest[sh.chips :]
    faces = rest[: sh.x_count + 1]
    inner_in, z_in, keep, send, z_ghost, hold, rows = rest[sh.x_count + 1 :]
    place_z_ghost(flags, inner_in, z_in, z_ghost)
    core = flags[CORE]
    chip = flags[CHIP]
    for j in range(sh.half):
        live = flags[HOLD + 6 * sh.half + j].astype(F32)

        def comp_step(comp, _, j=j, live=live):
            prior = [
                jnp.where(chip == 0, 0.0, incoming_slice(sh, coef, lasts, j, comp, h))
                for h in range(2)
            ]
            for l in range(sh.span):
                total = neighbour_sum(sh, flags, coef, field, faces, z_ghost, j, comp, l)
                for h in range(2):
                    now = field[j, comp, l, h]
                    value = scaled[j, comp, l, h] + total[h] - now + coef[j, Q, h] * prior[h]
                    prior[h] = now
                    hold[l, h] = value * (coef[j, INV, h] * live)
            for which, out in ((core, keep), (1 - core, send)):

                def tile(i, h, which=which):
                    return hold[which * sh.local + i, h]

                def write(c, value, out=out):
                    out[j, comp, :, c * LANES : (c + 1) * LANES] = value

                tiles_to_rows(tile, sh.local, rows.at[0 if out is keep else 1], write)
            return 0

        lax.fori_loop(0, COMPONENTS, comp_step, 0)


def bind(kernel, sh):
    def run(*refs):
        kernel(sh, *refs)

    return run


def body(
    iterate,
    forcing,
    initial_velocity,
    viscosity,
    peclet,
    live_patch_mask,
    neighbour_holder,
    neighbour_slot,
):
    n_time, places = lax.axis_size("tm"), lax.axis_size("space")
    slots, local = iterate.shape[:2]
    sh = Shape(slots, local, n_time, places)
    half = sh.half
    t, place = lax.axis_index("tm"), lax.axis_index("space")
    core, chip = t % 2, t // 2
    velocity = iterate.transpose(0, 2, 1, 3)
    force = forcing.transpose(0, 2, 1, 3)

    def partner_slots(value):
        return swap_cores(lax.dynamic_slice_in_dim(value, (1 - core) * half, half, 0), n_time)

    velocity_other = partner_slots(velocity)
    force_other = partner_slots(force)

    def side(bits):
        return 1 - position(place, bits) % 2

    held = lax.dynamic_slice_in_dim(neighbour_holder, core * half, half, 0) >= 0
    live = lax.dynamic_slice_in_dim(live_patch_mask, core * half, half, 0)
    flags = jnp.concatenate(
        [
            jnp.stack([core, chip, side(sh.bits[0]), side(sh.bits[1])]).astype(jnp.int32),
            held.astype(jnp.int32).reshape(-1),
            live.astype(jnp.int32),
        ]
    )
    rows = pltpu.VMEM((2, CHUNKS * local, LANES), F32)
    z_ghost = pltpu.VMEM((2,) + sh.z_shape, F32)
    messages = [sh.x_shape] * sh.x_count + [sh.y_shape, sh.z_shape, sh.z_shape]

    coef, first = call(
        bind(coefficient_kernel, sh),
        flags,
        [viscosity, peclet.transpose(1, 0, 2), initial_velocity.transpose(1, 0, 2)],
        [tile_shape(half, K0 + sh.chips), sh.slice],
        [pltpu.VMEM((CHUNKS * slots, LANES), F32), pltpu.VMEM(tile_shape(7, slots), F32)],
        name="coefficients",
    )
    field, last, *out = call(
        bind(gather_kernel, sh),
        flags,
        [velocity, velocity_other],
        [sh.field, sh.slice] + messages,
        [rows],
        name="gather",
    )
    before = lax.ppermute(last, "tm", [(a, a + 2) for a in range(n_time - 2)])
    faces = exchange(sh, out, n_time, places)
    (pushed,) = call(
        bind(force_kernel, sh), flags, [force, force_other], [sh.field], [rows], name="force"
    )
    scaled, partial, last = call(
        bind(residual_kernel, sh),
        flags,
        [coef, field, pushed, before, first] + faces,
        [sh.field, sh.field, sh.slice],
        [z_ghost],
        flops=8_000_000,
        name="residual",
    )

    def chip_ends(last):
        return [
            lax.ppermute(last, "tm", [(a, (a + 2 * back) % n_time) for a in range(n_time)])
            for back in range(1, sh.chips)
        ] + [last]

    correction = None
    for sweep in range(SWEEPS):
        if sweep > 0:
            partial, last = call(
                bind(sweep_kernel, sh),
                flags,
                [coef, correction, scaled] + faces,
                [sh.field, sh.slice],
                [z_ghost],
                flops=8_000_000,
                name="sweep",
            )
        ends = chip_ends(last)
        correction, *out = call(
            bind(close_kernel, sh),
            flags,
            [coef, partial] + ends,
            [sh.field] + messages,
            name="close",
        )
        faces = exchange(sh, out, n_time, places)
    native = (half, COMPONENTS, local, CHUNKS * LANES)
    keep, send = call(
        bind(velocity_kernel, sh),
        flags,
        [field, correction],
        [native, native],
        [rows],
        name="velocity",
    )

    def restore(keep, send):
        other = swap_cores(send, n_time)
        first_core = core == 0
        whole = jnp.concatenate(
            [jnp.where(first_core, keep, other), jnp.where(first_core, other, keep)], axis=0
        )
        return whole.transpose(0, 2, 1, 3)

    corrected_velocity = restore(keep, send)
    keep, send = call(
        bind(final_kernel, sh),
        flags,
        [coef, correction, scaled] + ends + faces,
        [native, native],
        [z_ghost, pltpu.VMEM(tile_shape(sh.span), F32), rows],
        flops=8_000_000,
        name="final",
    )
    return corrected_velocity, restore(keep, send)


def solution(mesh):
    return jax.shard_map(
        body,
        mesh=mesh,
        in_specs=(
            P("space", "tm", None, None),
            P("space", "tm", None, None),
            P("space", None, None),
            P("space", None),
            P("space", None, None),
            P("space"),
            P("space", None),
            P("space", None),
        ),
        out_specs=(P("space", "tm", None, None), P("space", "tm", None, None)),
        check_vma=False,
    )
```

time: 1320 us -> 136 us (0.10); the launches traced: 1310 us -> 135 us
  local copies, waits for them, and re-layouts: 1050 us -> 3.42 us
  waiting for transfers between devices: 102 us -> 44.2 us
  other arithmetic: 62.8 us -> 5.04 us
  Pallas kernels: 0 us -> 43.3 us
  blocking collectives: 23 us -> 0 us
  matrix products: 22.5 us -> 0 us
    slice x87 -> x0, local copies, waits for them, and re-layouts: 383 us -> none  [the longest x12 198 us: neighbour_faces(): cube_view[:, :, :, :, -1]]
    reshape x49 -> x1, local copies, waits for them, and re-layouts: 364 us -> 0.08 us  [body(): held.astype(jnp.int32).reshape(-1)]
    broadcast_in_dim x54 -> x0, local copies, waits for them, and re-layouts: 163 us -> none  [the longest x30 88.4 us: spread_third(): jnp.broadcast_to(layer.reshape(slot_count, channels, face_cells, 1), (slo...]
    all_to_all x9 -> x0, waiting for transfers between devices: 102 us -> none  [the longest x6 45.1 us: neighbour_faces(): lax.all_to_all(outgoing, 'space', split_axis=0, concat_axis=0, tiled=True)]
    another operation x19 -> x0, local copies, waits for them, and re-layouts: 79.6 us -> none  [the longest x6 41.8 us: neighbour_faces(): flat_field.reshape(slot_count, channels, BLOCK_EDGE, BLOCK_EDGE, BLOCK_EDGE)]
    unnamed x291 -> x14, local copies, waits for them, and re-layouts: 49.4 us -> 0.03 us
    ppermute x2 -> x34, waiting for transfers between devices: 0.2 us -> 44.2 us  [the longest x5 28.5 us: chip_ends(): lax.ppermute(last, 'tm', [(a, (a + 2 * back) % n_time) for a in range(n_t...]
    pallas_call x0 -> x15, Pallas kernels: none -> 43.3 us  [call(): pl.pallas_call(kernel, in_specs=[pl.BlockSpec(memory_space=pltpu.SMEM)] +...]
  transfers between devices with their start and end apart: 11 -> 34, of which waited for: 9 -> 15; matrix products, arithmetic and copies ran while one was open for 3% -> 1% of each run, Pallas kernels for 0% -> 8%
where the time goes in v1:
time: 136 us; the launch traced here: 135 us
  waiting for transfers between devices  44.2 us (32%)
  Pallas kernels  43.3 us (32%)
  starting transfers between devices  38.4 us (28%)
  other arithmetic  5.04 us (4%)
  local copies, waits for them, and re-layouts  3.42 us (3%)
    pallas_call x15, Pallas kernels, call(): pl.pallas_call(kernel, in_specs=[pl.BlockSpec(memory_space=pltpu.SMEM)] +...  43.3 us
    ppermute x5, waiting for transfers between devices, chip_ends(): lax.ppermute(last, 'tm', [(a, (a + 2 * back) % n_time) for a in range(n_t...  28.5 us
    ppermute x10, starting transfers between devices, swap_cores(): return lax.ppermute(value, 'tm', [(t, t ^ 1) for t in range(n_time)])  11.3 us
    ppermute x6, waiting for transfers between devices, exchange(): lax.ppermute(x_out[i], axes, pairs(bit, sh.bits[0], False))  7.91 us
    ppermute x6, starting transfers between devices, exchange(): lax.ppermute(x_out[i], axes, pairs(bit, sh.bits[0], False))  7.29 us
    ppermute x6, starting transfers between devices, exchange(): y_in = lax.ppermute(y_out, axes, pairs(sh.bits[1][0], sh.bits[1], False))  7.09 us
    ppermute x1, starting transfers between devices, body(): before = lax.ppermute(last, 'tm', [(a, a + 2) for a in range(n_time - 2)])  4.76 us
    ppermute x6, waiting for transfers between devices, exchange(): y_in = lax.ppermute(y_out, axes, pairs(sh.bits[1][0], sh.bits[1], False))  4.61 us
  transfers between devices with their start and end apart: 34, of which 15 were waited for; matrix products, arithmetic and copies ran while one was open for 1% of the time, Pallas kernels for 8%

profile of v1, /device:TPU:0, one launch (start us, length us, event | category | flops | bytes accessed | tf_op | source)
XLA Modules:
  0.0 135.3 jit_solution(14320198551262666237)
XLA Ops:
  0.7 2.2 %dynamic-slice_bitcast_fusion.1 = f32[4,3,4,4096]{3,2,1,0:T(4,128)} fusion(f32[8,4,3,4096]{3,1,2,0:T(4,128)} %param.8, s32[]{:T(128)S(6)} %select_n.53), kind=kLoop, calls=%fused_computation.3 | loop fusion | bytes 1572868 | tf_op jit(solution)/shard_map/dynamic_slice | solution.py:520
  5.7 2.9 %gather.1 = (f32[4,3,8,2,16,128]{5,4,3,2,1,0:T(8,128)S(1)}, f32[4,3,2,16,128]{4,3,2,1,0:T(8,128)S(1)}, f32[6,16,128]{2,1,0:T(8,128)S(1)}, f32[6,16,128]{2,1,0:T(...) custom-call(s32[32]{0:T(128)S(1)} %concatenate.9.refs_0_, f32[8,3,4,4096]{3,2,1,0:T(4,128)S(1)} %bitcast.16, ...), custom_call_target="tpu_custom_call" | custom-call | flops 2000000 | bytes 1000000 | tf_op jit(solution)/shard_map/gather/pallas_call | solution.py:30
  8.5 4.8 %collective-permute-start.2 = (f32[4,3,2,16,128]{4,3,2,1,0:T(8,128)S(1)}, f32[4,3,2,16,128]{4,3,2,1,0:T(8,128)S(1)}, u32[]{:S(2)}, u32[]{:S(2)}) collective-permute-start(f32[4,3,2,16,128]{4,3,2,1,0:T(8,128)S(1)} %get-tuple-element.52), channel_id=1, source_target_pairs={{0,16},{8,24},{1,17},{9,25},{2,18},{10,26},{3,19},{11,27},{4,20},{... | collective-permute-start | bytes 589832 | tf_op jit(solution)/shard_map/ppermute | solution.py:557
  20.1 4.4 %residual.1 = (f32[4,3,8,2,16,128]{5,4,3,2,1,0:T(8,128)S(1)}, f32[4,3,8,2,16,128]{5,4,3,2,1,0:T(8,128)S(1)}, f32[4,3,2,16,128]{4,3,2,1,0:T(8,128)S(1)}) custom-call(s32[32]{0:T(128)S(1)} %concatenate.9.refs_0_, f32[4,13,2,16,128]{4,3,2,1,0:T(8,128)S(1)} %get-tuple-element.51.refs_1_, f32[4,3,8,2,16,128]{5,4,3,2,1,0:T(8,128)S(1)} %get-tuple-element.50.refs_2_.refs_1_, ...), custom_call_target="tpu_custom_call" | custom-call | flops 8000000 | bytes 1000000 | tf_op jit(solution)/shard_map/residual/pallas_call | solution.py:30
  24.7 5.5 %collective-permute-done.7.refs_3_ = f32[4,3,2,16,128]{4,3,2,1,0:T(8,128)S(1)} collective-permute-done((f32[4,3,2,16,128]{4,3,2,1,0:T(8,128)S(1)}, f32[4,3,2,16,128]{4,3,2,1,0:T(8,128)S(1)}, u32[]{:S(2)}, u32[]{:S(2)}) %collective-permute-start.7) | collective-permute-done | bytes 196640 | tf_op jit(solution)/shard_map/ppermute | solution.py:574
  30.2 2.1 %close.5 = (f32[4,3,8,2,16,128]{5,4,3,2,1,0:T(8,128)S(1)}, f32[6,16,128]{2,1,0:T(8,128)S(1)}, f32[6,16,128]{2,1,0:T(8,128)S(1)}, f32[6,2,16,128]{3,2,1,0:T(8,128)S(1)}, f32[6,2,16,128]{3,2,1,0:T(8,128)S(1)}) custom-call(s32[32]{0:T(128)S(1)} %concatenate.9.refs_0_, f32[4,13,2,16,128]{4,3,2,1,0:T(8,128)S(1)} %get-tuple-element.51.refs_1_, ...), custom_call_target="tpu_custom_call" | custom-call | flops 2000000 | bytes 1000000 | tf_op jit(solution)/shard_map/close/pallas_call | solution.py:30
  32.3 2.3 %collective-permute-start.10 = (f32[6,2,16,128]{3,2,1,0:T(8,128)S(1)}, f32[6,2,16,128]{3,2,1,0:T(8,128)S(1)}, u32[]{:S(2)}, u32[]{:S(2)}) collective-permute-start(f32[6,2,16,128]{3,2,1,0:T(8,128)S(1)} %get-tuple-element.64), channel_id=1, source_target_pairs={{0,8},{8,0},{16,24},{24,16},{1,9},{9,1},{17,25},{25,17},{2,10},{10... | collective-permute-start | bytes 294920 | tf_op jit(solution)/shard_map/ppermute | solution.py:97
  36.8 2.6 %collective-permute-done.8.refs_4_ = f32[6,16,128]{2,1,0:T(8,128)S(1)} collective-permute-done((f32[6,16,128]{2,1,0:T(8,128)S(1)}, f32[6,16,128]{2,1,0:T(8,128)S(1)}, u32[]{:S(2)}, u32[]{:S(2)}) %collective-permute-start.8) | collective-permute-done | bytes 49184 | tf_op jit(solution)/shard_map/ppermute | solution.py:88
  39.9 4.3 %sweep.4 = (f32[4,3,8,2,16,128]{5,4,3,2,1,0:T(8,128)S(1)}, f32[4,3,2,16,128]{4,3,2,1,0:T(8,128)S(1)}) custom-call(s32[32]{0:T(128)S(1)} %concatenate.9.refs_0_, f32[4,13,2,16,128]{4,3,2,1,0:T(8,128)S(1)} %get-tuple-element.51.refs_1_, f32[4,3,8,2,16,128]{5,4,3,2,1,0:T(8,128)S(1)} %get-tuple-element.60.refs_2_, ...), custom_call_target="tpu_custom_call" | custom-call | flops 8000000 | bytes 1000000 | tf_op jit(solution)/shard_map/sweep/pallas_call | solution.py:30
  45.1 5.3 %collective-permute-done.12.refs_3_ = f32[4,3,2,16,128]{4,3,2,1,0:T(8,128)S(1)} collective-permute-done((f32[4,3,2,16,128]{4,3,2,1,0:T(8,128)S(1)}, f32[4,3,2,16,128]{4,3,2,1,0:T(8,128)S(1)}, u32[]{:S(2)}, u32[]{:S(2)}) %collective-permute-start.12) | collective-permute-done | bytes 196640 | tf_op jit(solution)/shard_map/ppermute | solution.py:574
  50.4 2.1 %close.6 = (f32[4,3,8,2,16,128]{5,4,3,2,1,0:T(8,128)S(1)}, f32[6,16,128]{2,1,0:T(8,128)S(1)}, f32[6,16,128]{2,1,0:T(8,128)S(1)}, f32[6,2,16,128]{3,2,1,0:T(8,128)S(1)}, f32[6,2,16,128]{3,2,1,0:T(8,128)S(1)}) custom-call(s32[32]{0:T(128)S(1)} %concatenate.9.refs_0_, f32[4,13,2,16,128]{4,3,2,1,0:T(8,128)S(1)} %get-tuple-element.51.refs_1_, ...), custom_call_target="tpu_custom_call" | custom-call | flops 2000000 | bytes 1000000 | tf_op jit(solution)/shard_map/close/pallas_call | solution.py:30
  54.7 2.8 %collective-permute-start.13 = (f32[6,16,128]{2,1,0:T(8,128)S(1)}, f32[6,16,128]{2,1,0:T(8,128)S(1)}, u32[]{:S(2)}, u32[]{:S(2)}) collective-permute-start(f32[6,16,128]{2,1,0:T(8,128)S(1)} %get-tuple-element.69), channel_id=1, source_target_pairs={{0,1},{1,0},{2,3},{3,2},{4,5},{5,4},{6,7},{7,6},{8,9},{9,8},{10,11... | collective-permute-start | bytes 147464 | tf_op jit(solution)/shard_map/ppermute | solution.py:88
  61.6 4.3 %sweep.5 = (f32[4,3,8,2,16,128]{5,4,3,2,1,0:T(8,128)S(1)}, f32[4,3,2,16,128]{4,3,2,1,0:T(8,128)S(1)}) custom-call(s32[32]{0:T(128)S(1)} %concatenate.9.refs_0_, f32[4,13,2,16,128]{4,3,2,1,0:T(8,128)S(1)} %get-tuple-element.51.refs_1_, f32[4,3,8,2,16,128]{5,4,3,2,1,0:T(8,128)S(1)} %get-tuple-element.68.refs_2_, ...), custom_call_target="tpu_custom_call" | custom-call | flops 8000000 | bytes 1000000 | tf_op jit(solution)/shard_map/sweep/pallas_call | solution.py:30
  67.1 6.5 %collective-permute-done.17.refs_3_ = f32[4,3,2,16,128]{4,3,2,1,0:T(8,128)S(1)} collective-permute-done((f32[4,3,2,16,128]{4,3,2,1,0:T(8,128)S(1)}, f32[4,3,2,16,128]{4,3,2,1,0:T(8,128)S(1)}, u32[]{:S(2)}, u32[]{:S(2)}) %collective-permute-start.17) | collective-permute-done | bytes 196640 | tf_op jit(solution)/shard_map/ppermute | solution.py:574
  73.6 2.1 %close.7 = (f32[4,3,8,2,16,128]{5,4,3,2,1,0:T(8,128)S(1)}, f32[6,16,128]{2,1,0:T(8,128)S(1)}, f32[6,16,128]{2,1,0:T(8,128)S(1)}, f32[6,2,16,128]{3,2,1,0:T(8,128)S(1)}, f32[6,2,16,128]{3,2,1,0:T(8,128)S(1)}) custom-call(s32[32]{0:T(128)S(1)} %concatenate.9.refs_0_, f32[4,13,2,16,128]{4,3,2,1,0:T(8,128)S(1)} %get-tuple-element.51.refs_1_, ...), custom_call_target="tpu_custom_call" | custom-call | flops 2000000 | bytes 1000000 | tf_op jit(solution)/shard_map/close/pallas_call | solution.py:30
  77.5 3.1 %collective-permute-done.18.refs_4_ = f32[6,16,128]{2,1,0:T(8,128)S(1)} collective-permute-done((f32[6,16,128]{2,1,0:T(8,128)S(1)}, f32[6,16,128]{2,1,0:T(8,128)S(1)}, u32[]{:S(2)}, u32[]{:S(2)}) %collective-permute-start.18) | collective-permute-done | bytes 49184 | tf_op jit(solution)/shard_map/ppermute | solution.py:88
  80.7 4.3 %sweep.6 = (f32[4,3,8,2,16,128]{5,4,3,2,1,0:T(8,128)S(1)}, f32[4,3,2,16,128]{4,3,2,1,0:T(8,128)S(1)}) custom-call(s32[32]{0:T(128)S(1)} %concatenate.9.refs_0_, f32[4,13,2,16,128]{4,3,2,1,0:T(8,128)S(1)} %get-tuple-element.51.refs_1_, f32[4,3,8,2,16,128]{5,4,3,2,1,0:T(8,128)S(1)} %get-tuple-element.75.refs_2_, ...), custom_call_target="tpu_custom_call" | custom-call | flops 8000000 | bytes 1000000 | tf_op jit(solution)/shard_map/sweep/pallas_call | solution.py:30
  85.5 5.3 %collective-permute-done.22.refs_3_ = f32[4,3,2,16,128]{4,3,2,1,0:T(8,128)S(1)} collective-permute-done((f32[4,3,2,16,128]{4,3,2,1,0:T(8,128)S(1)}, f32[4,3,2,16,128]{4,3,2,1,0:T(8,128)S(1)}, u32[]{:S(2)}, u32[]{:S(2)}) %collective-permute-start.22) | collective-permute-done | bytes 196640 | tf_op jit(solution)/shard_map/ppermute | solution.py:574
  92.8 2.4 %collective-permute-start.25 = (f32[6,2,16,128]{3,2,1,0:T(8,128)S(1)}, f32[6,2,16,128]{3,2,1,0:T(8,128)S(1)}, u32[]{:S(2)}, u32[]{:S(2)}) collective-permute-start(f32[6,2,16,128]{3,2,1,0:T(8,128)S(1)} %get-tuple-element.85), channel_id=1, source_target_pairs={{0,8},{8,0},{16,24},{24,16},{1,9},{9,1},{17,25},{25,17},{2,10},{10... | collective-permute-start | bytes 294920 | tf_op jit(solution)/shard_map/ppermute | solution.py:97
  95.8 2.1 %collective-permute-start.23 = (f32[6,16,128]{2,1,0:T(8,128)S(1)}, f32[6,16,128]{2,1,0:T(8,128)S(1)}, u32[]{:S(2)}, u32[]{:S(2)}) collective-permute-start(f32[6,16,128]{2,1,0:T(8,128)S(1)} %get-tuple-element.83), channel_id=1, source_target_pairs={{0,1},{1,0},{2,3},{3,2},{4,5},{5,4},{6,7},{7,6},{8,9},{9,8},{10,11... | collective-permute-start | bytes 147464 | tf_op jit(solution)/shard_map/ppermute | solution.py:88
  102.0 4.3 %sweep.7 = (f32[4,3,8,2,16,128]{5,4,3,2,1,0:T(8,128)S(1)}, f32[4,3,2,16,128]{4,3,2,1,0:T(8,128)S(1)}) custom-call(s32[32]{0:T(128)S(1)} %concatenate.9.refs_0_, f32[4,13,2,16,128]{4,3,2,1,0:T(8,128)S(1)} %get-tuple-element.51.refs_1_, f32[4,3,8,2,16,128]{5,4,3,2,1,0:T(8,128)S(1)} %get-tuple-element.82.refs_2_, ...), custom_call_target="tpu_custom_call" | custom-call | flops 8000000 | bytes 1000000 | tf_op jit(solution)/shard_map/sweep/pallas_call | solution.py:30
  107.4 5.9 %collective-permute-done.27.refs_3_.refs_4_ = f32[4,3,2,16,128]{4,3,2,1,0:T(8,128)S(1)} collective-permute-done((f32[4,3,2,16,128]{4,3,2,1,0:T(8,128)S(1)}, f32[4,3,2,16,128]{4,3,2,1,0:T(8,128)S(1)}, u32[]{:S(2)}, u32[]{:S(2)}) %collective-permute-start.27) | collective-permute-done | bytes 196640 | tf_op jit(solution)/shard_map/ppermute | solution.py:574
  119.8 3.3 %collective-permute-start.28 = (f32[4,3,4,4096]{3,2,1,0:T(4,128)S(1)}, f32[4,3,4,4096]{3,2,1,0:T(4,128)}, u32[]{:S(2)}, u32[]{:S(2)}) collective-permute-start(f32[4,3,4,4096]{3,2,1,0:T(4,128)S(1)} %get-tuple-element.91), channel_id=1, source_target_pairs={{0,8},{8,0},{16,24},{24,16},{1,9},{9,1},{17,25},{25,17},{2,10},{10... | collective-permute-start | bytes 2359304 | tf_op jit(solution)/shard_map/ppermute | solution.py:97
  123.1 4.7 %final.1 = (f32[4,3,4,4096]{3,2,1,0:T(4,128)S(1)}, f32[4,3,4,4096]{3,2,1,0:T(4,128)S(1)}) custom-call(s32[32]{0:T(128)S(1)} %concatenate.9.refs_0_, f32[4,13,2,16,128]{4,3,2,1,0:T(8,128)S(1)} %get-tuple-element.51.refs_1_, f32[4,3,8,2,16,128]{5,4,3,2,1,0:T(8,128)S(1)} %get-tuple-element.89.refs_2_, f32[4,3,8,2,16,128]{5,4,3,2,1,0:T(8,128)S(1)} %get-tuple-element.61.refs_3_, ...), custom_call_target="tpu_custom_call" | custom-call | flops 8000000 | bytes 1000000 | tf_op jit(solution)/shard_map/final/pallas_call | solution.py:30
  (82 shorter events, 45.0 us)
Async XLA Ops:
  4.3 11.3 %collective-permute-start.1 = (f32[4,3,4,4096]{3,2,1,0:T(4,128)}, f32[4,3,4,4096]{3,2,1,0:T(4,128)}, u32[]{:S(2)}, u32[]{:S(2)}) collective-permute-start(f32[4,3,4,4096]{3,2,1,0:T(4,128)} %dynamic-slice_bitcast_fusion), channel_id=1, source_target_pairs={{0,8},{8,0},{16,24},{24,16},{1,9},{9,1},{17,25},{25,17},{2,10},{10... | collective-permute-start | bytes 2359304 | tf_op jit(solution)/shard_map/ppermute | solution.py:97
  8.5 11.5 %collective-permute-start.2 = (f32[4,3,2,16,128]{4,3,2,1,0:T(8,128)S(1)}, f32[4,3,2,16,128]{4,3,2,1,0:T(8,128)S(1)}, u32[]{:S(2)}, u32[]{:S(2)}) collective-permute-start(f32[4,3,2,16,128]{4,3,2,1,0:T(8,128)S(1)} %get-tuple-element.52), channel_id=1, source_target_pairs={{0,16},{8,24},{1,17},{9,25},{2,18},{10,26},{3,19},{11,27},{4,20},{... | collective-permute-start | bytes 589832 | tf_op jit(solution)/shard_map/ppermute | solution.py:557
  13.3 6.7 %collective-permute-start.5 = (f32[6,2,16,128]{3,2,1,0:T(8,128)S(1)}, f32[6,2,16,128]{3,2,1,0:T(8,128)S(1)}, u32[]{:S(2)}, u32[]{:S(2)}) collective-permute-start(f32[6,2,16,128]{3,2,1,0:T(8,128)S(1)} %get-tuple-element.56), channel_id=1, source_target_pairs={{0,8},{8,0},{16,24},{24,16},{1,9},{9,1},{17,25},{25,17},{2,10},{10... | collective-permute-start | bytes 294920 | tf_op jit(solution)/shard_map/ppermute | solution.py:97
  13.4 6.7 %collective-permute-start.6 = (f32[6,2,16,128]{3,2,1,0:T(8,128)S(1)}, f32[6,2,16,128]{3,2,1,0:T(8,128)S(1)}, u32[]{:S(2)}, u32[]{:S(2)}) collective-permute-start(f32[6,2,16,128]{3,2,1,0:T(8,128)S(1)} %get-tuple-element.57), channel_id=1, source_target_pairs={{4,8},{5,9},{6,10},{7,11},{8,4},{9,5},{10,6},{11,7},{20,24},{21,25... | collective-permute-start | bytes 294920 | tf_op jit(solution)/shard_map/ppermute | solution.py:86
  14.1 6.0 %collective-permute-start.3 = (f32[6,16,128]{2,1,0:T(8,128)S(1)}, f32[6,16,128]{2,1,0:T(8,128)S(1)}, u32[]{:S(2)}, u32[]{:S(2)}) collective-permute-start(f32[6,16,128]{2,1,0:T(8,128)S(1)} %get-tuple-element.54), channel_id=1, source_target_pairs={{0,1},{1,0},{2,3},{3,2},{4,5},{5,4},{6,7},{7,6},{8,9},{9,8},{10,11... | collective-permute-start | bytes 147464 | tf_op jit(solution)/shard_map/ppermute | solution.py:88
  24.5 5.7 %collective-permute-start.7 = (f32[4,3,2,16,128]{4,3,2,1,0:T(8,128)S(1)}, f32[4,3,2,16,128]{4,3,2,1,0:T(8,128)S(1)}, u32[]{:S(2)}, u32[]{:S(2)}) collective-permute-start(f32[4,3,2,16,128]{4,3,2,1,0:T(8,128)S(1)} %get-tuple-element.59.refs_4_), channel_id=1, source_target_pairs={{0,16},{8,24},{16,0},{24,8},{1,17},{9,25},{17,1},{25,9},{2,18},{10... | collective-permute-start | bytes 589832 | tf_op jit(solution)/shard_map/ppermute | solution.py:574
  32.3 7.6 %collective-permute-start.10 = (f32[6,2,16,128]{3,2,1,0:T(8,128)S(1)}, f32[6,2,16,128]{3,2,1,0:T(8,128)S(1)}, u32[]{:S(2)}, u32[]{:S(2)}) collective-permute-start(f32[6,2,16,128]{3,2,1,0:T(8,128)S(1)} %get-tuple-element.64), channel_id=1, source_target_pairs={{0,8},{8,0},{16,24},{24,16},{1,9},{9,1},{17,25},{25,17},{2,10},{10... | collective-permute-start | bytes 294920 | tf_op jit(solution)/shard_map/ppermute | solution.py:97
  34.6 5.3 %collective-permute-start.11 = (f32[6,2,16,128]{3,2,1,0:T(8,128)S(1)}, f32[6,2,16,128]{3,2,1,0:T(8,128)S(1)}, u32[]{:S(2)}, u32[]{:S(2)}) collective-permute-start(f32[6,2,16,128]{3,2,1,0:T(8,128)S(1)} %get-tuple-element.65), channel_id=1, source_target_pairs={{4,8},{5,9},{6,10},{7,11},{8,4},{9,5},{10,6},{11,7},{20,24},{21,25... | collective-permute-start | bytes 294920 | tf_op jit(solution)/shard_map/ppermute | solution.py:86
  44.2 6.2 %collective-permute-start.12 = (f32[4,3,2,16,128]{4,3,2,1,0:T(8,128)S(1)}, f32[4,3,2,16,128]{4,3,2,1,0:T(8,128)S(1)}, u32[]{:S(2)}, u32[]{:S(2)}) collective-permute-start(f32[4,3,2,16,128]{4,3,2,1,0:T(8,128)S(1)} %get-tuple-element.67.refs_4_), channel_id=1, source_target_pairs={{0,16},{8,24},{16,0},{24,8},{1,17},{9,25},{17,1},{25,9},{2,18},{10... | collective-permute-start | bytes 589832 | tf_op jit(solution)/shard_map/ppermute | solution.py:574
  52.5 9.1 %collective-permute-start.15 = (f32[6,2,16,128]{3,2,1,0:T(8,128)S(1)}, f32[6,2,16,128]{3,2,1,0:T(8,128)S(1)}, u32[]{:S(2)}, u32[]{:S(2)}) collective-permute-start(f32[6,2,16,128]{3,2,1,0:T(8,128)S(1)} %get-tuple-element.71), channel_id=1, source_target_pairs={{0,8},{8,0},{16,24},{24,16},{1,9},{9,1},{17,25},{25,17},{2,10},{10... | collective-permute-start | bytes 294920 | tf_op jit(solution)/shard_map/ppermute | solution.py:97
  54.0 7.6 %collective-permute-start.16 = (f32[6,2,16,128]{3,2,1,0:T(8,128)S(1)}, f32[6,2,16,128]{3,2,1,0:T(8,128)S(1)}, u32[]{:S(2)}, u32[]{:S(2)}) collective-permute-start(f32[6,2,16,128]{3,2,1,0:T(8,128)S(1)} %get-tuple-element.72), channel_id=1, source_target_pairs={{4,8},{5,9},{6,10},{7,11},{8,4},{9,5},{10,6},{11,7},{20,24},{21,25... | collective-permute-start | bytes 294920 | tf_op jit(solution)/shard_map/ppermute | solution.py:86
  54.7 4.9 %collective-permute-start.13 = (f32[6,16,128]{2,1,0:T(8,128)S(1)}, f32[6,16,128]{2,1,0:T(8,128)S(1)}, u32[]{:S(2)}, u32[]{:S(2)}) collective-permute-start(f32[6,16,128]{2,1,0:T(8,128)S(1)} %get-tuple-element.69), channel_id=1, source_target_pairs={{0,1},{1,0},{2,3},{3,2},{4,5},{5,4},{6,7},{7,6},{8,9},{9,8},{10,11... | collective-permute-start | bytes 147464 | tf_op jit(solution)/shard_map/ppermute | solution.py:88
  65.9 7.7 %collective-permute-start.17 = (f32[4,3,2,16,128]{4,3,2,1,0:T(8,128)S(1)}, f32[4,3,2,16,128]{4,3,2,1,0:T(8,128)S(1)}, u32[]{:S(2)}, u32[]{:S(2)}) collective-permute-start(f32[4,3,2,16,128]{4,3,2,1,0:T(8,128)S(1)} %get-tuple-element.74.refs_4_), channel_id=1, source_target_pairs={{0,16},{8,24},{16,0},{24,8},{1,17},{9,25},{17,1},{25,9},{2,18},{10... | collective-permute-start | bytes 589832 | tf_op jit(solution)/shard_map/ppermute | solution.py:574
  75.7 5.0 %collective-permute-start.20 = (f32[6,2,16,128]{3,2,1,0:T(8,128)S(1)}, f32[6,2,16,128]{3,2,1,0:T(8,128)S(1)}, u32[]{:S(2)}, u32[]{:S(2)}) collective-permute-start(f32[6,2,16,128]{3,2,1,0:T(8,128)S(1)} %get-tuple-element.78), channel_id=1, source_target_pairs={{0,8},{8,0},{16,24},{24,16},{1,9},{9,1},{17,25},{25,17},{2,10},{10... | collective-permute-start | bytes 294920 | tf_op jit(solution)/shard_map/ppermute | solution.py:97
  75.8 4.9 %collective-permute-start.21 = (f32[6,2,16,128]{3,2,1,0:T(8,128)S(1)}, f32[6,2,16,128]{3,2,1,0:T(8,128)S(1)}, u32[]{:S(2)}, u32[]{:S(2)}) collective-permute-start(f32[6,2,16,128]{3,2,1,0:T(8,128)S(1)} %get-tuple-element.79), channel_id=1, source_target_pairs={{4,8},{5,9},{6,10},{7,11},{8,4},{9,5},{10,6},{11,7},{20,24},{21,25... | collective-permute-start | bytes 294920 | tf_op jit(solution)/shard_map/ppermute | solution.py:86
  85.0 5.7 %collective-permute-start.22 = (f32[4,3,2,16,128]{4,3,2,1,0:T(8,128)S(1)}, f32[4,3,2,16,128]{4,3,2,1,0:T(8,128)S(1)}, u32[]{:S(2)}, u32[]{:S(2)}) collective-permute-start(f32[4,3,2,16,128]{4,3,2,1,0:T(8,128)S(1)} %get-tuple-element.81.refs_4_), channel_id=1, source_target_pairs={{0,16},{8,24},{16,0},{24,8},{1,17},{9,25},{17,1},{25,9},{2,18},{10... | collective-permute-start | bytes 589832 | tf_op jit(solution)/shard_map/ppermute | solution.py:574
  92.8 9.2 %collective-permute-start.25 = (f32[6,2,16,128]{3,2,1,0:T(8,128)S(1)}, f32[6,2,16,128]{3,2,1,0:T(8,128)S(1)}, u32[]{:S(2)}, u32[]{:S(2)}) collective-permute-start(f32[6,2,16,128]{3,2,1,0:T(8,128)S(1)} %get-tuple-element.85), channel_id=1, source_target_pairs={{0,8},{8,0},{16,24},{24,16},{1,9},{9,1},{17,25},{25,17},{2,10},{10... | collective-permute-start | bytes 294920 | tf_op jit(solution)/shard_map/ppermute | solution.py:97
  95.2 6.8 %collective-permute-start.26 = (f32[6,2,16,128]{3,2,1,0:T(8,128)S(1)}, f32[6,2,16,128]{3,2,1,0:T(8,128)S(1)}, u32[]{:S(2)}, u32[]{:S(2)}) collective-permute-start(f32[6,2,16,128]{3,2,1,0:T(8,128)S(1)} %get-tuple-element.86), channel_id=1, source_target_pairs={{4,8},{5,9},{6,10},{7,11},{8,4},{9,5},{10,6},{11,7},{20,24},{21,25... | collective-permute-start | bytes 294920 | tf_op jit(solution)/shard_map/ppermute | solution.py:86
  106.3 6.9 %collective-permute-start.27 = (f32[4,3,2,16,128]{4,3,2,1,0:T(8,128)S(1)}, f32[4,3,2,16,128]{4,3,2,1,0:T(8,128)S(1)}, u32[]{:S(2)}, u32[]{:S(2)}) collective-permute-start(f32[4,3,2,16,128]{4,3,2,1,0:T(8,128)S(1)} %get-tuple-element.88.refs_4_.refs_5_), channel_id=1, source_target_pairs={{0,16},{8,24},{16,0},{24,8},{1,17},{9,25},{17,1},{25,9},{2,18},{10... | collective-permute-start | bytes 589832 | tf_op jit(solution)/shard_map/ppermute | solution.py:574
  115.3 7.8 %collective-permute-start.31 = (f32[6,2,16,128]{3,2,1,0:T(8,128)S(1)}, f32[6,2,16,128]{3,2,1,0:T(8,128)S(1)}, u32[]{:S(2)}, u32[]{:S(2)}) collective-permute-start(f32[6,2,16,128]{3,2,1,0:T(8,128)S(1)} %get-tuple-element.94), channel_id=1, source_target_pairs={{0,8},{8,0},{16,24},{24,16},{1,9},{9,1},{17,25},{25,17},{2,10},{10... | collective-permute-start | bytes 294920 | tf_op jit(solution)/shard_map/ppermute | solution.py:97
  116.1 7.0 %collective-permute-start.32 = (f32[6,2,16,128]{3,2,1,0:T(8,128)S(1)}, f32[6,2,16,128]{3,2,1,0:T(8,128)S(1)}, u32[]{:S(2)}, u32[]{:S(2)}) collective-permute-start(f32[6,2,16,128]{3,2,1,0:T(8,128)S(1)} %get-tuple-element.95), channel_id=1, source_target_pairs={{4,8},{5,9},{6,10},{7,11},{8,4},{9,5},{10,6},{11,7},{20,24},{21,25... | collective-permute-start | bytes 294920 | tf_op jit(solution)/shard_map/ppermute | solution.py:86
  116.9 6.2 %collective-permute-start.29 = (f32[6,16,128]{2,1,0:T(8,128)S(1)}, f32[6,16,128]{2,1,0:T(8,128)S(1)}, u32[]{:S(2)}, u32[]{:S(2)}) collective-permute-start(f32[6,16,128]{2,1,0:T(8,128)S(1)} %get-tuple-element.92), channel_id=1, source_target_pairs={{0,1},{1,0},{2,3},{3,2},{4,5},{5,4},{6,7},{7,6},{8,9},{9,8},{10,11... | collective-permute-start | bytes 147464 | tf_op jit(solution)/shard_map/ppermute | solution.py:88
  117.1 6.0 %collective-permute-start.30 = (f32[6,16,128]{2,1,0:T(8,128)S(1)}, f32[6,16,128]{2,1,0:T(8,128)S(1)}, u32[]{:S(2)}, u32[]{:S(2)}) collective-permute-start(f32[6,16,128]{2,1,0:T(8,128)S(1)} %get-tuple-element.93), channel_id=1, source_target_pairs={{0,2},{1,3},{2,0},{3,1},{4,6},{5,7},{6,4},{7,5},{8,10},{9,11},{10,... | collective-permute-start | bytes 147464 | tf_op jit(solution)/shard_map/ppermute | solution.py:91
  119.8 8.5 %collective-permute-start.28 = (f32[4,3,4,4096]{3,2,1,0:T(4,128)S(1)}, f32[4,3,4,4096]{3,2,1,0:T(4,128)}, u32[]{:S(2)}, u32[]{:S(2)}) collective-permute-start(f32[4,3,4,4096]{3,2,1,0:T(4,128)S(1)} %get-tuple-element.91), channel_id=1, source_target_pairs={{0,8},{8,0},{16,24},{24,16},{1,9},{9,1},{17,25},{25,17},{2,10},{10... | collective-permute-start | bytes 2359304 | tf_op jit(solution)/shard_map/ppermute | solution.py:97
  (17 other events, 91.9 us)

commit v2 on v1

v2 whole, which is shorter than its diff:
```python
import jax
import jax.numpy as jnp
from jax import lax
from jax.experimental import pallas as pl
from jax.experimental.pallas import tpu as pltpu
from jax.sharding import PartitionSpec as P

EDGE = 16
LANES = 128
CHUNKS = 32
COMPONENTS = 3
ALPHA_SCALE = 0.1
WINDOW_SLICES = 16
SWEEPS = 5
XP, XM, YP, YM, ZP, ZM, XG, YG, ZG, Q, INV, K0 = range(12)
CORE, CHIP, SIDE_X, SIDE_Y, HOLD = range(5)
F32 = jnp.float32


def iota(shape, axis):
    return lax.broadcasted_iota(jnp.int32, shape, axis)


def tile_shape(*lead):
    return lead + (2, EDGE, LANES)


def call(kernel, flags, ins, outs, scratch=(), flops=2_000_000, name=None):
    vmem = pl.BlockSpec(memory_space=pltpu.VMEM)
    return pl.pallas_call(
        kernel,
        in_specs=[pl.BlockSpec(memory_space=pltpu.SMEM)] + [vmem] * len(ins),
        out_specs=[vmem] * len(outs),
        out_shape=[jax.ShapeDtypeStruct(s, F32) for s in outs],
        scratch_shapes=list(scratch),
        compiler_params=pltpu.CompilerParams(vmem_limit_bytes=24 * 1024 * 1024),
        cost_estimate=pl.CostEstimate(flops=flops, bytes_accessed=1_000_000, transcendentals=0),
        name=name,
    )(flags, *ins)


class Shape:
    def __init__(self, slots, local, n_time, places):
        self.slots = slots
        self.half = slots // 2
        self.local = local
        self.span = 2 * local
        self.chips = n_time // 2
        levels = places.bit_length() - 1
        self.bits = [[b for b in range(levels) if b % 3 == d] for d in range(3)]
        self.y_per = max(1, 8 // self.span)
        self.z_per = max(1, 16 // self.span)
        self.x_shape = (2 * COMPONENTS, self.span * 2, LANES)
        self.y_shape = (-(-2 // self.y_per) * COMPONENTS, EDGE, LANES)
        self.z_shape = tile_shape(-(-self.half // self.z_per) * COMPONENTS)
        self.x_count = len(self.bits[0])
        self.field = tile_shape(self.half, COMPONENTS, self.span)
        self.slice = tile_shape(self.half, COMPONENTS)


def position(place, bits):
    if len(bits) == 1:
        return place >> bits[0] & 1
    low, high = place >> bits[0] & 1, place >> bits[1] & 1
    return 2 * high + (low ^ high)


def exchange(sh, messages, n_time, places):
    axes = ("tm", "space")
    received = []
    x_out, y_out, inner_out, z_out = messages[:-3], messages[-3], messages[-2], messages[-1]

    def pairs(bit, bits, crossed):
        table = []
        for t in range(n_time):
            for s in range(places):
                here, there = position(s, bits), position(s ^ (1 << bit), bits)
                if abs(here - there) != 1:
                    continue
                if crossed and (there > here) != (t % 2 == 1):
                    continue
                target = t ^ 1 if crossed else t
                table.append((t * places + s, target * places + (s ^ (1 << bit))))
        return table

    z_in = lax.ppermute(z_out, axes, pairs(sh.bits[2][0], sh.bits[2], True))
    x_in = [
        lax.ppermute(x_out[i], axes, pairs(bit, sh.bits[0], False))
        for i, bit in enumerate(sh.bits[0])
    ]
    y_in = lax.ppermute(y_out, axes, pairs(sh.bits[1][0], sh.bits[1], False))
    inner_in = swap_cores(inner_out, n_time)
    return x_in + [y_in, inner_in, z_in]


def swap_cores(value, n_time):
    return lax.ppermute(value, "tm", [(t, t ^ 1) for t in range(n_time)])


def pack_faces(sh, flags, tile, src, outs):
    core = flags[CORE]
    lane = iota((EDGE, LANES), 1)
    within, group_of_lane = lane % EDGE, lane // EDGE
    x_outs, y_out, inner_out, z_out = outs[:-3], outs[-3], outs[-2], outs[-1]
    side_y = flags[SIDE_Y]
    y_groups = -(-2 // sh.y_per)

    for g in range(-(-sh.half // sh.z_per)):
        slots = range(g * sh.z_per, min(sh.half, (g + 1) * sh.z_per))

        def comp_step(comp, _, g=g, slots=slots):
            low = [jnp.zeros((EDGE, LANES), F32)] * 2
            high = [jnp.zeros((EDGE, LANES), F32)] * 2
            for j in slots:
                for l in range(sh.span):
                    index = (j % sh.z_per) * sh.span + l
                    for h in range(2):
                        value = tile(j, comp, l, h)
                        value = pltpu.roll(value, index, 1) if index else value
                        low[h] = jnp.where(within == index, value, low[h])
                        high[h] = jnp.where(within == (index + EDGE - 1) % EDGE, value, high[h])
            for h in range(2):
                inner_out[g * COMPONENTS + comp, h] = jnp.where(core == 1, low[h], high[h])
                z_out[g * COMPONENTS + comp, h] = jnp.where(core == 1, high[h], low[h])
            for number, x_out in enumerate(x_outs):
                side = flags[SIDE_X] if number == 0 else 1 - flags[SIDE_X]
                for jj in range(slots[0] // 2, slots[-1] // 2 + 1):
                    for l in range(sh.span):
                        for h in range(2):
                            upper = src[2 * jj + 1, comp, l, h, EDGE - 1 : EDGE, :]
                            lower = src[2 * jj, comp, l, h, 0:1, :]
                            row = slice(2 * l + h, 2 * l + h + 1)
                            x_out[jj * COMPONENTS + comp, row, :] = jnp.where(
                                side == 1, upper, lower
                            )
            for half in range(slots[0] // 2, slots[-1] // 2 + 1):

                @pl.when(side_y == half)
                def _(half=half):
                    for y in range(y_groups):
                        packed = jnp.zeros((EDGE, LANES), F32)
                        for jj in range(y * sh.y_per, min(2, (y + 1) * sh.y_per)):
                            for l in range(sh.span):
                                index = (jj % sh.y_per) * sh.span + l
                                layer = src[2 * half + jj, comp, l, half]
                                shift = EDGE * (index + half) % LANES
                                layer = pltpu.roll(layer, shift, 1) if shift else layer
                                packed = jnp.where(group_of_lane == index, layer, packed)
                        y_out[y * COMPONENTS + comp] = packed

            return 0

        lax.fori_loop(0, COMPONENTS, comp_step, 0)


def inner_sum(sh, flags, coef, src, j, comp, l):
    lane = iota((EDGE, LANES), 1)
    row = iota((EDGE, LANES), 0)
    within = lane % EDGE
    hold = [flags[HOLD + j * 6 + face].astype(F32) for face in range(4)]
    tiles = [src[j, comp, l, h] for h in range(2)]
    if j // 2 == 0:
        below, above = 0.0, src[j ^ 2, comp, l, 0] * hold[3]
    else:
        below, above = src[j ^ 2, comp, l, 1] * hold[2], 0.0
    y_next = [jnp.where(lane < EDGE, tiles[1], tiles[0]), jnp.where(lane < EDGE, above, tiles[1])]
    last = lane >= LANES - EDGE
    y_back = [jnp.where(last, below, tiles[0]), jnp.where(last, tiles[0], tiles[1])]
    result = []
    for h in range(2):
        v = tiles[h]
        if j % 2 == 0:
            before, after = 0.0, src[j ^ 1, comp, l, h, 0:1, :] * hold[1]
        else:
            before, after = src[j ^ 1, comp, l, h, EDGE - 1 : EDGE, :] * hold[0], 0.0
        total = coef[j, YP, h] * pltpu.roll(y_next[h], LANES - EDGE, 1)
        total += coef[j, YM, h] * pltpu.roll(y_back[h], EDGE, 1)
        total += coef[j, ZP, h] * pltpu.roll(v, LANES - 1, 1)
        total += coef[j, ZM, h] * pltpu.roll(v, 1, 1)
        total += coef[j, XP, h] * pltpu.roll(jnp.where(row == 0, after, v), EDGE - 1, 0)
        total += coef[j, XM, h] * pltpu.roll(jnp.where(row == EDGE - 1, before, v), 1, 0)
        result.append(total)
    return result


def ghost_sum(sh, flags, coef, faces, z_ghost, total, j, comp, l):
    xs, y_in = faces[:-1], faces[-1]
    x_side, x_row = j % 2, j // 2
    y_side, y_row = j // 2, j % 2
    y_index = (y_row % sh.y_per) * sh.span + l
    z_index = (j % sh.z_per) * sh.span + l
    z_group = (j // sh.z_per) * COMPONENTS + comp
    outer = x_row * COMPONENTS + comp
    result = []
    for h in range(2):
        value = total[h]
        value += coef[j, ZG, h] * pltpu.roll(
            z_ghost[z_index % 2, z_group, h], LANES - EDGE + 1 - z_index, 1
        )
        if h == y_side:
            group = y_in[(y_row // sh.y_per) * COMPONENTS + comp]
            shift = ((LANES - EDGE if y_side else 0) - EDGE * y_index) % LANES
            value += coef[j, YG, h] * (pltpu.roll(group, shift, 1) if shift else group)
        row = slice(2 * l + h, 2 * l + h + 1)
        if len(xs) == 1:
            crossed = xs[0][outer, row, :]
        else:
            wanted = flags[SIDE_X] if x_side == 1 else 1 - flags[SIDE_X]
            crossed = jnp.where(wanted == 1, xs[0][outer, row, :], xs[1][outer, row, :])
        part = slice(8 * x_side, 8 * x_side + 8)
        changed = value[part] + coef[j, XG, h, part, :] * jnp.broadcast_to(crossed, (8, LANES))
        parts = [value[:8], changed] if x_side else [changed, value[8:]]
        result.append(jnp.concatenate(parts, axis=0))
    return result


def place_z_ghost(flags, inner_in, z_in, z_ghost):
    core = flags[CORE]
    odd = iota((EDGE, LANES), 1) % 2 == 1

    def step(g, _):
        for h in range(2):
            inner, outer = inner_in[g, h], z_in[g, h]
            upper = pltpu.roll(jnp.where(core == 1, outer, inner), 2 * EDGE - 2, 1)
            lower = jnp.where(core == 1, inner, outer)
            z_ghost[0, g, h] = jnp.where(odd, lower, upper)
            z_ghost[1, g, h] = jnp.where(odd, upper, lower)
        return 0

    lax.fori_loop(0, inner_in.shape[0], step, 0)


def rows_to_tiles(read, count, rows, write):
    for chunk in range(CHUNKS):
        rows[chunk * count : (chunk + 1) * count, :] = read(chunk)
    for i in range(count):
        for h in range(2):
            write(i, h, rows[pl.ds(h * count + i, EDGE, 2 * count), :])


def tiles_to_rows(tile, count, rows, write):
    for i in range(count):
        for h in range(2):
            rows[pl.ds(h * count + i, EDGE, 2 * count), :] = tile(i, h)
    for chunk in range(CHUNKS):
        write(chunk, rows[chunk * count : (chunk + 1) * count, :])


def coefficient_kernel(sh, flags, viscosity, peclet, initial, coef, first, rows, tiles):
    core = flags[CORE]
    chip = flags[CHIP]
    slots = sh.slots

    def unpack(source, kind):
        def write(i, h, value):
            tiles[kind, i, h] = value

        rows_to_tiles(lambda c: source(c), slots, rows, write)

    unpack(lambda c: viscosity[:, c * LANES : (c + 1) * LANES], 0)
    for d in range(3):
        unpack(lambda c, d=d: peclet[d, :, c * LANES : (c + 1) * LANES], 1 + d)
    for d in range(3):
        unpack(lambda c, d=d: initial[d, :, c * LANES : (c + 1) * LANES], 4 + d)

    lane = iota((EDGE, LANES), 1)
    row = iota((EDGE, LANES), 0)
    within = lane % EDGE
    zero = jnp.zeros((EDGE, LANES), F32)

    def step(j, _):
        slot = core * sh.half + j
        hold = [flags[HOLD + j * 6 + face].astype(F32) for face in range(6)]
        for h in range(2):
            nu = tiles[0, slot, h]
            inverse = 2.0 + 6.0 * nu
            q = 2.0 / inverse
            scale = nu / inverse
            plus = [scale * (1.0 - tiles[1 + d, slot, h]) for d in range(3)]
            minus = [scale * (1.0 + tiles[1 + d, slot, h]) for d in range(3)]
            for d, (upper, lower) in enumerate(((XP, XM), (YP, YM), (ZP, ZM))):
                coef[j, upper, h] = plus[d]
                coef[j, lower, h] = minus[d]
            coef[j, ZP, h] = jnp.where(within < EDGE - 1, plus[2], zero)
            coef[j, ZM, h] = jnp.where(within > 0, minus[2], zero)
            coef[j, XG, h] = jnp.where(
                row == 0,
                minus[0] * hold[0],
                jnp.where(row == EDGE - 1, plus[0] * hold[1], zero),
            )
            if h == 0:
                coef[j, YG, h] = jnp.where(lane < EDGE, minus[1] * hold[2], zero)
            else:
                coef[j, YG, h] = jnp.where(lane >= LANES - EDGE, plus[1] * hold[3], zero)
            coef[j, ZG, h] = jnp.where(
                within == 0,
                minus[2] * hold[4],
                jnp.where(within == EDGE - 1, plus[2] * hold[5], zero),
            )
            coef[j, Q, h] = q
            coef[j, INV, h] = inverse
            power = q
            for _ in range(sh.span.bit_length() - 1):
                power = power * power
            whole = power
            for _ in range(sh.chips.bit_length() - 1):
                whole = whole * whole
            weight = 1.0 / (1.0 - ALPHA_SCALE * whole)
            for back in range(1, sh.chips + 1):
                wrapped = jnp.where(chip < back, ALPHA_SCALE, 1.0)
                coef[j, K0 + back - 1, h] = weight * wrapped
                weight = weight * power
            for d in range(COMPONENTS):
                first[j, d, h] = tiles[4 + d, slot, h]
        return 0

    lax.fori_loop(0, sh.half, step, 0)


def assemble(sh, flags, whole, other, field, rows):
    core = flags[CORE]

    def step(k, _):
        j, comp = k // COMPONENTS, k % COMPONENTS
        slot = core * sh.half + j
        for part, source in enumerate((whole, other)):
            first = (core if part == 0 else 1 - core) * sh.local

            def write(i, h, value, first=first):
                field[j, comp, first + i, h] = value

            rows_to_tiles(
                lambda c, source=source: source[slot, comp, :, c * LANES : (c + 1) * LANES],
                sh.local,
                rows.at[part],
                write,
            )
        return 0

    lax.fori_loop(0, sh.half * COMPONENTS, step, 0)


def gather_kernel(sh, flags, whole, other, field, last, *rest):
    assemble(sh, flags, whole, other, field, rest[-1])

    def step(k, _):
        j, comp = k // COMPONENTS, k % COMPONENTS
        last[j, comp] = field[j, comp, sh.span - 1]
        return 0

    lax.fori_loop(0, sh.half * COMPONENTS, step, 0)
    pack_faces(sh, flags, lambda j, c, l, h: field[j, c, l, h], field, rest[:-1])


def over_tiles(sh, visit):
    for j in range(sh.half):

        def comp_step(comp, _, j=j):
            visit(j, comp)
            return 0

        lax.fori_loop(0, COMPONENTS, comp_step, 0)


def residual_inner_kernel(sh, flags, coef, field, whole, other, inner, force, rows):
    assemble(sh, flags, whole, other, force, rows)

    def visit(j, comp):
        prior = None
        for l in range(sh.span):
            total = inner_sum(sh, flags, coef, field, j, comp, l)
            now = [field[j, comp, l, h] for h in range(2)]
            for h in range(2):
                q = coef[j, Q, h]
                value = total[h] + (0.5 * q) * force[j, comp, l, h] - now[h]
                inner[j, comp, l, h] = value if prior is None else value + q * prior[h]
            prior = now

    over_tiles(sh, visit)


def residual_outer_kernel(sh, flags, coef, inner, before, first, *rest):
    faces = rest[: sh.x_count + 1]
    inner_in, z_in, scaled, partial, last, z_ghost = rest[sh.x_count + 1 :]
    place_z_ghost(flags, inner_in, z_in, z_ghost)
    chip = flags[CHIP]

    def visit(j, comp):
        live = flags[HOLD + 6 * sh.half + j].astype(F32)
        carry = [jnp.zeros((EDGE, LANES), F32)] * 2
        for l in range(sh.span):
            total = [inner[j, comp, l, h] for h in range(2)]
            if l == 0:
                for h in range(2):
                    prior = jnp.where(chip == 0, first[j, comp, h], before[j, comp, h])
                    total[h] = total[h] + coef[j, Q, h] * prior
            total = ghost_sum(sh, flags, coef, faces, z_ghost, total, j, comp, l)
            for h in range(2):
                value = total[h] * live
                scaled[j, comp, l, h] = value
                carry[h] = value + coef[j, Q, h] * carry[h]
                partial[j, comp, l, h] = carry[h]
        for h in range(2):
            last[j, comp, h] = carry[h]

    over_tiles(sh, visit)


def sweep_inner_kernel(sh, flags, coef, field, scaled, inner):
    def visit(j, comp):
        for l in range(sh.span):
            total = inner_sum(sh, flags, coef, field, j, comp, l)
            for h in range(2):
                inner[j, comp, l, h] = scaled[j, comp, l, h] + total[h]

    over_tiles(sh, visit)


def sweep_outer_kernel(sh, flags, coef, inner, *rest):
    faces = rest[: sh.x_count + 1]
    inner_in, z_in, partial, last, z_ghost = rest[sh.x_count + 1 :]
    place_z_ghost(flags, inner_in, z_in, z_ghost)

    def visit(j, comp):
        carry = [jnp.zeros((EDGE, LANES), F32)] * 2
        for l in range(sh.span):
            total = [inner[j, comp, l, h] for h in range(2)]
            total = ghost_sum(sh, flags, coef, faces, z_ghost, total, j, comp, l)
            for h in range(2):
                carry[h] = total[h] + coef[j, Q, h] * carry[h]
                partial[j, comp, l, h] = carry[h]
        for h in range(2):
            last[j, comp, h] = carry[h]

    over_tiles(sh, visit)


def incoming_slice(sh, coef, lasts, j, comp, h):
    total = coef[j, K0, h] * lasts[0][j, comp, h]
    for back in range(1, sh.chips):
        total += coef[j, K0 + back, h] * lasts[back][j, comp, h]
    return total


def close_kernel(sh, flags, coef, partial, *rest):
    lasts, (field, *messages) = rest[: sh.chips], rest[sh.chips :]
    term = {}

    def tile(j, comp, l, h):
        if l == 0:
            term[h] = incoming_slice(sh, coef, lasts, j, comp, h)
        term[h] = coef[j, Q, h] * term[h]
        value = partial[j, comp, l, h] + term[h]
        field[j, comp, l, h] = value
        return value

    pack_faces(sh, flags, tile, field, messages)


def velocity_kernel(sh, flags, whole, other, field, out, send, rows):
    core = flags[CORE]

    def step(k, _):
        j, comp = k // COMPONENTS, k % COMPONENTS
        slot = core * sh.half + j

        def keep(c, value):
            at = slice(c * LANES, (c + 1) * LANES)
            out[slot, comp, :, at] = whole[slot, comp, :, at] + value

        def pass_on(c, value):
            at = slice(c * LANES, (c + 1) * LANES)
            send[j, comp, :, at] = other[slot, comp, :, at] + value

        own, others = core * sh.local, (1 - core) * sh.local
        tiles_to_rows(lambda i, h: field[j, comp, own + i, h], sh.local, rows.at[0], keep)
        tiles_to_rows(lambda i, h: field[j, comp, others + i, h], sh.local, rows.at[1], pass_on)
        return 0

    lax.fori_loop(0, sh.half * COMPONENTS, step, 0)


def final_inner_kernel(sh, flags, coef, field, scaled, *rest):
    lasts, (inner,) = rest[: sh.chips], rest[sh.chips :]
    chip = flags[CHIP]

    def visit(j, comp):
        prior = [
            jnp.where(chip == 0, 0.0, incoming_slice(sh, coef, lasts, j, comp, h))
            for h in range(2)
        ]
        for l in range(sh.span):
            total = inner_sum(sh, flags, coef, field, j, comp, l)
            for h in range(2):
                now = field[j, comp, l, h]
                value = scaled[j, comp, l, h] + total[h] - now
                inner[j, comp, l, h] = value + coef[j, Q, h] * prior[h]
                prior[h] = now

    over_tiles(sh, visit)


def final_outer_kernel(sh, flags, coef, inner, *rest):
    faces = rest[: sh.x_count + 1]
    inner_in, z_in, out, send, z_ghost, hold, rows = rest[sh.x_count + 1 :]
    place_z_ghost(flags, inner_in, z_in, z_ghost)
    core = flags[CORE]

    def visit(j, comp):
        live = flags[HOLD + 6 * sh.half + j].astype(F32)
        for l in range(sh.span):
            total = [inner[j, comp, l, h] for h in range(2)]
            total = ghost_sum(sh, flags, coef, faces, z_ghost, total, j, comp, l)
            for h in range(2):
                hold[l, h] = total[h] * (coef[j, INV, h] * live)
        slot = core * sh.half + j

        def keep(c, value):
            out[slot, comp, :, c * LANES : (c + 1) * LANES] = value

        def pass_on(c, value):
            send[j, comp, :, c * LANES : (c + 1) * LANES] = value

        own, others = core * sh.local, (1 - core) * sh.local
        tiles_to_rows(lambda i, h: hold[own + i, h], sh.local, rows.at[0], keep)
        tiles_to_rows(lambda i, h: hold[others + i, h], sh.local, rows.at[1], pass_on)

    over_tiles(sh, visit)


def bind(kernel, sh):
    def run(*refs):
        kernel(sh, *refs)

    return run


def body(
    iterate,
    forcing,
    initial_velocity,
    viscosity,
    peclet,
    live_patch_mask,
    neighbour_holder,
    neighbour_slot,
):
    n_time, places = lax.axis_size("tm"), lax.axis_size("space")
    slots, local = iterate.shape[:2]
    sh = Shape(slots, local, n_time, places)
    half = sh.half
    t, place = lax.axis_index("tm"), lax.axis_index("space")
    core, chip = t % 2, t // 2
    velocity = iterate.transpose(0, 2, 1, 3)
    force = forcing.transpose(0, 2, 1, 3)

    velocity_other = swap_cores(velocity, n_time)
    force_other = swap_cores(force, n_time)

    def side(bits):
        return 1 - position(place, bits) % 2

    held = lax.dynamic_slice_in_dim(neighbour_holder, core * half, half, 0) >= 0
    live = lax.dynamic_slice_in_dim(live_patch_mask, core * half, half, 0)
    flags = jnp.concatenate(
        [
            jnp.stack([core, chip, side(sh.bits[0]), side(sh.bits[1])]).astype(jnp.int32),
            held.astype(jnp.int32).reshape(-1),
            live.astype(jnp.int32),
        ]
    )
    rows = pltpu.VMEM((2, CHUNKS * local, LANES), F32)
    z_ghost = pltpu.VMEM((2,) + sh.z_shape, F32)
    messages = [sh.x_shape] * sh.x_count + [sh.y_shape, sh.z_shape, sh.z_shape]

    coef, first = call(
        bind(coefficient_kernel, sh),
        flags,
        [viscosity, peclet.transpose(1, 0, 2), initial_velocity.transpose(1, 0, 2)],
        [tile_shape(half, K0 + sh.chips), sh.slice],
        [pltpu.VMEM((CHUNKS * slots, LANES), F32), pltpu.VMEM(tile_shape(7, slots), F32)],
        name="coefficients",
    )
    field, last, *out = call(
        bind(gather_kernel, sh),
        flags,
        [velocity, velocity_other],
        [sh.field, sh.slice] + messages,
        [rows],
        name="gather",
    )
    before = lax.ppermute(last, "tm", [(a, a + 2) for a in range(n_time - 2)])
    faces = exchange(sh, out, n_time, places)
    inner, _ = call(
        bind(residual_inner_kernel, sh),
        flags,
        [coef, field, force, force_other],
        [sh.field, sh.field],
        [rows],
        flops=20_000_000,
        name="residual_inner",
    )
    scaled, partial, last = call(
        bind(residual_outer_kernel, sh),
        flags,
        [coef, inner, before, first] + faces,
        [sh.field, sh.field, sh.slice],
        [z_ghost],
        name="residual_outer",
    )

    def chip_ends(last):
        return [
            lax.ppermute(last, "tm", [(a, (a + 2 * back) % n_time) for a in range(n_time)])
            for back in range(1, sh.chips)
        ] + [last]

    correction = None
    for sweep in range(SWEEPS):
        if sweep > 0:
            (inner,) = call(
                bind(sweep_inner_kernel, sh),
                flags,
                [coef, correction, scaled],
                [sh.field],
                flops=20_000_000,
                name="sweep_inner",
            )
            partial, last = call(
                bind(sweep_outer_kernel, sh),
                flags,
                [coef, inner] + faces,
                [sh.field, sh.slice],
                [z_ghost],
                name="sweep_outer",
            )
        ends = chip_ends(last)
        correction, *out = call(
            bind(close_kernel, sh),
            flags,
            [coef, partial] + ends,
            [sh.field] + messages,
            name="close",
        )
        faces = exchange(sh, out, n_time, places)
    native = (half, COMPONENTS, local, CHUNKS * LANES)
    whole = (slots,) + native[1:]

    def restore(out, send):
        other = swap_cores(send, n_time)
        start = ((1 - core) * half, 0, 0, 0)
        return lax.dynamic_update_slice(out, other, start).transpose(0, 2, 1, 3)

    (inner,) = call(
        bind(final_inner_kernel, sh),
        flags,
        [coef, correction, scaled] + ends,
        [sh.field],
        flops=20_000_000,
        name="final_inner",
    )
    out, send = call(
        bind(velocity_kernel, sh),
        flags,
        [velocity, velocity_other, correction],
        [whole, native],
        [rows],
        name="velocity",
    )
    corrected_velocity = restore(out, send)
    out, send = call(
        bind(final_outer_kernel, sh),
        flags,
        [coef, inner] + faces,
        [whole, native],
        [z_ghost, pltpu.VMEM(tile_shape(sh.span), F32), rows],
        name="final_outer",
    )
    return corrected_velocity, restore(out, send)


def solution(mesh):
    return jax.shard_map(
        body,
        mesh=mesh,
        in_specs=(
            P("space", "tm", None, None),
            P("space", "tm", None, None),
            P("space", None, None),
            P("space", None),
            P("space", None, None),
            P("space"),
            P("space", None),
            P("space", None),
        ),
        out_specs=(P("space", "tm", None, None), P("space", "tm", None, None)),
        check_vma=False,
    )
```

time: 136 us -> 126 us (0.926)
  waiting for transfers between devices: 44.2 us -> 34.9 us
  Pallas kernels: 43.3 us -> 50.7 us
  starting transfers between devices: 38.4 us -> 33.9 us
  other arithmetic: 5.04 us -> 0.69 us
    ppermute x6, waiting for transfers between devices: 7.91 us -> 0.4 us  [exchange(): lax.ppermute(x_out[i], axes, pairs(bit, sh.bits[0], False))]
    pallas_call x15 -> x20, Pallas kernels: 43.3 us -> 50.7 us  [call(): pl.pallas_call(kernel, in_specs=[pl.BlockSpec(memory_space=pltpu.SMEM)] +...]
    dynamic_slice x2 -> x0, local copies, waits for them, and re-layouts: 3.15 us -> none  [partner_slots(): lax.dynamic_slice_in_dim(value, (1 - core) * half, half, 0)]
    transpose x2 -> x0, other arithmetic: 3.1 us -> none  [restore(): return whole.transpose(0, 2, 1, 3)]
    unnamed x14 -> x16, local copies, waits for them, and re-layouts: 0.03 us -> 2.57 us
    ppermute x6, waiting for transfers between devices: 4.61 us -> 2.12 us  [exchange(): y_in = lax.ppermute(y_out, axes, pairs(sh.bits[1][0], sh.bits[1], False))]
    ppermute x5, starting transfers between devices: 3.85 us -> 1.53 us  [chip_ends(): lax.ppermute(last, 'tm', [(a, (a + 2 * back) % n_time) for a in range(n_t...]
    select_n x1 -> x0, other arithmetic: 1.94 us -> none  [restore(): jnp.where(first_core, keep, other)]
  transfers between devices with their start and end apart: 34 -> 34, of which waited for: 15 -> 14; matrix products, arithmetic and copies ran while one was open for 1% -> 2% of each run, Pallas kernels for 8% -> 22%
where the time goes in v2:
time: 126 us
  Pallas kernels  50.7 us (40%)
  waiting for transfers between devices  34.9 us (28%)
  starting transfers between devices  33.9 us (27%)
  local copies, waits for them, and re-layouts  4.5 us (4%)
    pallas_call x20, Pallas kernels, call(): pl.pallas_call(kernel, in_specs=[pl.BlockSpec(memory_space=pltpu.SMEM)] +...  50.7 us
    ppermute x5, waiting for transfers between devices, chip_ends(): lax.ppermute(last, 'tm', [(a, (a + 2 * back) % n_time) for a in range(n_t...  29.8 us
    ppermute x10, starting transfers between devices, swap_cores(): return lax.ppermute(value, 'tm', [(t, t ^ 1) for t in range(n_time)])  11.9 us
    ppermute x6, starting transfers between devices, exchange(): lax.ppermute(x_out[i], axes, pairs(bit, sh.bits[0], False))  6.4 us
    ppermute x6, starting transfers between devices, exchange(): y_in = lax.ppermute(y_out, axes, pairs(sh.bits[1][0], sh.bits[1], False))  5.33 us
    ppermute x1, starting transfers between devices, body(): before = lax.ppermute(last, 'tm', [(a, a + 2) for a in range(n_time - 2)])  4.76 us
    ppermute x6, starting transfers between devices, exchange(): z_in = lax.ppermute(z_out, axes, pairs(sh.bits[2][0], sh.bits[2], True))  3.94 us
    ppermute x10, waiting for transfers between devices, swap_cores(): return lax.ppermute(value, 'tm', [(t, t ^ 1) for t in range(n_time)])  2.57 us
  transfers between devices with their start and end apart: 34, of which 14 were waited for; matrix products, arithmetic and copies ran while one was open for 2% of the time, Pallas kernels for 22%

profile of v2, /device:TPU:0, one launch (start us, length us, event | category | flops | bytes accessed | tf_op | source)
XLA Modules:
  0.0 125.6 jit_solution(16952725969895314489)
XLA Ops:
  5.9 2.4 %gather.1 = (f32[4,3,8,2,16,128]{5,4,3,2,1,0:T(8,128)S(1)}, f32[4,3,2,16,128]{4,3,2,1,0:T(8,128)S(1)}, f32[6,16,128]{2,1,0:T(8,128)S(1)}, f32[6,16,128]{2,1,0:T(...) custom-call(s32[32]{0:T(128)S(1)} %concatenate.3.refs_0_, f32[8,3,4,4096]{3,2,1,0:T(4,128)S(1)} %bitcast.11, ...), custom_call_target="tpu_custom_call" | custom-call | flops 2000000 | bytes 1000000 | tf_op jit(solution)/shard_map/gather/pallas_call | solution.py:30
  8.2 4.8 %collective-permute-start.2 = (f32[4,3,2,16,128]{4,3,2,1,0:T(8,128)S(1)}, f32[4,3,2,16,128]{4,3,2,1,0:T(8,128)S(1)}, u32[]{:S(2)}, u32[]{:S(2)}) collective-permute-start(f32[4,3,2,16,128]{4,3,2,1,0:T(8,128)S(1)} %get-tuple-element.54), channel_id=1, source_target_pairs={{0,16},{8,24},{1,17},{9,25},{2,18},{10,26},{3,19},{11,27},{4,20},{... | collective-permute-start | bytes 589832 | tf_op jit(solution)/shard_map/ppermute | solution.py:592
  18.0 4.8 %residual_inner.1 = (f32[4,3,8,2,16,128]{5,4,3,2,1,0:T(8,128)S(1)}, f32[4,3,8,2,16,128]{5,4,3,2,1,0:T(8,128)}) custom-call(s32[32]{0:T(128)S(1)} %concatenate.3.refs_0_, f32[4,13,2,16,128]{4,3,2,1,0:T(8,128)S(1)} %get-tuple-element.51.refs_1_, f32[4,3,8,2,16,128]{5,4,3,2,1,0:T(8,128)S(1)} %get-tuple-element.52.refs_2_, f32[8,3,4,4096]{3,2,1,0:T(4,128)S(1)} %bitcast.14, ...), custom_call_target="tpu_custom_call" | custom-call | flops 20000000 | bytes 1000000 | tf_op jit(solution)/shard_map/residual_inner/pallas_call | solution.py:30
  22.9 2.5 %residual_outer.1 = (f32[4,3,8,2,16,128]{5,4,3,2,1,0:T(8,128)S(1)}, f32[4,3,8,2,16,128]{5,4,3,2,1,0:T(8,128)S(1)}, f32[4,3,2,16,128]{4,3,2,1,0:T(8,128)S(1)}) custom-call(s32[32]{0:T(128)S(1)} %concatenate.3.refs_0_, f32[4,13,2,16,128]{4,3,2,1,0:T(8,128)S(1)} %get-tuple-element.51.refs_1_, f32[4,3,8,2,16,128]{5,4,3,2,1,0:T(8,128)S(1)} %get-tuple-element.53.refs_2_, ...), custom_call_target="tpu_custom_call" | custom-call | flops 2000000 | bytes 1000000 | tf_op jit(solution)/shard_map/residual_outer/pallas_call | solution.py:30
  25.4 5.7 %collective-permute-done.7.refs_3_ = f32[4,3,2,16,128]{4,3,2,1,0:T(8,128)S(1)} collective-permute-done((f32[4,3,2,16,128]{4,3,2,1,0:T(8,128)S(1)}, f32[4,3,2,16,128]{4,3,2,1,0:T(8,128)S(1)}, u32[]{:S(2)}, u32[]{:S(2)}) %collective-permute-start.7) | collective-permute-done | bytes 196640 | tf_op jit(solution)/shard_map/ppermute | solution.py:614
  32.8 2.3 %collective-permute-start.10 = (f32[6,2,16,128]{3,2,1,0:T(8,128)S(1)}, f32[6,2,16,128]{3,2,1,0:T(8,128)S(1)}, u32[]{:S(2)}, u32[]{:S(2)}) collective-permute-start(f32[6,2,16,128]{3,2,1,0:T(8,128)S(1)} %get-tuple-element.66), channel_id=1, source_target_pairs={{0,8},{8,0},{16,24},{24,16},{1,9},{9,1},{17,25},{25,17},{2,10},{10... | collective-permute-start | bytes 294920 | tf_op jit(solution)/shard_map/ppermute | solution.py:97
  36.7 3.1 %sweep_inner.4.refs_2_ = f32[4,3,8,2,16,128]{5,4,3,2,1,0:T(8,128)S(1)} custom-call(s32[32]{0:T(128)S(1)} %concatenate.3.refs_0_, f32[4,13,2,16,128]{4,3,2,1,0:T(8,128)S(1)} %get-tuple-element.51.refs_1_, f32[4,3,8,2,16,128]{5,4,3,2,1,0:T(8,128)S(1)} %get-tuple-element.62.refs_2_, f32[4,3,8,2,16,128]{5,4,3,2,1,0:T(8,128)S(1)} %get-tuple-element.63.refs_3_), custom_call_target="tpu_custom_call" | custom-call | flops 20000000 | bytes 1000000 | tf_op jit(solution)/shard_map/sweep_inner/pallas_call | solution.py:30
  40.4 2.4 %sweep_outer.4 = (f32[4,3,8,2,16,128]{5,4,3,2,1,0:T(8,128)S(1)}, f32[4,3,2,16,128]{4,3,2,1,0:T(8,128)S(1)}) custom-call(s32[32]{0:T(128)S(1)} %concatenate.3.refs_0_, f32[4,13,2,16,128]{4,3,2,1,0:T(8,128)S(1)} %get-tuple-element.51.refs_1_, f32[4,3,8,2,16,128]{5,4,3,2,1,0:T(8,128)S(1)} %sweep_inner.4.refs_2_, ...), custom_call_target="tpu_custom_call" | custom-call | flops 2000000 | bytes 1000000 | tf_op jit(solution)/shard_map/sweep_outer/pallas_call | solution.py:30
  43.2 5.7 %collective-permute-done.12.refs_3_ = f32[4,3,2,16,128]{4,3,2,1,0:T(8,128)S(1)} collective-permute-done((f32[4,3,2,16,128]{4,3,2,1,0:T(8,128)S(1)}, f32[4,3,2,16,128]{4,3,2,1,0:T(8,128)S(1)}, u32[]{:S(2)}, u32[]{:S(2)}) %collective-permute-start.12) | collective-permute-done | bytes 196640 | tf_op jit(solution)/shard_map/ppermute | solution.py:614
  55.5 3.1 %sweep_inner.5.refs_2_ = f32[4,3,8,2,16,128]{5,4,3,2,1,0:T(8,128)S(1)} custom-call(s32[32]{0:T(128)S(1)} %concatenate.3.refs_0_, f32[4,13,2,16,128]{4,3,2,1,0:T(8,128)S(1)} %get-tuple-element.51.refs_1_, f32[4,3,8,2,16,128]{5,4,3,2,1,0:T(8,128)S(1)} %get-tuple-element.70.refs_2_, f32[4,3,8,2,16,128]{5,4,3,2,1,0:T(8,128)S(1)} %get-tuple-element.63.refs_3_), custom_call_target="tpu_custom_call" | custom-call | flops 20000000 | bytes 1000000 | tf_op jit(solution)/shard_map/sweep_inner/pallas_call | solution.py:30
  59.5 2.4 %sweep_outer.5 = (f32[4,3,8,2,16,128]{5,4,3,2,1,0:T(8,128)S(1)}, f32[4,3,2,16,128]{4,3,2,1,0:T(8,128)S(1)}) custom-call(s32[32]{0:T(128)S(1)} %concatenate.3.refs_0_, f32[4,13,2,16,128]{4,3,2,1,0:T(8,128)S(1)} %get-tuple-element.51.refs_1_, f32[4,3,8,2,16,128]{5,4,3,2,1,0:T(8,128)S(1)} %sweep_inner.5.refs_2_, ...), custom_call_target="tpu_custom_call" | custom-call | flops 2000000 | bytes 1000000 | tf_op jit(solution)/shard_map/sweep_outer/pallas_call | solution.py:30
  62.4 6.5 %collective-permute-done.17.refs_3_ = f32[4,3,2,16,128]{4,3,2,1,0:T(8,128)S(1)} collective-permute-done((f32[4,3,2,16,128]{4,3,2,1,0:T(8,128)S(1)}, f32[4,3,2,16,128]{4,3,2,1,0:T(8,128)S(1)}, u32[]{:S(2)}, u32[]{:S(2)}) %collective-permute-start.17) | collective-permute-done | bytes 196640 | tf_op jit(solution)/shard_map/ppermute | solution.py:614
  72.8 3.1 %sweep_inner.6.refs_2_ = f32[4,3,8,2,16,128]{5,4,3,2,1,0:T(8,128)S(1)} custom-call(s32[32]{0:T(128)S(1)} %concatenate.3.refs_0_, f32[4,13,2,16,128]{4,3,2,1,0:T(8,128)S(1)} %get-tuple-element.51.refs_1_, f32[4,3,8,2,16,128]{5,4,3,2,1,0:T(8,128)S(1)} %get-tuple-element.77.refs_2_, f32[4,3,8,2,16,128]{5,4,3,2,1,0:T(8,128)S(1)} %get-tuple-element.63.refs_3_), custom_call_target="tpu_custom_call" | custom-call | flops 20000000 | bytes 1000000 | tf_op jit(solution)/shard_map/sweep_inner/pallas_call | solution.py:30
  76.3 2.4 %sweep_outer.6 = (f32[4,3,8,2,16,128]{5,4,3,2,1,0:T(8,128)S(1)}, f32[4,3,2,16,128]{4,3,2,1,0:T(8,128)S(1)}) custom-call(s32[32]{0:T(128)S(1)} %concatenate.3.refs_0_, f32[4,13,2,16,128]{4,3,2,1,0:T(8,128)S(1)} %get-tuple-element.51.refs_1_, f32[4,3,8,2,16,128]{5,4,3,2,1,0:T(8,128)S(1)} %sweep_inner.6.refs_2_, ...), custom_call_target="tpu_custom_call" | custom-call | flops 2000000 | bytes 1000000 | tf_op jit(solution)/shard_map/sweep_outer/pallas_call | solution.py:30
  79.2 5.4 %collective-permute-done.22.refs_3_ = f32[4,3,2,16,128]{4,3,2,1,0:T(8,128)S(1)} collective-permute-done((f32[4,3,2,16,128]{4,3,2,1,0:T(8,128)S(1)}, f32[4,3,2,16,128]{4,3,2,1,0:T(8,128)S(1)}, u32[]{:S(2)}, u32[]{:S(2)}) %collective-permute-start.22) | collective-permute-done | bytes 196640 | tf_op jit(solution)/shard_map/ppermute | solution.py:614
  86.2 1.9 %collective-permute-start.25 = (f32[6,2,16,128]{3,2,1,0:T(8,128)S(1)}, f32[6,2,16,128]{3,2,1,0:T(8,128)S(1)}, u32[]{:S(2)}, u32[]{:S(2)}) collective-permute-start(f32[6,2,16,128]{3,2,1,0:T(8,128)S(1)} %get-tuple-element.87), channel_id=1, source_target_pairs={{0,8},{8,0},{16,24},{24,16},{1,9},{9,1},{17,25},{25,17},{2,10},{10... | collective-permute-start | bytes 294920 | tf_op jit(solution)/shard_map/ppermute | solution.py:97
  88.8 2.5 %collective-permute-start.23 = (f32[6,16,128]{2,1,0:T(8,128)S(1)}, f32[6,16,128]{2,1,0:T(8,128)S(1)}, u32[]{:S(2)}, u32[]{:S(2)}) collective-permute-start(f32[6,16,128]{2,1,0:T(8,128)S(1)} %get-tuple-element.85), channel_id=1, source_target_pairs={{0,1},{1,0},{2,3},{3,2},{4,5},{5,4},{6,7},{7,6},{8,9},{9,8},{10,11... | collective-permute-start | bytes 147464 | tf_op jit(solution)/shard_map/ppermute | solution.py:88
  92.0 3.1 %sweep_inner.7.refs_2_ = f32[4,3,8,2,16,128]{5,4,3,2,1,0:T(8,128)S(1)} custom-call(s32[32]{0:T(128)S(1)} %concatenate.3.refs_0_, f32[4,13,2,16,128]{4,3,2,1,0:T(8,128)S(1)} %get-tuple-element.51.refs_1_, f32[4,3,8,2,16,128]{5,4,3,2,1,0:T(8,128)S(1)} %get-tuple-element.84.refs_2_, f32[4,3,8,2,16,128]{5,4,3,2,1,0:T(8,128)S(1)} %get-tuple-element.63.refs_3_), custom_call_target="tpu_custom_call" | custom-call | flops 20000000 | bytes 1000000 | tf_op jit(solution)/shard_map/sweep_inner/pallas_call | solution.py:30
  95.6 2.4 %sweep_outer.7 = (f32[4,3,8,2,16,128]{5,4,3,2,1,0:T(8,128)S(1)}, f32[4,3,2,16,128]{4,3,2,1,0:T(8,128)S(1)}) custom-call(s32[32]{0:T(128)S(1)} %concatenate.3.refs_0_, f32[4,13,2,16,128]{4,3,2,1,0:T(8,128)S(1)} %get-tuple-element.51.refs_1_, f32[4,3,8,2,16,128]{5,4,3,2,1,0:T(8,128)S(1)} %sweep_inner.7.refs_2_, ...), custom_call_target="tpu_custom_call" | custom-call | flops 2000000 | bytes 1000000 | tf_op jit(solution)/shard_map/sweep_outer/pallas_call | solution.py:30
  98.3 6.6 %collective-permute-done.27.refs_3_.refs_4_ = f32[4,3,2,16,128]{4,3,2,1,0:T(8,128)S(1)} collective-permute-done((f32[4,3,2,16,128]{4,3,2,1,0:T(8,128)S(1)}, f32[4,3,2,16,128]{4,3,2,1,0:T(8,128)S(1)}, u32[]{:S(2)}, u32[]{:S(2)}) %collective-permute-start.27) | collective-permute-done | bytes 196640 | tf_op jit(solution)/shard_map/ppermute | solution.py:614
  106.6 2.5 %velocity.1 = (f32[8,3,4,4096]{3,2,1,0:T(4,128)}, f32[4,3,4,4096]{3,2,1,0:T(4,128)S(1)}) custom-call(s32[32]{0:T(128)S(1)} %concatenate.3.refs_0_, f32[8,3,4,4096]{3,2,1,0:T(4,128)S(1)} %bitcast.12, f32[8,3,4,4096]{3,2,1,0:T(4,128)S(1)} %collective-permute-done.refs_2_, f32[4,3,8,2,16,128]{5,4,3,2,1,0:T(8,128)S(1)} %get-tuple-element.91.refs_3_.refs_2_), custom_call_target="tpu_custom_call" | custom-call | flops 2000000 | bytes 1000000 | tf_op jit(solution)/shard_map/velocity/pallas_call | solution.py:30
  111.7 3.1 %final_inner.1.refs_2_ = f32[4,3,8,2,16,128]{5,4,3,2,1,0:T(8,128)S(1)} custom-call(s32[32]{0:T(128)S(1)} %concatenate.3.refs_0_, f32[4,13,2,16,128]{4,3,2,1,0:T(8,128)S(1)} %get-tuple-element.51.refs_1_, f32[4,3,8,2,16,128]{5,4,3,2,1,0:T(8,128)S(1)} %get-tuple-element.91.refs_3_.refs_2_, f32[4,3,8,2,16,128]{5,4,3,2,1,0:T(8,128)S(1)} %get-tuple-element.63.refs_3_, ...), custom_call_target="tpu_custom_call" | custom-call | flops 20000000 | bytes 1000000 | tf_op jit(solution)/shard_map/final_inner/pallas_call | solution.py:30
  114.9 3.9 %final_outer.1 = (f32[8,3,4,4096]{3,2,1,0:T(4,128)}, f32[4,3,4,4096]{3,2,1,0:T(4,128)S(1)}) custom-call(s32[32]{0:T(128)S(1)} %concatenate.3.refs_0_, f32[4,13,2,16,128]{4,3,2,1,0:T(8,128)S(1)} %get-tuple-element.51.refs_1_, f32[4,3,8,2,16,128]{5,4,3,2,1,0:T(8,128)S(1)} %final_inner.1.refs_2_, f32[6,16,128]{2,1,0:T(8,128)S(1)} %collective-permute-done.29.refs_3_, ...), custom_call_target="tpu_custom_call" | custom-call | flops 2000000 | bytes 1000000 | tf_op jit(solution)/shard_map/final_outer/pallas_call | solution.py:30
  118.8 3.6 %collective-permute-start.33 = (f32[4,3,4,4096]{3,2,1,0:T(4,128)S(1)}, f32[4,3,4,4096]{3,2,1,0:T(4,128)S(1)}, u32[]{:S(2)}, u32[]{:S(2)}) collective-permute-start(f32[4,3,4,4096]{3,2,1,0:T(4,128)S(1)} %get-tuple-element.99), channel_id=1, source_target_pairs={{0,8},{8,0},{16,24},{24,16},{1,9},{9,1},{17,25},{25,17},{2,10},{10... | collective-permute-start | bytes 2359304 | tf_op jit(solution)/shard_map/ppermute | solution.py:97
  (86 shorter events, 38.6 us)
Async XLA Ops:
  1.2 14.2 %collective-permute-start.1 = (f32[8,3,4,4096]{3,2,1,0:T(4,128)}, f32[8,3,4,4096]{3,2,1,0:T(4,128)S(1)}, u32[]{:S(2)}, u32[]{:S(2)}) collective-permute-start(f32[8,3,4,4096]{3,2,1,0:T(4,128)} %bitcast.13), channel_id=1, source_target_pairs={{0,8},{8,0},{16,24},{24,16},{1,9},{9,1},{17,25},{25,17},{2,10},{10... | collective-permute-start | bytes 4718600 | tf_op jit(solution)/shard_map/ppermute | solution.py:97
  8.2 14.6 %collective-permute-start.2 = (f32[4,3,2,16,128]{4,3,2,1,0:T(8,128)S(1)}, f32[4,3,2,16,128]{4,3,2,1,0:T(8,128)S(1)}, u32[]{:S(2)}, u32[]{:S(2)}) collective-permute-start(f32[4,3,2,16,128]{4,3,2,1,0:T(8,128)S(1)} %get-tuple-element.54), channel_id=1, source_target_pairs={{0,16},{8,24},{1,17},{9,25},{2,18},{10,26},{3,19},{11,27},{4,20},{... | collective-permute-start | bytes 589832 | tf_op jit(solution)/shard_map/ppermute | solution.py:592
  13.0 9.8 %collective-permute-start.5 = (f32[6,2,16,128]{3,2,1,0:T(8,128)S(1)}, f32[6,2,16,128]{3,2,1,0:T(8,128)S(1)}, u32[]{:S(2)}, u32[]{:S(2)}) collective-permute-start(f32[6,2,16,128]{3,2,1,0:T(8,128)S(1)} %get-tuple-element.58), channel_id=1, source_target_pairs={{0,8},{8,0},{16,24},{24,16},{1,9},{9,1},{17,25},{25,17},{2,10},{10... | collective-permute-start | bytes 294920 | tf_op jit(solution)/shard_map/ppermute | solution.py:97
  13.1 9.8 %collective-permute-start.6 = (f32[6,2,16,128]{3,2,1,0:T(8,128)S(1)}, f32[6,2,16,128]{3,2,1,0:T(8,128)S(1)}, u32[]{:S(2)}, u32[]{:S(2)}) collective-permute-start(f32[6,2,16,128]{3,2,1,0:T(8,128)S(1)} %get-tuple-element.59), channel_id=1, source_target_pairs={{4,8},{5,9},{6,10},{7,11},{8,4},{9,5},{10,6},{11,7},{20,24},{21,25... | collective-permute-start | bytes 294920 | tf_op jit(solution)/shard_map/ppermute | solution.py:86
  13.8 9.1 %collective-permute-start.3 = (f32[6,16,128]{2,1,0:T(8,128)S(1)}, f32[6,16,128]{2,1,0:T(8,128)S(1)}, u32[]{:S(2)}, u32[]{:S(2)}) collective-permute-start(f32[6,16,128]{2,1,0:T(8,128)S(1)} %get-tuple-element.56), channel_id=1, source_target_pairs={{0,1},{1,0},{2,3},{3,2},{4,5},{5,4},{6,7},{7,6},{8,9},{9,8},{10,11... | collective-permute-start | bytes 147464 | tf_op jit(solution)/shard_map/ppermute | solution.py:88
  15.3 7.5 %collective-permute-start.4 = (f32[6,16,128]{2,1,0:T(8,128)S(1)}, f32[6,16,128]{2,1,0:T(8,128)S(1)}, u32[]{:S(2)}, u32[]{:S(2)}) collective-permute-start(f32[6,16,128]{2,1,0:T(8,128)S(1)} %get-tuple-element.57), channel_id=1, source_target_pairs={{0,2},{1,3},{2,0},{3,1},{4,6},{5,7},{6,4},{7,5},{8,10},{9,11},{10,... | collective-permute-start | bytes 147464 | tf_op jit(solution)/shard_map/ppermute | solution.py:91
  25.3 5.7 %collective-permute-start.7 = (f32[4,3,2,16,128]{4,3,2,1,0:T(8,128)S(1)}, f32[4,3,2,16,128]{4,3,2,1,0:T(8,128)S(1)}, u32[]{:S(2)}, u32[]{:S(2)}) collective-permute-start(f32[4,3,2,16,128]{4,3,2,1,0:T(8,128)S(1)} %get-tuple-element.61.refs_4_), channel_id=1, source_target_pairs={{0,16},{8,24},{16,0},{24,8},{1,17},{9,25},{17,1},{25,9},{2,18},{10... | collective-permute-start | bytes 589832 | tf_op jit(solution)/shard_map/ppermute | solution.py:614
  32.8 7.6 %collective-permute-start.10 = (f32[6,2,16,128]{3,2,1,0:T(8,128)S(1)}, f32[6,2,16,128]{3,2,1,0:T(8,128)S(1)}, u32[]{:S(2)}, u32[]{:S(2)}) collective-permute-start(f32[6,2,16,128]{3,2,1,0:T(8,128)S(1)} %get-tuple-element.66), channel_id=1, source_target_pairs={{0,8},{8,0},{16,24},{24,16},{1,9},{9,1},{17,25},{25,17},{2,10},{10... | collective-permute-start | bytes 294920 | tf_op jit(solution)/shard_map/ppermute | solution.py:97
  35.1 5.3 %collective-permute-start.11 = (f32[6,2,16,128]{3,2,1,0:T(8,128)S(1)}, f32[6,2,16,128]{3,2,1,0:T(8,128)S(1)}, u32[]{:S(2)}, u32[]{:S(2)}) collective-permute-start(f32[6,2,16,128]{3,2,1,0:T(8,128)S(1)} %get-tuple-element.67), channel_id=1, source_target_pairs={{4,8},{5,9},{6,10},{7,11},{8,4},{9,5},{10,6},{11,7},{20,24},{21,25... | collective-permute-start | bytes 294920 | tf_op jit(solution)/shard_map/ppermute | solution.py:86
  42.8 6.0 %collective-permute-start.12 = (f32[4,3,2,16,128]{4,3,2,1,0:T(8,128)S(1)}, f32[4,3,2,16,128]{4,3,2,1,0:T(8,128)S(1)}, u32[]{:S(2)}, u32[]{:S(2)}) collective-permute-start(f32[4,3,2,16,128]{4,3,2,1,0:T(8,128)S(1)} %get-tuple-element.69.refs_4_), channel_id=1, source_target_pairs={{0,16},{8,24},{16,0},{24,8},{1,17},{9,25},{17,1},{25,9},{2,18},{10... | collective-permute-start | bytes 589832 | tf_op jit(solution)/shard_map/ppermute | solution.py:614
  50.5 9.0 %collective-permute-start.15 = (f32[6,2,16,128]{3,2,1,0:T(8,128)S(1)}, f32[6,2,16,128]{3,2,1,0:T(8,128)S(1)}, u32[]{:S(2)}, u32[]{:S(2)}) collective-permute-start(f32[6,2,16,128]{3,2,1,0:T(8,128)S(1)} %get-tuple-element.73), channel_id=1, source_target_pairs={{0,8},{8,0},{16,24},{24,16},{1,9},{9,1},{17,25},{25,17},{2,10},{10... | collective-permute-start | bytes 294920 | tf_op jit(solution)/shard_map/ppermute | solution.py:97
  52.3 7.3 %collective-permute-start.16 = (f32[6,2,16,128]{3,2,1,0:T(8,128)S(1)}, f32[6,2,16,128]{3,2,1,0:T(8,128)S(1)}, u32[]{:S(2)}, u32[]{:S(2)}) collective-permute-start(f32[6,2,16,128]{3,2,1,0:T(8,128)S(1)} %get-tuple-element.74), channel_id=1, source_target_pairs={{4,8},{5,9},{6,10},{7,11},{8,4},{9,5},{10,6},{11,7},{20,24},{21,25... | collective-permute-start | bytes 294920 | tf_op jit(solution)/shard_map/ppermute | solution.py:86
  52.9 5.7 %collective-permute-start.13 = (f32[6,16,128]{2,1,0:T(8,128)S(1)}, f32[6,16,128]{2,1,0:T(8,128)S(1)}, u32[]{:S(2)}, u32[]{:S(2)}) collective-permute-start(f32[6,16,128]{2,1,0:T(8,128)S(1)} %get-tuple-element.71), channel_id=1, source_target_pairs={{0,1},{1,0},{2,3},{3,2},{4,5},{5,4},{6,7},{7,6},{8,9},{9,8},{10,11... | collective-permute-start | bytes 147464 | tf_op jit(solution)/shard_map/ppermute | solution.py:88
  54.5 5.0 %collective-permute-start.14 = (f32[6,16,128]{2,1,0:T(8,128)S(1)}, f32[6,16,128]{2,1,0:T(8,128)S(1)}, u32[]{:S(2)}, u32[]{:S(2)}) collective-permute-start(f32[6,16,128]{2,1,0:T(8,128)S(1)} %get-tuple-element.72), channel_id=1, source_target_pairs={{0,2},{1,3},{2,0},{3,1},{4,6},{5,7},{6,4},{7,5},{8,10},{9,11},{10,... | collective-permute-start | bytes 147464 | tf_op jit(solution)/shard_map/ppermute | solution.py:91
  62.0 7.0 %collective-permute-start.17 = (f32[4,3,2,16,128]{4,3,2,1,0:T(8,128)S(1)}, f32[4,3,2,16,128]{4,3,2,1,0:T(8,128)S(1)}, u32[]{:S(2)}, u32[]{:S(2)}) collective-permute-start(f32[4,3,2,16,128]{4,3,2,1,0:T(8,128)S(1)} %get-tuple-element.76.refs_4_), channel_id=1, source_target_pairs={{0,16},{8,24},{16,0},{24,8},{1,17},{9,25},{17,1},{25,9},{2,18},{10... | collective-permute-start | bytes 589832 | tf_op jit(solution)/shard_map/ppermute | solution.py:614
  70.6 5.6 %collective-permute-start.20 = (f32[6,2,16,128]{3,2,1,0:T(8,128)S(1)}, f32[6,2,16,128]{3,2,1,0:T(8,128)S(1)}, u32[]{:S(2)}, u32[]{:S(2)}) collective-permute-start(f32[6,2,16,128]{3,2,1,0:T(8,128)S(1)} %get-tuple-element.80), channel_id=1, source_target_pairs={{0,8},{8,0},{16,24},{24,16},{1,9},{9,1},{17,25},{25,17},{2,10},{10... | collective-permute-start | bytes 294920 | tf_op jit(solution)/shard_map/ppermute | solution.py:97
  78.7 5.8 %collective-permute-start.22 = (f32[4,3,2,16,128]{4,3,2,1,0:T(8,128)S(1)}, f32[4,3,2,16,128]{4,3,2,1,0:T(8,128)S(1)}, u32[]{:S(2)}, u32[]{:S(2)}) collective-permute-start(f32[4,3,2,16,128]{4,3,2,1,0:T(8,128)S(1)} %get-tuple-element.83.refs_4_), channel_id=1, source_target_pairs={{0,16},{8,24},{16,0},{24,8},{1,17},{9,25},{17,1},{25,9},{2,18},{10... | collective-permute-start | bytes 589832 | tf_op jit(solution)/shard_map/ppermute | solution.py:614
  86.2 9.4 %collective-permute-start.25 = (f32[6,2,16,128]{3,2,1,0:T(8,128)S(1)}, f32[6,2,16,128]{3,2,1,0:T(8,128)S(1)}, u32[]{:S(2)}, u32[]{:S(2)}) collective-permute-start(f32[6,2,16,128]{3,2,1,0:T(8,128)S(1)} %get-tuple-element.87), channel_id=1, source_target_pairs={{0,8},{8,0},{16,24},{24,16},{1,9},{9,1},{17,25},{25,17},{2,10},{10... | collective-permute-start | bytes 294920 | tf_op jit(solution)/shard_map/ppermute | solution.py:97
  88.2 7.5 %collective-permute-start.26 = (f32[6,2,16,128]{3,2,1,0:T(8,128)S(1)}, f32[6,2,16,128]{3,2,1,0:T(8,128)S(1)}, u32[]{:S(2)}, u32[]{:S(2)}) collective-permute-start(f32[6,2,16,128]{3,2,1,0:T(8,128)S(1)} %get-tuple-element.88), channel_id=1, source_target_pairs={{4,8},{5,9},{6,10},{7,11},{8,4},{9,5},{10,6},{11,7},{20,24},{21,25... | collective-permute-start | bytes 294920 | tf_op jit(solution)/shard_map/ppermute | solution.py:86
  88.8 6.2 %collective-permute-start.23 = (f32[6,16,128]{2,1,0:T(8,128)S(1)}, f32[6,16,128]{2,1,0:T(8,128)S(1)}, u32[]{:S(2)}, u32[]{:S(2)}) collective-permute-start(f32[6,16,128]{2,1,0:T(8,128)S(1)} %get-tuple-element.85), channel_id=1, source_target_pairs={{0,1},{1,0},{2,3},{3,2},{4,5},{5,4},{6,7},{7,6},{8,9},{9,8},{10,11... | collective-permute-start | bytes 147464 | tf_op jit(solution)/shard_map/ppermute | solution.py:88
  98.1 6.8 %collective-permute-start.27 = (f32[4,3,2,16,128]{4,3,2,1,0:T(8,128)S(1)}, f32[4,3,2,16,128]{4,3,2,1,0:T(8,128)S(1)}, u32[]{:S(2)}, u32[]{:S(2)}) collective-permute-start(f32[4,3,2,16,128]{4,3,2,1,0:T(8,128)S(1)} %get-tuple-element.90.refs_4_.refs_5_), channel_id=1, source_target_pairs={{0,16},{8,24},{16,0},{24,8},{1,17},{9,25},{17,1},{25,9},{2,18},{10... | collective-permute-start | bytes 589832 | tf_op jit(solution)/shard_map/ppermute | solution.py:614
  109.1 13.4 %collective-permute-start.28 = (f32[4,3,4,4096]{3,2,1,0:T(4,128)S(1)}, f32[4,3,4,4096]{3,2,1,0:T(4,128)S(1)}, u32[]{:S(2)}, u32[]{:S(2)}) collective-permute-start(f32[4,3,4,4096]{3,2,1,0:T(4,128)S(1)} %get-tuple-element.93), channel_id=1, source_target_pairs={{0,8},{8,0},{16,24},{24,16},{1,9},{9,1},{17,25},{25,17},{2,10},{10... | collective-permute-start | bytes 2359304 | tf_op jit(solution)/shard_map/ppermute | solution.py:97
  110.0 4.9 %collective-permute-start.31 = (f32[6,2,16,128]{3,2,1,0:T(8,128)S(1)}, f32[6,2,16,128]{3,2,1,0:T(8,128)S(1)}, u32[]{:S(2)}, u32[]{:S(2)}) collective-permute-start(f32[6,2,16,128]{3,2,1,0:T(8,128)S(1)} %get-tuple-element.96), channel_id=1, source_target_pairs={{0,8},{8,0},{16,24},{24,16},{1,9},{9,1},{17,25},{25,17},{2,10},{10... | collective-permute-start | bytes 294920 | tf_op jit(solution)/shard_map/ppermute | solution.py:97
  118.8 5.5 %collective-permute-start.33 = (f32[4,3,4,4096]{3,2,1,0:T(4,128)S(1)}, f32[4,3,4,4096]{3,2,1,0:T(4,128)S(1)}, u32[]{:S(2)}, u32[]{:S(2)}) collective-permute-start(f32[4,3,4,4096]{3,2,1,0:T(4,128)S(1)} %get-tuple-element.99), channel_id=1, source_target_pairs={{0,8},{8,0},{16,24},{24,16},{1,9},{9,1},{17,25},{25,17},{2,10},{10... | collective-permute-start | bytes 2359304 | tf_op jit(solution)/shard_map/ppermute | solution.py:97
  (18 other events, 101.1 us)

commit v3 on v2

--- a/solution.py
+++ b/solution.py
@@ -12,6 +12,8 @@
 ALPHA_SCALE = 0.1
 WINDOW_SLICES = 16
 SWEEPS = 5
+STREAMS = ((0, 3),)
+WORK = 6_000_000
 XP, XM, YP, YM, ZP, ZM, XG, YG, ZG, Q, INV, K0 = range(12)
 CORE, CHIP, SIDE_X, SIDE_Y, HOLD = range(5)
 F32 = jnp.float32
@@ -40,7 +42,9 @@
 
 
 class Shape:
-    def __init__(self, slots, local, n_time, places):
+    def __init__(self, slots, local, n_time, places, base, comps):
+        self.base = base
+        self.comps = comps
         self.slots = slots
         self.half = slots // 2
         self.local = local
@@ -50,12 +54,14 @@
         self.bits = [[b for b in range(levels) if b % 3 == d] for d in range(3)]
         self.y_per = max(1, 8 // self.span)
         self.z_per = max(1, 16 // self.span)
-        self.x_shape = (2 * COMPONENTS, self.span * 2, LANES)
-        self.y_shape = (-(-2 // self.y_per) * COMPONENTS, EDGE, LANES)
-        self.z_shape = tile_shape(-(-self.half // self.z_per) * COMPONENTS)
+        self.x_shape = (2 * comps, self.span * 2, LANES)
+        self.y_shape = (-(-2 // self.y_per) * comps, EDGE, LANES)
+        self.z_shape = tile_shape(-(-self.half // self.z_per) * comps)
         self.x_count = len(self.bits[0])
-        self.field = tile_shape(self.half, COMPONENTS, self.span)
-        self.slice = tile_shape(self.half, COMPONENTS)
+        self.field = tile_shape(self.half, comps, self.span)
+        self.slice = tile_shape(self.half, comps)
+        self.messages = [self.x_shape] * self.x_count + [self.y_shape, self.z_shape, self.z_shape]
+        self.z_ghost = pltpu.VMEM((2,) + self.z_shape, F32)
 
 
 def position(place, bits):
@@ -97,21 +103,38 @@
     return lax.ppermute(value, "tm", [(t, t ^ 1) for t in range(n_time)])
 
 
+def over_components(sh, visit):
+    if sh.comps == 1:
+        visit(0)
+        return
+
+    def step(comp, _):
+        visit(comp)
+        return 0
+
+    lax.fori_loop(0, sh.comps, step, 0)
+
+
+def over_tiles(sh, visit):
+    def all_slots(comp):
+        for j in range(sh.half):
+            visit(j, comp)
+
+    over_components(sh, all_slots)
+
+
 def pack_faces(sh, flags, tile, src, outs):
     core = flags[CORE]
     lane = iota((EDGE, LANES), 1)
     within, group_of_lane = lane % EDGE, lane // EDGE
     x_outs, y_out, inner_out, z_out = outs[:-3], outs[-3], outs[-2], outs[-1]
     side_y = flags[SIDE_Y]
-    y_groups = -(-2 // sh.y_per)
-
-    for g in range(-(-sh.half // sh.z_per)):
-        slots = range(g * sh.z_per, min(sh.half, (g + 1) * sh.z_per))
-
-        def comp_step(comp, _, g=g, slots=slots):
+
+    def pack(comp):
+        for g in range(-(-sh.half // sh.z_per)):
             low = [jnp.zeros((EDGE, LANES), F32)] * 2
             high = [jnp.zeros((EDGE, LANES), F32)] * 2
-            for j in slots:
+            for j in range(g * sh.z_per, min(sh.half, (g + 1) * sh.z_per)):
                 for l in range(sh.span):
                     index = (j % sh.z_per) * sh.span + l
                     for h in range(2):
@@ -120,37 +143,29 @@
                         low[h] = jnp.where(within == index, value, low[h])
                         high[h] = jnp.where(within == (index + EDGE - 1) % EDGE, value, high[h])
             for h in range(2):
-                inner_out[g * COMPONENTS + comp, h] = jnp.where(core == 1, low[h], high[h])
-                z_out[g * COMPONENTS + comp, h] = jnp.where(core == 1, high[h], low[h])
-            for number, x_out in enumerate(x_outs):
-                side = flags[SIDE_X] if number == 0 else 1 - flags[SIDE_X]
-                for jj in range(slots[0] // 2, slots[-1] // 2 + 1):
-                    for l in range(sh.span):
-                        for h in range(2):
-                            upper = src[2 * jj + 1, comp, l, h, EDGE - 1 : EDGE, :]
-                            lower = src[2 * jj, comp, l, h, 0:1, :]
-                            row = slice(2 * l + h, 2 * l + h + 1)
-                            x_out[jj * COMPONENTS + comp, row, :] = jnp.where(
-                                side == 1, upper, lower
-                            )
-            for half in range(slots[0] // 2, slots[-1] // 2 + 1):
-
-                @pl.when(side_y == half)
-                def _(half=half):
-                    for y in range(y_groups):
-                        packed = jnp.zeros((EDGE, LANES), F32)
-                        for jj in range(y * sh.y_per, min(2, (y + 1) * sh.y_per)):
-                            for l in range(sh.span):
-                                index = (jj % sh.y_per) * sh.span + l
-                                layer = src[2 * half + jj, comp, l, half]
-                                shift = EDGE * (index + half) % LANES
-                                layer = pltpu.roll(layer, shift, 1) if shift else layer
-                                packed = jnp.where(group_of_lane == index, layer, packed)
-                        y_out[y * COMPONENTS + comp] = packed
-
-            return 0
-
-        lax.fori_loop(0, COMPONENTS, comp_step, 0)
+                inner_out[g * sh.comps + comp, h] = jnp.where(core == 1, low[h], high[h])
+                z_out[g * sh.comps + comp, h] = jnp.where(core == 1, high[h], low[h])
+        for number, x_out in enumerate(x_outs):
+            side = flags[SIDE_X] if number == 0 else 1 - flags[SIDE_X]
+            for jj in range(2):
+                for l in range(sh.span):
+                    for h in range(2):
+                        upper = src[2 * jj + 1, comp, l, h, EDGE - 1 : EDGE, :]
+                        lower = src[2 * jj, comp, l, h, 0:1, :]
+                        row = slice(2 * l + h, 2 * l + h + 1)
+                        x_out[jj * sh.comps + comp, row, :] = jnp.where(side == 1, upper, lower)
+        for y in range(-(-2 // sh.y_per)):
+            packed = jnp.zeros((EDGE, LANES), F32)
+            for jj in range(y * sh.y_per, min(2, (y + 1) * sh.y_per)):
+                for l in range(sh.span):
+                    index = (jj % sh.y_per) * sh.span + l
+                    layer = src[2 * side_y + jj, comp, l, side_y]
+                    layer = pltpu.roll(layer, EDGE * index, 1) if index else layer
+                    packed = jnp.where(group_of_lane == (index + 7 * side_y) % 8, layer, packed)
+            packed = jnp.where(side_y == 1, pltpu.roll(packed, EDGE, 1), packed)
+            y_out[y * sh.comps + comp] = packed
+
+    over_components(sh, pack)
 
 
 def inner_sum(sh, flags, coef, src, j, comp, l):
@@ -189,8 +204,8 @@
     y_side, y_row = j // 2, j % 2
     y_index = (y_row % sh.y_per) * sh.span + l
     z_index = (j % sh.z_per) * sh.span + l
-    z_group = (j // sh.z_per) * COMPONENTS + comp
-    outer = x_row * COMPONENTS + comp
+    z_group = (j // sh.z_per) * sh.comps + comp
+    outer = x_row * sh.comps + comp
     result = []
     for h in range(2):
         value = total[h]
@@ -198,7 +213,7 @@
             z_ghost[z_index % 2, z_group, h], LANES - EDGE + 1 - z_index, 1
         )
         if h == y_side:
-            group = y_in[(y_row // sh.y_per) * COMPONENTS + comp]
+            group = y_in[(y_row // sh.y_per) * sh.comps + comp]
             shift = ((LANES - EDGE if y_side else 0) - EDGE * y_index) % LANES
             value += coef[j, YG, h] * (pltpu.roll(group, shift, 1) if shift else group)
         row = slice(2 * l + h, 2 * l + h + 1)
@@ -320,46 +335,30 @@
 def assemble(sh, flags, whole, other, field, rows):
     core = flags[CORE]
 
-    def step(k, _):
-        j, comp = k // COMPONENTS, k % COMPONENTS
+    def visit(j, comp):
         slot = core * sh.half + j
         for part, source in enumerate((whole, other)):
             first = (core if part == 0 else 1 - core) * sh.local
 
+            def read(c, source=source):
+                return source[slot, sh.base + comp, :, c * LANES : (c + 1) * LANES]
+
             def write(i, h, value, first=first):
                 field[j, comp, first + i, h] = value
 
-            rows_to_tiles(
-                lambda c, source=source: source[slot, comp, :, c * LANES : (c + 1) * LANES],
-                sh.local,
-                rows.at[part],
-                write,
-            )
-        return 0
-
-    lax.fori_loop(0, sh.half * COMPONENTS, step, 0)
+            rows_to_tiles(read, sh.local, rows.at[2 * j + part], write)
+
+    over_tiles(sh, visit)
 
 
 def gather_kernel(sh, flags, whole, other, field, last, *rest):
     assemble(sh, flags, whole, other, field, rest[-1])
 
-    def step(k, _):
-        j, comp = k // COMPONENTS, k % COMPONENTS
+    def visit(j, comp):
         last[j, comp] = field[j, comp, sh.span - 1]
-        return 0
-
-    lax.fori_loop(0, sh.half * COMPONENTS, step, 0)
+
+    over_tiles(sh, visit)
     pack_faces(sh, flags, lambda j, c, l, h: field[j, c, l, h], field, rest[:-1])
-
-
-def over_tiles(sh, visit):
-    for j in range(sh.half):
-
-        def comp_step(comp, _, j=j):
-            visit(j, comp)
-            return 0
-
-        lax.fori_loop(0, COMPONENTS, comp_step, 0)
 
 
 def residual_inner_kernel(sh, flags, coef, field, whole, other, inner, force, rows):
@@ -392,7 +391,7 @@
             total = [inner[j, comp, l, h] for h in range(2)]
             if l == 0:
                 for h in range(2):
-                    prior = jnp.where(chip == 0, first[j, comp, h], before[j, comp, h])
+                    prior = jnp.where(chip == 0, first[j, sh.base + comp, h], before[j, comp, h])
                     total[h] = total[h] + coef[j, Q, h] * prior
             total = ghost_sum(sh, flags, coef, faces, z_ghost, total, j, comp, l)
             for h in range(2):
@@ -457,27 +456,31 @@
     pack_faces(sh, flags, tile, field, messages)
 
 
-def velocity_kernel(sh, flags, whole, other, field, out, send, rows):
+def store_rows(sh, core, j, tile, keep, pass_on, rows):
+    own, others = core * sh.local, (1 - core) * sh.local
+    tiles_to_rows(lambda i, h: tile(own + i, h), sh.local, rows.at[2 * j], keep)
+    tiles_to_rows(lambda i, h: tile(others + i, h), sh.local, rows.at[2 * j + 1], pass_on)
+
+
+def velocity_kernel(shapes, flags, whole, other, *rest):
     core = flags[CORE]
-
-    def step(k, _):
-        j, comp = k // COMPONENTS, k % COMPONENTS
-        slot = core * sh.half + j
-
-        def keep(c, value):
-            at = slice(c * LANES, (c + 1) * LANES)
-            out[slot, comp, :, at] = whole[slot, comp, :, at] + value
-
-        def pass_on(c, value):
-            at = slice(c * LANES, (c + 1) * LANES)
-            send[j, comp, :, at] = other[slot, comp, :, at] + value
-
-        own, others = core * sh.local, (1 - core) * sh.local
-        tiles_to_rows(lambda i, h: field[j, comp, own + i, h], sh.local, rows.at[0], keep)
-        tiles_to_rows(lambda i, h: field[j, comp, others + i, h], sh.local, rows.at[1], pass_on)
-        return 0
-
-    lax.fori_loop(0, sh.half * COMPONENTS, step, 0)
+    fields, (out, send, rows) = rest[: len(shapes)], rest[len(shapes) :]
+    for sh, field in zip(shapes, fields):
+
+        def visit(j, comp, sh=sh, field=field):
+            slot = core * sh.half + j
+
+            def keep(c, value):
+                at = slice(c * LANES, (c + 1) * LANES)
+                out[slot, sh.base + comp, :, at] = whole[slot, sh.base + comp, :, at] + value
+
+            def pass_on(c, value):
+                at = slice(c * LANES, (c + 1) * LANES)
+                send[j, sh.base + comp, :, at] = other[slot, sh.base + comp, :, at] + value
+
+            store_rows(sh, core, j, lambda l, h: field[j, comp, l, h], keep, pass_on, rows)
+
+        over_tiles(sh, visit)
 
 
 def final_inner_kernel(sh, flags, coef, field, scaled, *rest):
@@ -500,32 +503,34 @@
     over_tiles(sh, visit)
 
 
-def final_outer_kernel(sh, flags, coef, inner, *rest):
-    faces = rest[: sh.x_count + 1]
-    inner_in, z_in, out, send, z_ghost, hold, rows = rest[sh.x_count + 1 :]
-    place_z_ghost(flags, inner_in, z_in, z_ghost)
+def final_outer_kernel(shapes, flags, coef, *rest):
     core = flags[CORE]
-
-    def visit(j, comp):
-        live = flags[HOLD + 6 * sh.half + j].astype(F32)
-        for l in range(sh.span):
-            total = [inner[j, comp, l, h] for h in range(2)]
-            total = ghost_sum(sh, flags, coef, faces, z_ghost, total, j, comp, l)
-            for h in range(2):
-                hold[l, h] = total[h] * (coef[j, INV, h] * live)
-        slot = core * sh.half + j
-
-        def keep(c, value):
-            out[slot, comp, :, c * LANES : (c + 1) * LANES] = value
-
-        def pass_on(c, value):
-            send[j, comp, :, c * LANES : (c + 1) * LANES] = value
-
-        own, others = core * sh.local, (1 - core) * sh.local
-        tiles_to_rows(lambda i, h: hold[own + i, h], sh.local, rows.at[0], keep)
-        tiles_to_rows(lambda i, h: hold[others + i, h], sh.local, rows.at[1], pass_on)
-
-    over_tiles(sh, visit)
+    count = shapes[0].x_count + 4
+    ins, rest = rest[: count * len(shapes)], rest[count * len(shapes) :]
+    out, send, hold, rows, *ghosts = rest
+    for number, (sh, z_ghost) in enumerate(zip(shapes, ghosts)):
+        inner, *faces = ins[number * count : (number + 1) * count]
+        faces, inner_in, z_in = faces[:-2], faces[-2], faces[-1]
+        place_z_ghost(flags, inner_in, z_in, z_ghost)
+
+        def visit(j, comp, sh=sh, z_ghost=z_ghost, inner=inner, faces=faces):
+            live = flags[HOLD + 6 * sh.half + j].astype(F32)
+            for l in range(sh.span):
+                total = [inner[j, comp, l, h] for h in range(2)]
+                total = ghost_sum(sh, flags, coef, faces, z_ghost, total, j, comp, l)
+                for h in range(2):
+                    hold[j, l, h] = total[h] * (coef[j, INV, h] * live)
+            slot = core * sh.half + j
+
+            def keep(c, value):
+                out[slot, sh.base + comp, :, c * LANES : (c + 1) * LANES] = value
+
+            def pass_on(c, value):
+                send[j, sh.base + comp, :, c * LANES : (c + 1) * LANES] = value
+
+            store_rows(sh, core, j, lambda l, h: hold[j, l, h], keep, pass_on, rows)
+
+        over_tiles(sh, visit)
 
 
 def bind(kernel, sh):
@@ -547,7 +552,8 @@
 ):
     n_time, places = lax.axis_size("tm"), lax.axis_size("space")
     slots, local = iterate.shape[:2]
-    sh = Shape(slots, local, n_time, places)
+    shapes = [Shape(slots, local, n_time, places, base, comps) for base, comps in STREAMS]
+    sh = shapes[0]
     half = sh.half
     t, place = lax.axis_index("tm"), lax.axis_index("space")
     core, chip = t % 2, t // 2
@@ -569,80 +575,91 @@
             live.astype(jnp.int32),
         ]
     )
-    rows = pltpu.VMEM((2, CHUNKS * local, LANES), F32)
-    z_ghost = pltpu.VMEM((2,) + sh.z_shape, F32)
-    messages = [sh.x_shape] * sh.x_count + [sh.y_shape, sh.z_shape, sh.z_shape]
+    rows = pltpu.VMEM((2 * half, CHUNKS * local, LANES), F32)
 
     coef, first = call(
         bind(coefficient_kernel, sh),
         flags,
         [viscosity, peclet.transpose(1, 0, 2), initial_velocity.transpose(1, 0, 2)],
-        [tile_shape(half, K0 + sh.chips), sh.slice],
+        [tile_shape(half, K0 + sh.chips), tile_shape(half, COMPONENTS)],
         [pltpu.VMEM((CHUNKS * slots, LANES), F32), pltpu.VMEM(tile_shape(7, slots), F32)],
         name="coefficients",
     )
-    field, last, *out = call(
-        bind(gather_kernel, sh),
-        flags,
-        [velocity, velocity_other],
-        [sh.field, sh.slice] + messages,
-        [rows],
-        name="gather",
-    )
-    before = lax.ppermute(last, "tm", [(a, a + 2) for a in range(n_time - 2)])
-    faces = exchange(sh, out, n_time, places)
-    inner, _ = call(
-        bind(residual_inner_kernel, sh),
-        flags,
-        [coef, field, force, force_other],
-        [sh.field, sh.field],
-        [rows],
-        flops=20_000_000,
-        name="residual_inner",
-    )
-    scaled, partial, last = call(
-        bind(residual_outer_kernel, sh),
-        flags,
-        [coef, inner, before, first] + faces,
-        [sh.field, sh.field, sh.slice],
-        [z_ghost],
-        name="residual_outer",
-    )
-
-    def chip_ends(last):
+    fields, faces, befores = [], [], []
+    for sh in shapes:
+        field, last, *out = call(
+            bind(gather_kernel, sh),
+            flags,
+            [velocity, velocity_other],
+            [sh.field, sh.slice] + sh.messages,
+            [rows],
+            name="gather",
+        )
+        befores.append(lax.ppermute(last, "tm", [(a, a + 2) for a in range(n_time - 2)]))
+        faces.append(exchange(sh, out, n_time, places))
+        fields.append(field)
+
+    def chip_ends(sh, last):
         return [
             lax.ppermute(last, "tm", [(a, (a + 2 * back) % n_time) for a in range(n_time)])
             for back in range(1, sh.chips)
         ] + [last]
 
-    correction = None
+    scaleds, partials, ends = [], [], []
+    for sh, field, before, face in zip(shapes, fields, befores, faces):
+        inner, _ = call(
+            bind(residual_inner_kernel, sh),
+            flags,
+            [coef, field, force, force_other],
+            [sh.field, sh.field],
+            [rows],
+            flops=sh.comps * WORK,
+            name="residual_inner",
+        )
+        scaled, partial, last = call(
+            bind(residual_outer_kernel, sh),
+            flags,
+            [coef, inner, before, first] + face,
+            [sh.field, sh.field, sh.slice],
+            [sh.z_ghost],
+            flops=sh.comps * WORK,
+            name="residual_outer",
+        )
+        scaleds.append(scaled)
+        partials.append(partial)
+        ends.append(chip_ends(sh, last))
+
+    corrections = [None] * len(shapes)
     for sweep in range(SWEEPS):
-        if sweep > 0:
-            (inner,) = call(
-                bind(sweep_inner_kernel, sh),
+        for number, sh in enumerate(shapes):
+            if sweep > 0:
+                (inner,) = call(
+                    bind(sweep_inner_kernel, sh),
+                    flags,
+                    [coef, corrections[number], scaleds[number]],
+                    [sh.field],
+                    flops=sh.comps * WORK,
+                    name="sweep_inner",
+                )
+                partials[number], last = call(
+                    bind(sweep_outer_kernel, sh),
+                    flags,
+                    [coef, inner] + faces[number],
+                    [sh.field, sh.slice],
+                    [sh.z_ghost],
+                    flops=sh.comps * WORK,
+                    name="sweep_outer",
+                )
+                ends[number] = chip_ends(sh, last)
+            corrections[number], *out = call(
+                bind(close_kernel, sh),
                 flags,
-                [coef, correction, scaled],
-                [sh.field],
-                flops=20_000_000,
-                name="sweep_inner",
+                [coef, partials[number]] + ends[number],
+                [sh.field] + sh.messages,
+                flops=sh.comps * WORK,
+                name="close",
             )
-            partial, last = call(
-                bind(sweep_outer_kernel, sh),
-                flags,
-                [coef, inner] + faces,
-                [sh.field, sh.slice],
-                [z_ghost],
-                name="sweep_outer",
-            )
-        ends = chip_ends(last)
-        correction, *out = call(
-            bind(close_kernel, sh),
-            flags,
-            [coef, partial] + ends,
-            [sh.field] + messages,
-            name="close",
-        )
-        faces = exchange(sh, out, n_time, places)
+            faces[number] = exchange(sh, out, n_time, places)
     native = (half, COMPONENTS, local, CHUNKS * LANES)
     whole = (slots,) + native[1:]
 
@@ -651,29 +668,33 @@
         start = ((1 - core) * half, 0, 0, 0)
         return lax.dynamic_update_slice(out, other, start).transpose(0, 2, 1, 3)
 
-    (inner,) = call(
-        bind(final_inner_kernel, sh),
+    ins = []
+    for number, sh in enumerate(shapes):
+        ins += call(
+            bind(final_inner_kernel, sh),
+            flags,
+            [coef, corrections[number], scaleds[number]] + ends[number],
+            [sh.field],
+            flops=sh.comps * WORK,
+            name="final_inner",
+        )
+        ins += faces[number]
+    out, send = call(
+        bind(velocity_kernel, shapes),
         flags,
-        [coef, correction, scaled] + ends,
-        [sh.field],
-        flops=20_000_000,
-        name="final_inner",
-    )
-    out, send = call(
-        bind(velocity_kernel, sh),
-        flags,
-        [velocity, velocity_other, correction],
+        [velocity, velocity_other] + corrections,
         [whole, native],
         [rows],
+        flops=WORK,
         name="velocity",
     )
     corrected_velocity = restore(out, send)
     out, send = call(
-        bind(final_outer_kernel, sh),
+        bind(final_outer_kernel, shapes),
         flags,
-        [coef, inner] + faces,
+        [coef] + ins,
         [whole, native],
-        [z_ghost, pltpu.VMEM(tile_shape(sh.span), F32), rows],
+        [pltpu.VMEM(tile_shape(half, sh.span), F32), rows] + [sh.z_ghost for sh in shapes],
         name="final_outer",
     )
     return corrected_velocity, restore(out, send)

time: 126 us -> 117 us (0.929)
  Pallas kernels: 50.7 us -> 40 us
  waiting for transfers between devices: 34.9 us -> 39.2 us
  starting transfers between devices: 33.9 us -> 31.4 us
    pallas_call x20, Pallas kernels: 50.7 us -> 40 us  [call(): pl.pallas_call(kernel, in_specs=[pl.BlockSpec(memory_space=pltpu.SMEM)] +...]
    ppermute x6, waiting for transfers between devices: 0.4 us -> 2.56 us  [exchange(): lax.ppermute(x_out[i], axes, pairs(bit, sh.bits[0], False))]
    ppermute x6, waiting for transfers between devices: 2.12 us -> 3.9 us  [exchange(): y_in = lax.ppermute(y_out, axes, pairs(sh.bits[1][0], sh.bits[1], False))]
    ppermute x6, starting transfers between devices: 5.33 us -> 3.76 us  [exchange(): y_in = lax.ppermute(y_out, axes, pairs(sh.bits[1][0], sh.bits[1], False))]
  transfers between devices with their start and end apart: 34 -> 34, of which waited for: 14 -> 15; matrix products, arithmetic and copies ran while one was open for 2% -> 2% of each run, Pallas kernels for 22% -> 19%
where the time goes in v3:
time: 117 us
  Pallas kernels  40 us (34%)
  waiting for transfers between devices  39.2 us (34%)
  starting transfers between devices  31.4 us (27%)
  local copies, waits for them, and re-layouts  4.5 us (4%)
    pallas_call x20, Pallas kernels, call(): pl.pallas_call(kernel, in_specs=[pl.BlockSpec(memory_space=pltpu.SMEM)] +...  40 us
    ppermute x5, waiting for transfers between devices, chip_ends(): lax.ppermute(last, 'tm', [(a, (a + 2 * back) % n_time) for a in range(n_t...  30.1 us
    ppermute x10, starting transfers between devices, swap_cores(): return lax.ppermute(value, 'tm', [(t, t ^ 1) for t in range(n_time)])  11.2 us
    ppermute x6, starting transfers between devices, exchange(): lax.ppermute(x_out[i], axes, pairs(bit, sh.bits[0], False))  6.26 us
    ppermute x1, starting transfers between devices, body(): lax.ppermute(last, 'tm', [(a, a + 2) for a in range(n_time - 2)])  4.76 us
    ppermute x6, starting transfers between devices, exchange(): z_in = lax.ppermute(z_out, axes, pairs(sh.bits[2][0], sh.bits[2], True))  3.94 us
    ppermute x6, waiting for transfers between devices, exchange(): y_in = lax.ppermute(y_out, axes, pairs(sh.bits[1][0], sh.bits[1], False))  3.9 us
    ppermute x6, starting transfers between devices, exchange(): y_in = lax.ppermute(y_out, axes, pairs(sh.bits[1][0], sh.bits[1], False))  3.76 us
  transfers between devices with their start and end apart: 34, of which 15 were waited for; matrix products, arithmetic and copies ran while one was open for 2% of the time, Pallas kernels for 19%

profile of v3, /device:TPU:0, one launch (start us, length us, event | category | flops | bytes accessed | tf_op | source)
XLA Modules:
  0.0 116.7 jit_solution(15623178560573130667)
XLA Ops:
  5.9 1.7 %gather.1 = (f32[4,3,8,2,16,128]{5,4,3,2,1,0:T(8,128)S(1)}, f32[4,3,2,16,128]{4,3,2,1,0:T(8,128)S(1)}, f32[6,16,128]{2,1,0:T(8,128)S(1)}, f32[6,16,128]{2,1,0:T(...) custom-call(s32[32]{0:T(128)S(1)} %concatenate.3.refs_0_, f32[8,3,4,4096]{3,2,1,0:T(4,128)S(1)} %bitcast.11, ...), custom_call_target="tpu_custom_call" | custom-call | flops 2000000 | bytes 1000000 | tf_op jit(solution)/shard_map/gather/pallas_call | solution.py:32
  7.6 4.8 %collective-permute-start.2 = (f32[4,3,2,16,128]{4,3,2,1,0:T(8,128)S(1)}, f32[4,3,2,16,128]{4,3,2,1,0:T(8,128)S(1)}, u32[]{:S(2)}, u32[]{:S(2)}) collective-permute-start(f32[4,3,2,16,128]{4,3,2,1,0:T(8,128)S(1)} %get-tuple-element.54), channel_id=1, source_target_pairs={{0,16},{8,24},{1,17},{9,25},{2,18},{10,26},{3,19},{11,27},{4,20},{... | collective-permute-start | bytes 589832 | tf_op jit(solution)/shard_map/ppermute | solution.py:598
  17.4 4.0 %residual_inner.1 = (f32[4,3,8,2,16,128]{5,4,3,2,1,0:T(8,128)S(1)}, f32[4,3,8,2,16,128]{5,4,3,2,1,0:T(8,128)}) custom-call(s32[32]{0:T(128)S(1)} %concatenate.3.refs_0_, f32[4,13,2,16,128]{4,3,2,1,0:T(8,128)S(1)} %get-tuple-element.51.refs_1_, f32[4,3,8,2,16,128]{5,4,3,2,1,0:T(8,128)S(1)} %get-tuple-element.52.refs_2_, f32[8,3,4,4096]{3,2,1,0:T(4,128)S(1)} %bitcast.14, ...), custom_call_target="tpu_custom_call" | custom-call | flops 18000000 | bytes 1000000 | tf_op jit(solution)/shard_map/residual_inner/pallas_call | solution.py:32
  21.4 1.8 %residual_outer.1 = (f32[4,3,8,2,16,128]{5,4,3,2,1,0:T(8,128)S(1)}, f32[4,3,8,2,16,128]{5,4,3,2,1,0:T(8,128)S(1)}, f32[4,3,2,16,128]{4,3,2,1,0:T(8,128)S(1)}) custom-call(s32[32]{0:T(128)S(1)} %concatenate.3.refs_0_, f32[4,13,2,16,128]{4,3,2,1,0:T(8,128)S(1)} %get-tuple-element.51.refs_1_, f32[4,3,8,2,16,128]{5,4,3,2,1,0:T(8,128)S(1)} %get-tuple-element.53.refs_2_, ...), custom_call_target="tpu_custom_call" | custom-call | flops 18000000 | bytes 1000000 | tf_op jit(solution)/shard_map/residual_outer/pallas_call | solution.py:32
  23.3 5.7 %collective-permute-done.7.refs_3_ = f32[4,3,2,16,128]{4,3,2,1,0:T(8,128)S(1)} collective-permute-done((f32[4,3,2,16,128]{4,3,2,1,0:T(8,128)S(1)}, f32[4,3,2,16,128]{4,3,2,1,0:T(8,128)S(1)}, u32[]{:S(2)}, u32[]{:S(2)}) %collective-permute-start.7) | collective-permute-done | bytes 196640 | tf_op jit(solution)/shard_map/ppermute | solution.py:604
  30.3 2.3 %collective-permute-start.10 = (f32[6,2,16,128]{3,2,1,0:T(8,128)S(1)}, f32[6,2,16,128]{3,2,1,0:T(8,128)S(1)}, u32[]{:S(2)}, u32[]{:S(2)}) collective-permute-start(f32[6,2,16,128]{3,2,1,0:T(8,128)S(1)} %get-tuple-element.66), channel_id=1, source_target_pairs={{0,8},{8,0},{16,24},{24,16},{1,9},{9,1},{17,25},{25,17},{2,10},{10... | collective-permute-start | bytes 294920 | tf_op jit(solution)/shard_map/ppermute | solution.py:103
  34.3 2.4 %sweep_inner.4.refs_2_ = f32[4,3,8,2,16,128]{5,4,3,2,1,0:T(8,128)S(1)} custom-call(s32[32]{0:T(128)S(1)} %concatenate.3.refs_0_, f32[4,13,2,16,128]{4,3,2,1,0:T(8,128)S(1)} %get-tuple-element.51.refs_1_, f32[4,3,8,2,16,128]{5,4,3,2,1,0:T(8,128)S(1)} %get-tuple-element.62.refs_2_, f32[4,3,8,2,16,128]{5,4,3,2,1,0:T(8,128)S(1)} %get-tuple-element.63.refs_3_), custom_call_target="tpu_custom_call" | custom-call | flops 18000000 | bytes 1000000 | tf_op jit(solution)/shard_map/sweep_inner/pallas_call | solution.py:32
  37.9 1.8 %sweep_outer.4 = (f32[4,3,8,2,16,128]{5,4,3,2,1,0:T(8,128)S(1)}, f32[4,3,2,16,128]{4,3,2,1,0:T(8,128)S(1)}) custom-call(s32[32]{0:T(128)S(1)} %concatenate.3.refs_0_, f32[4,13,2,16,128]{4,3,2,1,0:T(8,128)S(1)} %get-tuple-element.51.refs_1_, f32[4,3,8,2,16,128]{5,4,3,2,1,0:T(8,128)S(1)} %sweep_inner.4.refs_2_, ...), custom_call_target="tpu_custom_call" | custom-call | flops 18000000 | bytes 1000000 | tf_op jit(solution)/shard_map/sweep_outer/pallas_call | solution.py:32
  40.1 5.7 %collective-permute-done.12.refs_3_ = f32[4,3,2,16,128]{4,3,2,1,0:T(8,128)S(1)} collective-permute-done((f32[4,3,2,16,128]{4,3,2,1,0:T(8,128)S(1)}, f32[4,3,2,16,128]{4,3,2,1,0:T(8,128)S(1)}, u32[]{:S(2)}, u32[]{:S(2)}) %collective-permute-start.12) | collective-permute-done | bytes 196640 | tf_op jit(solution)/shard_map/ppermute | solution.py:604
  51.5 2.4 %sweep_inner.5.refs_2_ = f32[4,3,8,2,16,128]{5,4,3,2,1,0:T(8,128)S(1)} custom-call(s32[32]{0:T(128)S(1)} %concatenate.3.refs_0_, f32[4,13,2,16,128]{4,3,2,1,0:T(8,128)S(1)} %get-tuple-element.51.refs_1_, f32[4,3,8,2,16,128]{5,4,3,2,1,0:T(8,128)S(1)} %get-tuple-element.70.refs_2_, f32[4,3,8,2,16,128]{5,4,3,2,1,0:T(8,128)S(1)} %get-tuple-element.63.refs_3_), custom_call_target="tpu_custom_call" | custom-call | flops 18000000 | bytes 1000000 | tf_op jit(solution)/shard_map/sweep_inner/pallas_call | solution.py:32
  55.2 1.8 %sweep_outer.5 = (f32[4,3,8,2,16,128]{5,4,3,2,1,0:T(8,128)S(1)}, f32[4,3,2,16,128]{4,3,2,1,0:T(8,128)S(1)}) custom-call(s32[32]{0:T(128)S(1)} %concatenate.3.refs_0_, f32[4,13,2,16,128]{4,3,2,1,0:T(8,128)S(1)} %get-tuple-element.51.refs_1_, f32[4,3,8,2,16,128]{5,4,3,2,1,0:T(8,128)S(1)} %sweep_inner.5.refs_2_, ...), custom_call_target="tpu_custom_call" | custom-call | flops 18000000 | bytes 1000000 | tf_op jit(solution)/shard_map/sweep_outer/pallas_call | solution.py:32
  57.4 6.5 %collective-permute-done.17.refs_3_ = f32[4,3,2,16,128]{4,3,2,1,0:T(8,128)S(1)} collective-permute-done((f32[4,3,2,16,128]{4,3,2,1,0:T(8,128)S(1)}, f32[4,3,2,16,128]{4,3,2,1,0:T(8,128)S(1)}, u32[]{:S(2)}, u32[]{:S(2)}) %collective-permute-start.17) | collective-permute-done | bytes 196640 | tf_op jit(solution)/shard_map/ppermute | solution.py:604
  67.7 2.4 %sweep_inner.6.refs_2_ = f32[4,3,8,2,16,128]{5,4,3,2,1,0:T(8,128)S(1)} custom-call(s32[32]{0:T(128)S(1)} %concatenate.3.refs_0_, f32[4,13,2,16,128]{4,3,2,1,0:T(8,128)S(1)} %get-tuple-element.51.refs_1_, f32[4,3,8,2,16,128]{5,4,3,2,1,0:T(8,128)S(1)} %get-tuple-element.77.refs_2_, f32[4,3,8,2,16,128]{5,4,3,2,1,0:T(8,128)S(1)} %get-tuple-element.63.refs_3_), custom_call_target="tpu_custom_call" | custom-call | flops 18000000 | bytes 1000000 | tf_op jit(solution)/shard_map/sweep_inner/pallas_call | solution.py:32
  71.3 1.8 %sweep_outer.6 = (f32[4,3,8,2,16,128]{5,4,3,2,1,0:T(8,128)S(1)}, f32[4,3,2,16,128]{4,3,2,1,0:T(8,128)S(1)}) custom-call(s32[32]{0:T(128)S(1)} %concatenate.3.refs_0_, f32[4,13,2,16,128]{4,3,2,1,0:T(8,128)S(1)} %get-tuple-element.51.refs_1_, f32[4,3,8,2,16,128]{5,4,3,2,1,0:T(8,128)S(1)} %sweep_inner.6.refs_2_, ...), custom_call_target="tpu_custom_call" | custom-call | flops 18000000 | bytes 1000000 | tf_op jit(solution)/shard_map/sweep_outer/pallas_call | solution.py:32
  73.5 5.7 %collective-permute-done.22.refs_3_ = f32[4,3,2,16,128]{4,3,2,1,0:T(8,128)S(1)} collective-permute-done((f32[4,3,2,16,128]{4,3,2,1,0:T(8,128)S(1)}, f32[4,3,2,16,128]{4,3,2,1,0:T(8,128)S(1)}, u32[]{:S(2)}, u32[]{:S(2)}) %collective-permute-start.22) | collective-permute-done | bytes 196640 | tf_op jit(solution)/shard_map/ppermute | solution.py:604
  80.5 1.7 %collective-permute-start.25 = (f32[6,2,16,128]{3,2,1,0:T(8,128)S(1)}, f32[6,2,16,128]{3,2,1,0:T(8,128)S(1)}, u32[]{:S(2)}, u32[]{:S(2)}) collective-permute-start(f32[6,2,16,128]{3,2,1,0:T(8,128)S(1)} %get-tuple-element.87), channel_id=1, source_target_pairs={{0,8},{8,0},{16,24},{24,16},{1,9},{9,1},{17,25},{25,17},{2,10},{10... | collective-permute-start | bytes 294920 | tf_op jit(solution)/shard_map/ppermute | solution.py:103
  82.8 1.7 %collective-permute-start.23 = (f32[6,16,128]{2,1,0:T(8,128)S(1)}, f32[6,16,128]{2,1,0:T(8,128)S(1)}, u32[]{:S(2)}, u32[]{:S(2)}) collective-permute-start(f32[6,16,128]{2,1,0:T(8,128)S(1)} %get-tuple-element.85), channel_id=1, source_target_pairs={{0,1},{1,0},{2,3},{3,2},{4,5},{5,4},{6,7},{7,6},{8,9},{9,8},{10,11... | collective-permute-start | bytes 147464 | tf_op jit(solution)/shard_map/ppermute | solution.py:94
  85.0 2.4 %sweep_inner.7.refs_2_ = f32[4,3,8,2,16,128]{5,4,3,2,1,0:T(8,128)S(1)} custom-call(s32[32]{0:T(128)S(1)} %concatenate.3.refs_0_, f32[4,13,2,16,128]{4,3,2,1,0:T(8,128)S(1)} %get-tuple-element.51.refs_1_, f32[4,3,8,2,16,128]{5,4,3,2,1,0:T(8,128)S(1)} %get-tuple-element.84.refs_2_, f32[4,3,8,2,16,128]{5,4,3,2,1,0:T(8,128)S(1)} %get-tuple-element.63.refs_3_), custom_call_target="tpu_custom_call" | custom-call | flops 18000000 | bytes 1000000 | tf_op jit(solution)/shard_map/sweep_inner/pallas_call | solution.py:32
  88.8 1.8 %sweep_outer.7 = (f32[4,3,8,2,16,128]{5,4,3,2,1,0:T(8,128)S(1)}, f32[4,3,2,16,128]{4,3,2,1,0:T(8,128)S(1)}) custom-call(s32[32]{0:T(128)S(1)} %concatenate.3.refs_0_, f32[4,13,2,16,128]{4,3,2,1,0:T(8,128)S(1)} %get-tuple-element.51.refs_1_, f32[4,3,8,2,16,128]{5,4,3,2,1,0:T(8,128)S(1)} %sweep_inner.7.refs_2_, ...), custom_call_target="tpu_custom_call" | custom-call | flops 18000000 | bytes 1000000 | tf_op jit(solution)/shard_map/sweep_outer/pallas_call | solution.py:32
  91.0 6.6 %collective-permute-done.27.refs_3_.refs_4_ = f32[4,3,2,16,128]{4,3,2,1,0:T(8,128)S(1)} collective-permute-done((f32[4,3,2,16,128]{4,3,2,1,0:T(8,128)S(1)}, f32[4,3,2,16,128]{4,3,2,1,0:T(8,128)S(1)}, u32[]{:S(2)}, u32[]{:S(2)}) %collective-permute-start.27) | collective-permute-done | bytes 196640 | tf_op jit(solution)/shard_map/ppermute | solution.py:604
  99.0 2.4 %velocity.1 = (f32[8,3,4,4096]{3,2,1,0:T(4,128)}, f32[4,3,4,4096]{3,2,1,0:T(4,128)S(1)}) custom-call(s32[32]{0:T(128)S(1)} %concatenate.3.refs_0_, f32[8,3,4,4096]{3,2,1,0:T(4,128)S(1)} %bitcast.12, f32[8,3,4,4096]{3,2,1,0:T(4,128)S(1)} %collective-permute-done.refs_2_, f32[4,3,8,2,16,128]{5,4,3,2,1,0:T(8,128)S(1)} %get-tuple-element.91.refs_3_.refs_2_), custom_call_target="tpu_custom_call" | custom-call | flops 6000000 | bytes 1000000 | tf_op jit(solution)/shard_map/velocity/pallas_call | solution.py:32
  103.4 2.4 %final_inner.1.refs_2_ = f32[4,3,8,2,16,128]{5,4,3,2,1,0:T(8,128)S(1)} custom-call(s32[32]{0:T(128)S(1)} %concatenate.3.refs_0_, f32[4,13,2,16,128]{4,3,2,1,0:T(8,128)S(1)} %get-tuple-element.51.refs_1_, f32[4,3,8,2,16,128]{5,4,3,2,1,0:T(8,128)S(1)} %get-tuple-element.91.refs_3_.refs_2_, f32[4,3,8,2,16,128]{5,4,3,2,1,0:T(8,128)S(1)} %get-tuple-element.63.refs_3_, ...), custom_call_target="tpu_custom_call" | custom-call | flops 18000000 | bytes 1000000 | tf_op jit(solution)/shard_map/final_inner/pallas_call | solution.py:32
  107.1 3.2 %final_outer.1 = (f32[8,3,4,4096]{3,2,1,0:T(4,128)}, f32[4,3,4,4096]{3,2,1,0:T(4,128)S(1)}) custom-call(s32[32]{0:T(128)S(1)} %concatenate.3.refs_0_, f32[4,13,2,16,128]{4,3,2,1,0:T(8,128)S(1)} %get-tuple-element.51.refs_1_, f32[4,3,8,2,16,128]{5,4,3,2,1,0:T(8,128)S(1)} %final_inner.1.refs_2_, f32[6,16,128]{2,1,0:T(8,128)S(1)} %collective-permute-done.29.refs_3_, ...), custom_call_target="tpu_custom_call" | custom-call | flops 2000000 | bytes 1000000 | tf_op jit(solution)/shard_map/final_outer/pallas_call | solution.py:32
  110.2 3.3 %collective-permute-start.33 = (f32[4,3,4,4096]{3,2,1,0:T(4,128)S(1)}, f32[4,3,4,4096]{3,2,1,0:T(4,128)S(1)}, u32[]{:S(2)}, u32[]{:S(2)}) collective-permute-start(f32[4,3,4,4096]{3,2,1,0:T(4,128)S(1)} %get-tuple-element.99), channel_id=1, source_target_pairs={{0,8},{8,0},{16,24},{24,16},{1,9},{9,1},{17,25},{25,17},{2,10},{10... | collective-permute-start | bytes 2359304 | tf_op jit(solution)/shard_map/ppermute | solution.py:103
  (86 shorter events, 39.7 us)
Async XLA Ops:
  1.2 13.5 %collective-permute-start.1 = (f32[8,3,4,4096]{3,2,1,0:T(4,128)}, f32[8,3,4,4096]{3,2,1,0:T(4,128)S(1)}, u32[]{:S(2)}, u32[]{:S(2)}) collective-permute-start(f32[8,3,4,4096]{3,2,1,0:T(4,128)} %bitcast.13), channel_id=1, source_target_pairs={{0,8},{8,0},{16,24},{24,16},{1,9},{9,1},{17,25},{25,17},{2,10},{10... | collective-permute-start | bytes 4718600 | tf_op jit(solution)/shard_map/ppermute | solution.py:103
  7.6 13.8 %collective-permute-start.2 = (f32[4,3,2,16,128]{4,3,2,1,0:T(8,128)S(1)}, f32[4,3,2,16,128]{4,3,2,1,0:T(8,128)S(1)}, u32[]{:S(2)}, u32[]{:S(2)}) collective-permute-start(f32[4,3,2,16,128]{4,3,2,1,0:T(8,128)S(1)} %get-tuple-element.54), channel_id=1, source_target_pairs={{0,16},{8,24},{1,17},{9,25},{2,18},{10,26},{3,19},{11,27},{4,20},{... | collective-permute-start | bytes 589832 | tf_op jit(solution)/shard_map/ppermute | solution.py:598
  12.4 9.0 %collective-permute-start.5 = (f32[6,2,16,128]{3,2,1,0:T(8,128)S(1)}, f32[6,2,16,128]{3,2,1,0:T(8,128)S(1)}, u32[]{:S(2)}, u32[]{:S(2)}) collective-permute-start(f32[6,2,16,128]{3,2,1,0:T(8,128)S(1)} %get-tuple-element.58), channel_id=1, source_target_pairs={{0,8},{8,0},{16,24},{24,16},{1,9},{9,1},{17,25},{25,17},{2,10},{10... | collective-permute-start | bytes 294920 | tf_op jit(solution)/shard_map/ppermute | solution.py:103
  12.4 8.9 %collective-permute-start.6 = (f32[6,2,16,128]{3,2,1,0:T(8,128)S(1)}, f32[6,2,16,128]{3,2,1,0:T(8,128)S(1)}, u32[]{:S(2)}, u32[]{:S(2)}) collective-permute-start(f32[6,2,16,128]{3,2,1,0:T(8,128)S(1)} %get-tuple-element.59), channel_id=1, source_target_pairs={{4,8},{5,9},{6,10},{7,11},{8,4},{9,5},{10,6},{11,7},{20,24},{21,25... | collective-permute-start | bytes 294920 | tf_op jit(solution)/shard_map/ppermute | solution.py:92
  13.1 8.3 %collective-permute-start.3 = (f32[6,16,128]{2,1,0:T(8,128)S(1)}, f32[6,16,128]{2,1,0:T(8,128)S(1)}, u32[]{:S(2)}, u32[]{:S(2)}) collective-permute-start(f32[6,16,128]{2,1,0:T(8,128)S(1)} %get-tuple-element.56), channel_id=1, source_target_pairs={{0,1},{1,0},{2,3},{3,2},{4,5},{5,4},{6,7},{7,6},{8,9},{9,8},{10,11... | collective-permute-start | bytes 147464 | tf_op jit(solution)/shard_map/ppermute | solution.py:94
  14.7 6.7 %collective-permute-start.4 = (f32[6,16,128]{2,1,0:T(8,128)S(1)}, f32[6,16,128]{2,1,0:T(8,128)S(1)}, u32[]{:S(2)}, u32[]{:S(2)}) collective-permute-start(f32[6,16,128]{2,1,0:T(8,128)S(1)} %get-tuple-element.57), channel_id=1, source_target_pairs={{0,2},{1,3},{2,0},{3,1},{4,6},{5,7},{6,4},{7,5},{8,10},{9,11},{10,... | collective-permute-start | bytes 147464 | tf_op jit(solution)/shard_map/ppermute | solution.py:97
  23.2 5.7 %collective-permute-start.7 = (f32[4,3,2,16,128]{4,3,2,1,0:T(8,128)S(1)}, f32[4,3,2,16,128]{4,3,2,1,0:T(8,128)S(1)}, u32[]{:S(2)}, u32[]{:S(2)}) collective-permute-start(f32[4,3,2,16,128]{4,3,2,1,0:T(8,128)S(1)} %get-tuple-element.61.refs_4_), channel_id=1, source_target_pairs={{0,16},{8,24},{16,0},{24,8},{1,17},{9,25},{17,1},{25,9},{2,18},{10... | collective-permute-start | bytes 589832 | tf_op jit(solution)/shard_map/ppermute | solution.py:604
  30.3 7.6 %collective-permute-start.10 = (f32[6,2,16,128]{3,2,1,0:T(8,128)S(1)}, f32[6,2,16,128]{3,2,1,0:T(8,128)S(1)}, u32[]{:S(2)}, u32[]{:S(2)}) collective-permute-start(f32[6,2,16,128]{3,2,1,0:T(8,128)S(1)} %get-tuple-element.66), channel_id=1, source_target_pairs={{0,8},{8,0},{16,24},{24,16},{1,9},{9,1},{17,25},{25,17},{2,10},{10... | collective-permute-start | bytes 294920 | tf_op jit(solution)/shard_map/ppermute | solution.py:103
  32.6 5.3 %collective-permute-start.11 = (f32[6,2,16,128]{3,2,1,0:T(8,128)S(1)}, f32[6,2,16,128]{3,2,1,0:T(8,128)S(1)}, u32[]{:S(2)}, u32[]{:S(2)}) collective-permute-start(f32[6,2,16,128]{3,2,1,0:T(8,128)S(1)} %get-tuple-element.67), channel_id=1, source_target_pairs={{4,8},{5,9},{6,10},{7,11},{8,4},{9,5},{10,6},{11,7},{20,24},{21,25... | collective-permute-start | bytes 294920 | tf_op jit(solution)/shard_map/ppermute | solution.py:92
  39.7 6.0 %collective-permute-start.12 = (f32[4,3,2,16,128]{4,3,2,1,0:T(8,128)S(1)}, f32[4,3,2,16,128]{4,3,2,1,0:T(8,128)S(1)}, u32[]{:S(2)}, u32[]{:S(2)}) collective-permute-start(f32[4,3,2,16,128]{4,3,2,1,0:T(8,128)S(1)} %get-tuple-element.69.refs_4_), channel_id=1, source_target_pairs={{0,16},{8,24},{16,0},{24,8},{1,17},{9,25},{17,1},{25,9},{2,18},{10... | collective-permute-start | bytes 589832 | tf_op jit(solution)/shard_map/ppermute | solution.py:604
  47.1 8.1 %collective-permute-start.15 = (f32[6,2,16,128]{3,2,1,0:T(8,128)S(1)}, f32[6,2,16,128]{3,2,1,0:T(8,128)S(1)}, u32[]{:S(2)}, u32[]{:S(2)}) collective-permute-start(f32[6,2,16,128]{3,2,1,0:T(8,128)S(1)} %get-tuple-element.73), channel_id=1, source_target_pairs={{0,8},{8,0},{16,24},{24,16},{1,9},{9,1},{17,25},{25,17},{2,10},{10... | collective-permute-start | bytes 294920 | tf_op jit(solution)/shard_map/ppermute | solution.py:103
  48.8 6.4 %collective-permute-start.16 = (f32[6,2,16,128]{3,2,1,0:T(8,128)S(1)}, f32[6,2,16,128]{3,2,1,0:T(8,128)S(1)}, u32[]{:S(2)}, u32[]{:S(2)}) collective-permute-start(f32[6,2,16,128]{3,2,1,0:T(8,128)S(1)} %get-tuple-element.74), channel_id=1, source_target_pairs={{4,8},{5,9},{6,10},{7,11},{8,4},{9,5},{10,6},{11,7},{20,24},{21,25... | collective-permute-start | bytes 294920 | tf_op jit(solution)/shard_map/ppermute | solution.py:92
  57.0 6.9 %collective-permute-start.17 = (f32[4,3,2,16,128]{4,3,2,1,0:T(8,128)S(1)}, f32[4,3,2,16,128]{4,3,2,1,0:T(8,128)S(1)}, u32[]{:S(2)}, u32[]{:S(2)}) collective-permute-start(f32[4,3,2,16,128]{4,3,2,1,0:T(8,128)S(1)} %get-tuple-element.76.refs_4_), channel_id=1, source_target_pairs={{0,16},{8,24},{16,0},{24,8},{1,17},{9,25},{17,1},{25,9},{2,18},{10... | collective-permute-start | bytes 589832 | tf_op jit(solution)/shard_map/ppermute | solution.py:604
  65.3 6.1 %collective-permute-start.20 = (f32[6,2,16,128]{3,2,1,0:T(8,128)S(1)}, f32[6,2,16,128]{3,2,1,0:T(8,128)S(1)}, u32[]{:S(2)}, u32[]{:S(2)}) collective-permute-start(f32[6,2,16,128]{3,2,1,0:T(8,128)S(1)} %get-tuple-element.80), channel_id=1, source_target_pairs={{0,8},{8,0},{16,24},{24,16},{1,9},{9,1},{17,25},{25,17},{2,10},{10... | collective-permute-start | bytes 294920 | tf_op jit(solution)/shard_map/ppermute | solution.py:103
  66.1 5.3 %collective-permute-start.21 = (f32[6,2,16,128]{3,2,1,0:T(8,128)S(1)}, f32[6,2,16,128]{3,2,1,0:T(8,128)S(1)}, u32[]{:S(2)}, u32[]{:S(2)}) collective-permute-start(f32[6,2,16,128]{3,2,1,0:T(8,128)S(1)} %get-tuple-element.81), channel_id=1, source_target_pairs={{4,8},{5,9},{6,10},{7,11},{8,4},{9,5},{10,6},{11,7},{20,24},{21,25... | collective-permute-start | bytes 294920 | tf_op jit(solution)/shard_map/ppermute | solution.py:92
  73.1 6.0 %collective-permute-start.22 = (f32[4,3,2,16,128]{4,3,2,1,0:T(8,128)S(1)}, f32[4,3,2,16,128]{4,3,2,1,0:T(8,128)S(1)}, u32[]{:S(2)}, u32[]{:S(2)}) collective-permute-start(f32[4,3,2,16,128]{4,3,2,1,0:T(8,128)S(1)} %get-tuple-element.83.refs_4_), channel_id=1, source_target_pairs={{0,16},{8,24},{16,0},{24,8},{1,17},{9,25},{17,1},{25,9},{2,18},{10... | collective-permute-start | bytes 589832 | tf_op jit(solution)/shard_map/ppermute | solution.py:604
  80.5 8.3 %collective-permute-start.25 = (f32[6,2,16,128]{3,2,1,0:T(8,128)S(1)}, f32[6,2,16,128]{3,2,1,0:T(8,128)S(1)}, u32[]{:S(2)}, u32[]{:S(2)}) collective-permute-start(f32[6,2,16,128]{3,2,1,0:T(8,128)S(1)} %get-tuple-element.87), channel_id=1, source_target_pairs={{0,8},{8,0},{16,24},{24,16},{1,9},{9,1},{17,25},{25,17},{2,10},{10... | collective-permute-start | bytes 294920 | tf_op jit(solution)/shard_map/ppermute | solution.py:103
  82.2 6.6 %collective-permute-start.26 = (f32[6,2,16,128]{3,2,1,0:T(8,128)S(1)}, f32[6,2,16,128]{3,2,1,0:T(8,128)S(1)}, u32[]{:S(2)}, u32[]{:S(2)}) collective-permute-start(f32[6,2,16,128]{3,2,1,0:T(8,128)S(1)} %get-tuple-element.88), channel_id=1, source_target_pairs={{4,8},{5,9},{6,10},{7,11},{8,4},{9,5},{10,6},{11,7},{20,24},{21,25... | collective-permute-start | bytes 294920 | tf_op jit(solution)/shard_map/ppermute | solution.py:92
  82.8 4.5 %collective-permute-start.23 = (f32[6,16,128]{2,1,0:T(8,128)S(1)}, f32[6,16,128]{2,1,0:T(8,128)S(1)}, u32[]{:S(2)}, u32[]{:S(2)}) collective-permute-start(f32[6,16,128]{2,1,0:T(8,128)S(1)} %get-tuple-element.85), channel_id=1, source_target_pairs={{0,1},{1,0},{2,3},{3,2},{4,5},{5,4},{6,7},{7,6},{8,9},{9,8},{10,11... | collective-permute-start | bytes 147464 | tf_op jit(solution)/shard_map/ppermute | solution.py:94
  90.6 7.0 %collective-permute-start.27 = (f32[4,3,2,16,128]{4,3,2,1,0:T(8,128)S(1)}, f32[4,3,2,16,128]{4,3,2,1,0:T(8,128)S(1)}, u32[]{:S(2)}, u32[]{:S(2)}) collective-permute-start(f32[4,3,2,16,128]{4,3,2,1,0:T(8,128)S(1)} %get-tuple-element.90.refs_4_.refs_5_), channel_id=1, source_target_pairs={{0,16},{8,24},{16,0},{24,8},{1,17},{9,25},{17,1},{25,9},{2,18},{10... | collective-permute-start | bytes 589832 | tf_op jit(solution)/shard_map/ppermute | solution.py:604
  101.4 12.2 %collective-permute-start.28 = (f32[4,3,4,4096]{3,2,1,0:T(4,128)S(1)}, f32[4,3,4,4096]{3,2,1,0:T(4,128)S(1)}, u32[]{:S(2)}, u32[]{:S(2)}) collective-permute-start(f32[4,3,4,4096]{3,2,1,0:T(4,128)S(1)} %get-tuple-element.93), channel_id=1, source_target_pairs={{0,8},{8,0},{16,24},{24,16},{1,9},{9,1},{17,25},{25,17},{2,10},{10... | collective-permute-start | bytes 2359304 | tf_op jit(solution)/shard_map/ppermute | solution.py:103
  102.0 5.0 %collective-permute-start.31 = (f32[6,2,16,128]{3,2,1,0:T(8,128)S(1)}, f32[6,2,16,128]{3,2,1,0:T(8,128)S(1)}, u32[]{:S(2)}, u32[]{:S(2)}) collective-permute-start(f32[6,2,16,128]{3,2,1,0:T(8,128)S(1)} %get-tuple-element.96), channel_id=1, source_target_pairs={{0,8},{8,0},{16,24},{24,16},{1,9},{9,1},{17,25},{25,17},{2,10},{10... | collective-permute-start | bytes 294920 | tf_op jit(solution)/shard_map/ppermute | solution.py:103
  102.0 5.0 %collective-permute-start.32 = (f32[6,2,16,128]{3,2,1,0:T(8,128)S(1)}, f32[6,2,16,128]{3,2,1,0:T(8,128)S(1)}, u32[]{:S(2)}, u32[]{:S(2)}) collective-permute-start(f32[6,2,16,128]{3,2,1,0:T(8,128)S(1)} %get-tuple-element.97), channel_id=1, source_target_pairs={{4,8},{5,9},{6,10},{7,11},{8,4},{9,5},{10,6},{11,7},{20,24},{21,25... | collective-permute-start | bytes 294920 | tf_op jit(solution)/shard_map/ppermute | solution.py:92
  110.2 5.2 %collective-permute-start.33 = (f32[4,3,4,4096]{3,2,1,0:T(4,128)S(1)}, f32[4,3,4,4096]{3,2,1,0:T(4,128)S(1)}, u32[]{:S(2)}, u32[]{:S(2)}) collective-permute-start(f32[4,3,4,4096]{3,2,1,0:T(4,128)S(1)} %get-tuple-element.99), channel_id=1, source_target_pairs={{0,8},{8,0},{16,24},{24,16},{1,9},{9,1},{17,25},{25,17},{2,10},{10... | collective-permute-start | bytes 2359304 | tf_op jit(solution)/shard_map/ppermute | solution.py:103
  (18 other events, 97.1 us)

commit v4 on v3

v4 whole, which is shorter than its diff:
```python
import jax
import jax.numpy as jnp
from jax import lax
from jax.experimental import pallas as pl
from jax.experimental.pallas import tpu as pltpu
from jax.sharding import PartitionSpec as P


EDGE = 16
LANES = 128
CHUNKS = 32
COMPONENTS = 3
ALPHA_SCALE = 0.1
SWEEPS = 5
STREAMS = ((0, 3),)
WORK = 6_000_000
XP, XM, YP, YM, ZP, ZM, XG, YG, ZG, Q, INV, LIVE, K0 = range(13)
FACES = 6
F32 = jnp.float32


def iota(shape, axis):
    return lax.broadcasted_iota(jnp.int32, shape, axis)


def tile_shape(*lead):
    return lead + (2, EDGE, LANES)


def call(kernel, tables, ins, outs, scratch=(), flops=2_000_000, in_hbm=None):
    vmem = pl.BlockSpec(memory_space=pltpu.VMEM)
    tables = tables or []
    return pl.pallas_call(
        kernel,
        in_specs=[pl.BlockSpec(memory_space=pltpu.SMEM)] * len(tables) + [vmem] * len(ins),
        out_specs=[vmem if s != in_hbm else pl.BlockSpec(memory_space=pltpu.HBM) for s in outs],
        out_shape=[jax.ShapeDtypeStruct(s, F32) for s in outs],
        scratch_shapes=list(scratch),
        compiler_params=pltpu.CompilerParams(vmem_limit_bytes=24 * 1024 * 1024),
        cost_estimate=pl.CostEstimate(flops=flops, bytes_accessed=1_000_000, transcendentals=0),
    )(*tables, *ins)


class Shape:
    def __init__(self, slots, local, n_time, places, base, comps):
        self.base = base
        self.comps = comps
        self.slots = slots
        self.half = slots // 2
        self.local = local
        self.span = 2 * local
        self.chips = n_time // 2
        levels = places.bit_length() - 1
        self.bits = [[b for b in range(levels) if b % 3 == d] for d in range(3)]
        self.y_per = max(1, 8 // self.span)
        self.z_per = max(1, 16 // self.span)
        self.x_shape = (2 * comps, self.span * 2, LANES)
        self.y_shape = (-(-2 // self.y_per) * comps, EDGE, LANES)
        self.z_shape = tile_shape(-(-self.half // self.z_per) * comps)
        self.x_count = len(self.bits[0])
        self.field = tile_shape(self.half, comps, self.span)
        self.slice = tile_shape(self.half, comps)
        self.messages = [self.x_shape] * self.x_count + [self.y_shape, self.z_shape, self.z_shape]
        self.z_ghost = pltpu.VMEM((2,) + self.z_shape, F32)


    def core(self):
        return lax.axis_index("tm") & 1

    def upper(self):
        return self.core() ^ (position(lax.axis_index("space"), self.bits[2]) & 1)

    def chip(self):
        return lax.axis_index("tm") >> 1

    def side(self, d):
        return 1 - (position(lax.axis_index("space"), self.bits[d]) & 1)


def position(place, bits):
    if len(bits) == 1:
        return place >> bits[0] & 1
    low, high = place >> bits[0] & 1, place >> bits[1] & 1
    return 2 * high + (low ^ high)


def exchange(sh, messages, n_time, places):
    axes = ("tm", "space")
    x_out, y_out, inner_out, z_out = messages[:-3], messages[-3], messages[-2], messages[-1]

    def pairs(bit, bits, halved):
        table = []
        for t in range(n_time):
            for s in range(places):
                here, there = position(s, bits), position(s ^ (1 << bit), bits)
                if abs(here - there) != 1:
                    continue
                if halved and (min(here, there) % 2 == 0) != (t % 2 == 1):
                    continue
                table.append((t * places + s, t * places + (s ^ (1 << bit))))
        return table

    z_in = lax.ppermute(z_out, axes, pairs(sh.bits[2][0], sh.bits[2], True))
    x_in = []
    for i, bit in enumerate(sh.bits[0]):
        x_in.append(lax.ppermute(x_out[i], axes, pairs(bit, sh.bits[0], False)))
    y_in = lax.ppermute(y_out, axes, pairs(sh.bits[1][0], sh.bits[1], False))
    inner_in = swap_cores(inner_out, n_time)
    return x_in + [y_in, inner_in, z_in]


def swap_cores(value, n_time):
    return lax.ppermute(value, "tm", [(t, t ^ 1) for t in range(n_time)])


def over_components(sh, visit):
    if sh.comps == 1:
        visit(0)
        return

    def step(comp, _):
        visit(comp)
        return 0

    lax.fori_loop(0, sh.comps, step, 0)


def over_tiles(sh, visit):
    def all_slots(comp):
        for j in range(sh.half):
            visit(j, comp)

    over_components(sh, all_slots)


def pack_faces(sh, tile, src, outs):
    on_top = sh.upper()
    lane = iota((EDGE, LANES), 1)
    within, group_of_lane = lane % EDGE, lane // EDGE
    x_outs, y_out, inner_out, z_out = outs[:-3], outs[-3], outs[-2], outs[-1]
    side_y = sh.side(1)

    def pack(comp):
        for g in range(-(-sh.half // sh.z_per)):
            low = [jnp.zeros((EDGE, LANES), F32)] * 2
            high = [jnp.zeros((EDGE, LANES), F32)] * 2
            for j in range(g * sh.z_per, min(sh.half, (g + 1) * sh.z_per)):
                for l in range(sh.span):
                    index = (j % sh.z_per) * sh.span + l
                    for h in range(2):
                        value = tile(j, comp, l, h)
                        value = pltpu.roll(value, index, 1) if index else value
                        low[h] = jnp.where(within == index, value, low[h])
                        high[h] = jnp.where(within == (index + EDGE - 1) % EDGE, value, high[h])
            for h in range(2):
                inner_out[g * sh.comps + comp, h] = jnp.where(on_top == 1, low[h], high[h])
                z_out[g * sh.comps + comp, h] = jnp.where(on_top == 1, high[h], low[h])
        for number, x_out in enumerate(x_outs):
            side = sh.side(0) if number == 0 else 1 - sh.side(0)
            for jj in range(2):
                for l in range(sh.span):
                    for h in range(2):
                        upper = src[2 * jj + 1, comp, l, h, EDGE - 1 : EDGE, :]
                        lower = src[2 * jj, comp, l, h, 0:1, :]
                        row = slice(2 * l + h, 2 * l + h + 1)
                        x_out[jj * sh.comps + comp, row, :] = jnp.where(side == 1, upper, lower)
        for y in range(-(-2 // sh.y_per)):
            packed = jnp.zeros((EDGE, LANES), F32)
            for jj in range(y * sh.y_per, min(2, (y + 1) * sh.y_per)):
                for l in range(sh.span):
                    index = (jj % sh.y_per) * sh.span + l
                    layer = src[2 * side_y + jj, comp, l, side_y]
                    layer = pltpu.roll(layer, EDGE * index, 1) if index else layer
                    packed = jnp.where(group_of_lane == (index + 7 * side_y) % 8, layer, packed)
            packed = jnp.where(side_y == 1, pltpu.roll(packed, EDGE, 1), packed)
            y_out[y * sh.comps + comp] = packed

    over_components(sh, pack)


def inner_sum(coef, src, j, comp, l):
    lane = iota((EDGE, LANES), 1)
    row = iota((EDGE, LANES), 0)
    tiles = [src[j, comp, l, h] for h in range(2)]
    if j // 2 == 0:
        below, above = 0.0, src[j ^ 2, comp, l, 0]
    else:
        below, above = src[j ^ 2, comp, l, 1], 0.0
    y_next = [jnp.where(lane < EDGE, tiles[1], tiles[0]), jnp.where(lane < EDGE, above, tiles[1])]
    last = lane >= LANES - EDGE
    y_back = [jnp.where(last, below, tiles[0]), jnp.where(last, tiles[0], tiles[1])]
    result = []
    for h in range(2):
        v = tiles[h]
        if j % 2 == 0:
            before, after = 0.0, src[j ^ 1, comp, l, h, 0:1, :]
        else:
            before, after = src[j ^ 1, comp, l, h, EDGE - 1 : EDGE, :], 0.0
        total = coef[j, YP, h] * pltpu.roll(y_next[h], LANES - EDGE, 1)
        total += coef[j, YM, h] * pltpu.roll(y_back[h], EDGE, 1)
        total += coef[j, ZP, h] * pltpu.roll(v, LANES - 1, 1)
        total += coef[j, ZM, h] * pltpu.roll(v, 1, 1)
        total += coef[j, XP, h] * pltpu.roll(jnp.where(row == 0, after, v), EDGE - 1, 0)
        total += coef[j, XM, h] * pltpu.roll(jnp.where(row == EDGE - 1, before, v), 1, 0)
        result.append(total)
    return result


def ghost_sum(sh, coef, faces, z_ghost, total, j, comp, l):
    xs, y_in = faces[:-1], faces[-1]
    x_side, x_row = j % 2, j // 2
    y_side, y_row = j // 2, j % 2
    y_index = (y_row % sh.y_per) * sh.span + l
    z_index = (j % sh.z_per) * sh.span + l
    z_group = (j // sh.z_per) * sh.comps + comp
    outer = x_row * sh.comps + comp
    result = []
    for h in range(2):
        value = total[h]
        value += coef[j, ZG, h] * pltpu.roll(
            z_ghost[z_index % 2, z_group, h], LANES - EDGE + 1 - z_index, 1
        )
        if h == y_side:
            group = y_in[(y_row // sh.y_per) * sh.comps + comp]
            shift = ((LANES - EDGE if y_side else 0) - EDGE * y_index) % LANES
            value += coef[j, YG, h] * (pltpu.roll(group, shift, 1) if shift else group)
        row = slice(2 * l + h, 2 * l + h + 1)
        if len(xs) == 1:
            crossed = xs[0][outer, row, :]
        else:
            wanted = sh.side(0) if x_side == 1 else 1 - sh.side(0)
            crossed = jnp.where(wanted == 1, xs[0][outer, row, :], xs[1][outer, row, :])
        part = slice(8 * x_side, 8 * x_side + 8)
        changed = value[part] + coef[j, XG, h, part, :] * jnp.broadcast_to(crossed, (8, LANES))
        parts = [value[:8], changed] if x_side else [changed, value[8:]]
        result.append(jnp.concatenate(parts, axis=0))
    return result


def place_z_ghost(sh, inner_in, z_in, z_ghost):
    upper = sh.upper()
    odd = iota((EDGE, LANES), 1) % 2 == 1

    def step(g, _):
        for h in range(2):
            inner, outer = inner_in[g, h], z_in[g, h]
            above = pltpu.roll(jnp.where(upper == 1, outer, inner), 2 * EDGE - 2, 1)
            below = jnp.where(upper == 1, inner, outer)
            z_ghost[0, g, h] = jnp.where(odd, below, above)
            z_ghost[1, g, h] = jnp.where(odd, above, below)
        return 0

    lax.fori_loop(0, inner_in.shape[0], step, 0)


def rows_to_tiles(read, count, rows, write):
    for chunk in range(CHUNKS):
        rows[chunk * count : (chunk + 1) * count, :] = read(chunk)
    for i in range(count):
        for h in range(2):
            write(i, h, rows[pl.ds(h * count + i, EDGE, 2 * count), :])


def tiles_to_rows(tile, count, rows, write):
    for i in range(count):
        for h in range(2):
            rows[pl.ds(h * count + i, EDGE, 2 * count), :] = tile(i, h)
    for chunk in range(CHUNKS):
        write(chunk, rows[chunk * count : (chunk + 1) * count, :])


def present(holder, slot, face):
    return jnp.where(holder[slot, face] >= 0, 1.0, 0.0).astype(F32)


def coefficient_kernel(sh, holder, mask, viscosity, peclet, initial, coef, first, rows, tiles):
    chip = sh.chip()
    slots = sh.slots

    def unpack(source, kind):
        def write(i, h, value):
            tiles[kind, i, h] = value

        rows_to_tiles(lambda c: source(c), slots, rows, write)

    unpack(lambda c: viscosity[:, c * LANES : (c + 1) * LANES], 0)
    for d in range(3):
        unpack(lambda c, d=d: peclet[d, :, c * LANES : (c + 1) * LANES], 1 + d)
    for d in range(3):
        unpack(lambda c, d=d: initial[d, :, c * LANES : (c + 1) * LANES], 4 + d)

    lane = iota((EDGE, LANES), 1)
    row = iota((EDGE, LANES), 0)
    within = lane % EDGE
    zero = jnp.zeros((EDGE, LANES), F32)

    def step(j, _):
        slot = sh.upper() * sh.half + j
        hold = [present(holder, slot, face) for face in range(FACES)]
        live = mask[slot].astype(F32)
        for h in range(2):
            nu = tiles[0, slot, h]
            inverse = 2.0 + 6.0 * nu
            q = 2.0 / inverse
            scale = nu / inverse
            plus = [scale * (1.0 - tiles[1 + d, slot, h]) for d in range(3)]
            minus = [scale * (1.0 + tiles[1 + d, slot, h]) for d in range(3)]
            for d, (upper, lower) in enumerate(((XP, XM), (YP, YM), (ZP, ZM))):
                coef[j, upper, h] = plus[d]
                coef[j, lower, h] = minus[d]
            coef[j, XP, h] = jnp.where(row < EDGE - 1, plus[0], plus[0] * hold[1])
            coef[j, XM, h] = jnp.where(row > 0, minus[0], minus[0] * hold[0])
            if h == 0:
                coef[j, YM, h] = jnp.where(lane >= EDGE, minus[1], minus[1] * hold[2])
            else:
                coef[j, YP, h] = jnp.where(lane < LANES - EDGE, plus[1], plus[1] * hold[3])
            coef[j, ZP, h] = jnp.where(within < EDGE - 1, plus[2], zero)
            coef[j, ZM, h] = jnp.where(within > 0, minus[2], zero)
            coef[j, XG, h] = jnp.where(
                row == 0,
                minus[0] * hold[0],
                jnp.where(row == EDGE - 1, plus[0] * hold[1], zero),
            )
            if h == 0:
                coef[j, YG, h] = jnp.where(lane < EDGE, minus[1] * hold[2], zero)
            else:
                coef[j, YG, h] = jnp.where(lane >= LANES - EDGE, plus[1] * hold[3], zero)
            coef[j, ZG, h] = jnp.where(
                within == 0,
                minus[2] * hold[4],
                jnp.where(within == EDGE - 1, plus[2] * hold[5], zero),
            )
            coef[j, Q, h] = q
            coef[j, INV, h] = inverse * live
            coef[j, LIVE, h] = jnp.zeros_like(nu) + live
            power = q
            for _ in range(sh.span.bit_length() - 1):
                power = power * power
            whole = power
            for _ in range(sh.chips.bit_length() - 1):
                whole = whole * whole
            weight = 1.0 / (1.0 - ALPHA_SCALE * whole)
            for back in range(1, sh.chips + 1):
                wrapped = jnp.where(chip < back, ALPHA_SCALE, 1.0)
                coef[j, K0 + back - 1, h] = weight * wrapped
                weight = weight * power
            for d in range(COMPONENTS):
                first[j, d, h] = tiles[4 + d, slot, h]
        return 0

    lax.fori_loop(0, sh.half, step, 0)


def assemble(sh, whole, other, field, rows):
    core = sh.core()

    def visit(j, comp):
        slot = sh.upper() * sh.half + j
        for part, source in enumerate((whole, other)):
            first = (core if part == 0 else 1 - core) * sh.local

            def read(c, source=source):
                return source[slot, sh.base + comp, :, c * LANES : (c + 1) * LANES]

            def write(i, h, value, first=first):
                field[j, comp, first + i, h] = value

            rows_to_tiles(read, sh.local, rows.at[2 * j + part], write)

    over_tiles(sh, visit)


def gather_kernel(sh, whole, other, field, last, *rest):
    assemble(sh, whole, other, field, rest[-1])

    def visit(j, comp):
        last[j, comp] = field[j, comp, sh.span - 1]

    over_tiles(sh, visit)
    pack_faces(sh, lambda j, c, l, h: field[j, c, l, h], field, rest[:-1])


def residual_inner_kernel(sh, coef, field, whole, other, inner, force, rows):
    assemble(sh, whole, other, force, rows)

    def visit(j, comp):
        prior = None
        for l in range(sh.span):
            total = inner_sum(coef, field, j, comp, l)
            now = [field[j, comp, l, h] for h in range(2)]
            for h in range(2):
                q = coef[j, Q, h]
                value = total[h] + (0.5 * q) * force[j, comp, l, h] - now[h]
                inner[j, comp, l, h] = value if prior is None else value + q * prior[h]
            prior = now

    over_tiles(sh, visit)


def residual_outer_kernel(sh, coef, inner, before, first, *rest):
    faces = rest[: sh.x_count + 1]
    inner_in, z_in, scaled, partial, last, z_ghost = rest[sh.x_count + 1 :]
    place_z_ghost(sh, inner_in, z_in, z_ghost)
    chip = sh.chip()

    def visit(j, comp):
        carry = [jnp.zeros((EDGE, LANES), F32)] * 2
        for l in range(sh.span):
            total = [inner[j, comp, l, h] for h in range(2)]
            if l == 0:
                for h in range(2):
                    prior = jnp.where(chip == 0, first[j, sh.base + comp, h], before[j, comp, h])
                    total[h] = total[h] + coef[j, Q, h] * prior
            total = ghost_sum(sh, coef, faces, z_ghost, total, j, comp, l)
            for h in range(2):
                value = total[h] * coef[j, LIVE, h]
                scaled[j, comp, l, h] = value
                carry[h] = value + coef[j, Q, h] * carry[h]
                partial[j, comp, l, h] = carry[h]
        for h in range(2):
            last[j, comp, h] = carry[h]

    over_tiles(sh, visit)


def sweep_inner_kernel(sh, coef, field, scaled, inner):
    def visit(j, comp):
        for l in range(sh.span):
            total = inner_sum(coef, field, j, comp, l)
            for h in range(2):
                inner[j, comp, l, h] = scaled[j, comp, l, h] + total[h]

    over_tiles(sh, visit)


def sweep_outer_kernel(sh, coef, inner, *rest):
    faces = rest[: sh.x_count + 1]
    inner_in, z_in, partial, last, z_ghost = rest[sh.x_count + 1 :]
    place_z_ghost(sh, inner_in, z_in, z_ghost)

    def visit(j, comp):
        carry = [jnp.zeros((EDGE, LANES), F32)] * 2
        for l in range(sh.span):
            total = [inner[j, comp, l, h] for h in range(2)]
            total = ghost_sum(sh, coef, faces, z_ghost, total, j, comp, l)
            for h in range(2):
                carry[h] = total[h] + coef[j, Q, h] * carry[h]
                partial[j, comp, l, h] = carry[h]
        for h in range(2):
            last[j, comp, h] = carry[h]

    over_tiles(sh, visit)


def incoming_slice(sh, coef, lasts, j, comp, h):
    total = coef[j, K0, h] * lasts[0][j, comp, h]
    for back in range(1, sh.chips):
        total += coef[j, K0 + back, h] * lasts[back][j, comp, h]
    return total


def close_kernel(sh, coef, partial, *rest):
    lasts, (field, *messages) = rest[: sh.chips], rest[sh.chips :]
    term = {}

    def tile(j, comp, l, h):
        if l == 0:
            term[h] = incoming_slice(sh, coef, lasts, j, comp, h)
        term[h] = coef[j, Q, h] * term[h]
        value = partial[j, comp, l, h] + term[h]
        field[j, comp, l, h] = value
        return value

    pack_faces(sh, tile, field, messages)


def velocity_kernel(sh, whole, other, field, out, send, rows, kept, sem):
    core = sh.core()
    own, others = core * sh.local, (1 - core) * sh.local

    def visit(j, comp):
        slot = sh.upper() * sh.half + j

        def keep(c, value):
            at = slice(c * LANES, (c + 1) * LANES)
            kept[j, comp, :, at] = whole[slot, comp, :, at] + value

        def pass_on(c, value):
            at = slice(c * LANES, (c + 1) * LANES)
            send[j, comp, :, at] = other[slot, comp, :, at] + value

        tiles_to_rows(lambda i, h: field[j, comp, own + i, h], sh.local, rows.at[2 * j], keep)
        tiles_to_rows(
            lambda i, h: field[j, comp, others + i, h], sh.local, rows.at[2 * j + 1], pass_on
        )

    over_tiles(sh, visit)
    put_half(sh, sh.upper(), kept, out, sem)


def put_half(sh, which, source, out, sem):
    copy = pltpu.make_async_copy(source, out.at[pl.ds(which * sh.half, sh.half)], sem)
    copy.start()
    copy.wait()


def place_kernel(sh, half, partial, out, sem):
    put_half(sh, 1 - sh.upper(), half, out, sem)


def final_inner_kernel(sh, coef, field, scaled, *rest):
    lasts, (inner,) = rest[: sh.chips], rest[sh.chips :]
    chip = sh.chip()

    def visit(j, comp):
        prior = [
            jnp.where(chip == 0, 0.0, incoming_slice(sh, coef, lasts, j, comp, h))
            for h in range(2)
        ]
        for l in range(sh.span):
            total = inner_sum(coef, field, j, comp, l)
            for h in range(2):
                now = field[j, comp, l, h]
                value = scaled[j, comp, l, h] + total[h] - now
                inner[j, comp, l, h] = value + coef[j, Q, h] * prior[h]
                prior[h] = now

    over_tiles(sh, visit)


def final_outer_kernel(sh, mine, coef, inner, *rest):
    faces = rest[: sh.x_count + 1]
    inner_in, z_in, out, z_ghost, hold, rows, *kept = rest[sh.x_count + 1 :]
    target = kept[0] if mine else out
    place_z_ghost(sh, inner_in, z_in, z_ghost)
    core = sh.core()

    for number in range(2):

        def visit(j, comp, number=number):
            for i in range(sh.local):
                l = number * sh.local + i
                total = [inner[j, comp, l, h] for h in range(2)]
                total = ghost_sum(sh, coef, faces, z_ghost, total, j, comp, l)
                for h in range(2):
                    hold[j, i, h] = total[h] * coef[j, INV, h]

            def write(c, value):
                target[j, comp, :, c * LANES : (c + 1) * LANES] = value

            tiles_to_rows(lambda i, h: hold[j, i, h], sh.local, rows.at[j], write)

        @pl.when(core == (number if mine else 1 - number))
        def _(visit=visit):
            over_tiles(sh, visit)

    if mine:
        put_half(sh, sh.upper(), kept[0], out, kept[1])


def bind(kernel, sh, *fixed):
    def run(*refs):
        kernel(sh, *fixed, *refs)

    return run


def body(
    iterate,
    forcing,
    initial_velocity,
    viscosity,
    peclet,
    live_patch_mask,
    neighbour_holder,
    neighbour_slot,
):
    n_time, places = lax.axis_size("tm"), lax.axis_size("space")
    slots, local = iterate.shape[:2]
    shapes = [Shape(slots, local, n_time, places, base, comps) for base, comps in STREAMS]
    sh = shapes[0]
    half = sh.half
    velocity = iterate.transpose(0, 2, 1, 3)
    force = forcing.transpose(0, 2, 1, 3)

    velocity_other = swap_cores(velocity, n_time)
    force_other = swap_cores(force, n_time)

    rows = pltpu.VMEM((2 * half, CHUNKS * local, LANES), F32)

    coef, first = call(
        bind(coefficient_kernel, sh),
        [neighbour_holder, live_patch_mask],
        [viscosity, peclet.transpose(1, 0, 2), initial_velocity.transpose(1, 0, 2)],
        [tile_shape(half, K0 + sh.chips), tile_shape(half, COMPONENTS)],
        [pltpu.VMEM((CHUNKS * slots, LANES), F32), pltpu.VMEM(tile_shape(7, slots), F32)],
    )
    fields, faces, befores = [], [], []
    for sh in shapes:
        field, last, *out = call(
            bind(gather_kernel, sh),
            None,
            [velocity, velocity_other],
            [sh.field, sh.slice] + sh.messages,
            [rows],
        )
        befores.append(lax.ppermute(last, "tm", [(a, a + 2) for a in range(n_time - 2)]))
        faces.append(exchange(sh, out, n_time, places))
        fields.append(field)

    def chip_ends(sh, last):
        return [
            lax.ppermute(last, "tm", [(a, (a + 2 * back) % n_time) for a in range(n_time)])
            for back in range(1, sh.chips)
        ] + [last]

    scaleds, partials, ends = [], [], []
    for sh, field, before, face in zip(shapes, fields, befores, faces):
        inner, _ = call(
            bind(residual_inner_kernel, sh),
            None,
            [coef, field, force, force_other],
            [sh.field, sh.field],
            [rows],
            flops=sh.comps * WORK,
        )
        scaled, partial, last = call(
            bind(residual_outer_kernel, sh),
            None,
            [coef, inner, before, first] + face,
            [sh.field, sh.field, sh.slice],
            [sh.z_ghost],
            flops=sh.comps * WORK,
        )
        scaleds.append(scaled)
        partials.append(partial)
        ends.append(chip_ends(sh, last))

    corrections = [None] * len(shapes)
    for sweep in range(SWEEPS):
        for number, sh in enumerate(shapes):
            if sweep > 0:
                (inner,) = call(
                    bind(sweep_inner_kernel, sh),
                    None,
                    [coef, corrections[number], scaleds[number]],
                    [sh.field],
                    flops=sh.comps * WORK,
                )
                partials[number], last = call(
                    bind(sweep_outer_kernel, sh),
                    None,
                    [coef, inner] + faces[number],
                    [sh.field, sh.slice],
                    [sh.z_ghost],
                    flops=sh.comps * WORK,
                )
                ends[number] = chip_ends(sh, last)
            corrections[number], *out = call(
                bind(close_kernel, sh),
                None,
                [coef, partials[number]] + ends[number],
                [sh.field] + sh.messages,
                flops=sh.comps * WORK,
            )
            faces[number] = exchange(sh, out, n_time, places)
    native = (half, COMPONENTS, local, CHUNKS * LANES)
    whole = (slots,) + native[1:]

    def place(out, other):
        placed = pl.pallas_call(
            bind(place_kernel, sh),
            in_specs=[
                pl.BlockSpec(memory_space=pltpu.VMEM),
                pl.BlockSpec(memory_space=pltpu.HBM),
            ],
            out_specs=pl.BlockSpec(memory_space=pltpu.HBM),
            out_shape=jax.ShapeDtypeStruct(whole, F32),
            scratch_shapes=[pltpu.SemaphoreType.DMA(())],
            input_output_aliases={1: 0},
            name="place",
        )(other, out)
        return placed.transpose(0, 2, 1, 3)

    sh = shapes[0]
    (inner,) = call(
        bind(final_inner_kernel, sh),
        None,
        [coef, corrections[0], scaleds[0]] + ends[0],
        [sh.field],
        flops=sh.comps * WORK,
    )
    held_back, inner = lax.optimization_barrier((corrections[0], inner))
    (send,) = call(
        bind(final_outer_kernel, sh, False),
        None,
        [coef, inner] + faces[0],
        [native],
        [sh.z_ghost, pltpu.VMEM(tile_shape(half, local), F32), rows],
        flops=WORK,
    )
    residual_other = swap_cores(send, n_time)
    copied = [pltpu.VMEM(native, F32), pltpu.SemaphoreType.DMA(())]
    (residual_out,) = call(
        bind(final_outer_kernel, sh, True),
        None,
        [coef, inner] + faces[0],
        [whole],
        [sh.z_ghost, pltpu.VMEM(tile_shape(half, local), F32), rows] + copied,
        flops=WORK,
        in_hbm=whole,
    )
    out, send = call(
        bind(velocity_kernel, sh),
        None,
        [velocity, velocity_other, held_back],
        [whole, native],
        [rows] + copied,
        flops=WORK,
        in_hbm=whole,
    )
    corrected_velocity = place(out, swap_cores(send, n_time))
    return corrected_velocity, place(residual_out, residual_other)


def solution(mesh):
    return jax.shard_map(
        body,
        mesh=mesh,
        in_specs=(
            P("space", "tm", None, None),
            P("space", "tm", None, None),
            P("space", None, None),
            P("space", None),
            P("space", None, None),
            P("space"),
            P("space", None),
            P("space", None),
        ),
        out_specs=(P("space", "tm", None, None), P("space", "tm", None, None)),
        check_vma=False,
    )
```

time: 117 us -> 112 us (0.957)
  Pallas kernels: 40 us -> 33.9 us
  waiting for transfers between devices: 39.2 us -> 41.4 us
  local copies, waits for them, and re-layouts: 4.5 us -> 3.24 us
    pallas_call x20 -> x23, Pallas kernels: 40 us -> 33.9 us  [the longest x21 29.8 us: call(): pl.pallas_call(kernel, in_specs=[pl.BlockSpec(memory_space=pltpu.SMEM)] *...]
    unnamed x16 -> x20, local copies, waits for them, and re-layouts: 2.57 us -> 3.24 us
  transfers between devices with their start and end apart: 34 -> 34, of which waited for: 15 -> 14; matrix products, arithmetic and copies ran while one was open for 2% -> 0% of each run, Pallas kernels for 19% -> 19%
where the time goes in v4:
time: 112 us; the launch traced here: 111 us
  waiting for transfers between devices  41.4 us (37%)
  Pallas kernels  33.9 us (30%)
  starting transfers between devices  31.6 us (28%)
  local copies, waits for them, and re-layouts  3.24 us (3%)
    ppermute x5, waiting for transfers between devices, chip_ends(): lax.ppermute(last, 'tm', [(a, (a + 2 * back) % n_time) for a in range(n_t...  30.1 us
    pallas_call x21, Pallas kernels, call(): pl.pallas_call(kernel, in_specs=[pl.BlockSpec(memory_space=pltpu.SMEM)] *...  29.8 us
    ppermute x10, starting transfers between devices, swap_cores(): return lax.ppermute(value, 'tm', [(t, t ^ 1) for t in range(n_time)])  10.5 us
    ppermute x6, starting transfers between devices, exchange(): x_in.append(lax.ppermute(x_out[i], axes, pairs(bit, sh.bits[0], False)))  7.06 us
    ppermute x6, waiting for transfers between devices, exchange(): y_in = lax.ppermute(y_out, axes, pairs(sh.bits[1][0], sh.bits[1], False))  4.98 us
    ppermute x1, starting transfers between devices, body(): lax.ppermute(last, 'tm', [(a, a + 2) for a in range(n_time - 2)])  4.76 us
    pallas_call x2, Pallas kernels, place(): pl.pallas_call(bind(place_kernel, sh), in_specs=[pl.BlockSpec(memory_spac...  4.04 us
    ppermute x6, starting transfers between devices, exchange(): z_in = lax.ppermute(z_out, axes, pairs(sh.bits[2][0], sh.bits[2], True))  3.95 us
  transfers between devices with their start and end apart: 34, of which 14 were waited for; matrix products, arithmetic and copies ran while one was open for 0% of the time, Pallas kernels for 19%

profile of v4, /device:TPU:0, one launch (start us, length us, event | category | flops | bytes accessed | tf_op | source)
XLA Modules:
  0.0 111.2 jit_solution(6022016666452126246)
XLA Ops:
  1.3 3.2 %collective-permute-done.refs_1_ = f32[8,3,4,4096]{3,2,1,0:T(4,128)S(1)} collective-permute-done((f32[8,3,4,4096]{3,2,1,0:T(4,128)}, f32[8,3,4,4096]{3,2,1,0:T(4,128)S(1)}, u32[]{:S(2)}, u32[]{:S(2)}) %collective-permute-start) | collective-permute-done | bytes 1572896 | tf_op jit(solution)/shard_map/ppermute | solution.py:113
  7.1 4.8 %collective-permute-start.2 = (f32[4,3,2,16,128]{4,3,2,1,0:T(8,128)S(1)}, f32[4,3,2,16,128]{4,3,2,1,0:T(8,128)S(1)}, u32[]{:S(2)}, u32[]{:S(2)}) collective-permute-start(f32[4,3,2,16,128]{4,3,2,1,0:T(8,128)S(1)} %get-tuple-element.54), channel_id=1, source_target_pairs={{0,16},{8,24},{1,17},{9,25},{2,18},{10,26},{3,19},{11,27},{4,20},{... | collective-permute-start | bytes 589832 | tf_op jit(solution)/shard_map/ppermute | solution.py:607
  12.6 1.6 %collective-permute-start.3 = (f32[6,16,128]{2,1,0:T(8,128)S(1)}, f32[6,16,128]{2,1,0:T(8,128)S(1)}, u32[]{:S(2)}, u32[]{:S(2)}) collective-permute-start(f32[6,16,128]{2,1,0:T(8,128)S(1)} %get-tuple-element.56), channel_id=1, source_target_pairs={{0,1},{1,0},{2,3},{3,2},{4,5},{5,4},{6,7},{7,6},{8,9},{9,8},{10,11... | collective-permute-start | bytes 147464 | tf_op jit(solution)/shard_map/ppermute | solution.py:106
  14.2 1.6 %collective-permute-start.4 = (f32[6,16,128]{2,1,0:T(8,128)S(1)}, f32[6,16,128]{2,1,0:T(8,128)S(1)}, u32[]{:S(2)}, u32[]{:S(2)}) collective-permute-start(f32[6,16,128]{2,1,0:T(8,128)S(1)} %get-tuple-element.57), channel_id=1, source_target_pairs={{0,2},{1,3},{2,0},{3,1},{4,6},{5,7},{6,4},{7,5},{8,10},{9,11},{10,... | collective-permute-start | bytes 147464 | tf_op jit(solution)/shard_map/ppermute | solution.py:107
  16.9 3.5 %shard_map.88 = (f32[4,3,8,2,16,128]{5,4,3,2,1,0:T(8,128)S(1)}, f32[4,3,8,2,16,128]{5,4,3,2,1,0:T(8,128)}) custom-call(f32[4,14,2,16,128]{4,3,2,1,0:T(8,128)S(1)} %get-tuple-element.51.refs_0_, f32[4,3,8,2,16,128]{5,4,3,2,1,0:T(8,128)S(1)} %get-tuple-element.52.refs_1_, f32[8,3,4,4096]{3,2,1,0:T(4,128)S(1)} %bitcast.10, ...), custom_call_target="tpu_custom_call" | custom-call | flops 18000000 | bytes 1000000 | tf_op jit(solution)/shard_map/pallas_call | solution.py:33
  21.8 5.7 %collective-permute-done.7.refs_2_ = f32[4,3,2,16,128]{4,3,2,1,0:T(8,128)S(1)} collective-permute-done((f32[4,3,2,16,128]{4,3,2,1,0:T(8,128)S(1)}, f32[4,3,2,16,128]{4,3,2,1,0:T(8,128)S(1)}, u32[]{:S(2)}, u32[]{:S(2)}) %collective-permute-start.7) | collective-permute-done | bytes 196640 | tf_op jit(solution)/shard_map/ppermute | solution.py:613
  28.2 2.4 %collective-permute-start.10 = (f32[6,2,16,128]{3,2,1,0:T(8,128)S(1)}, f32[6,2,16,128]{3,2,1,0:T(8,128)S(1)}, u32[]{:S(2)}, u32[]{:S(2)}) collective-permute-start(f32[6,2,16,128]{3,2,1,0:T(8,128)S(1)} %get-tuple-element.66), channel_id=1, source_target_pairs={{0,8},{8,0},{16,24},{24,16},{1,9},{9,1},{17,25},{25,17},{2,10},{10... | collective-permute-start | bytes 294920 | tf_op jit(solution)/shard_map/ppermute | solution.py:113
  32.3 1.8 %shard_map.91.refs_1_ = f32[4,3,8,2,16,128]{5,4,3,2,1,0:T(8,128)S(1)} custom-call(f32[4,14,2,16,128]{4,3,2,1,0:T(8,128)S(1)} %get-tuple-element.51.refs_0_, f32[4,3,8,2,16,128]{5,4,3,2,1,0:T(8,128)S(1)} %get-tuple-element.62.refs_1_, f32[4,3,8,2,16,128]{5,4,3,2,1,0:T(8,128)S(1)} %get-tuple-element.63.refs_2_), custom_call_target="tpu_custom_call" | custom-call | flops 18000000 | bytes 1000000 | tf_op jit(solution)/shard_map/pallas_call | solution.py:33
  37.5 6.0 %collective-permute-done.12.refs_2_ = f32[4,3,2,16,128]{4,3,2,1,0:T(8,128)S(1)} collective-permute-done((f32[4,3,2,16,128]{4,3,2,1,0:T(8,128)S(1)}, f32[4,3,2,16,128]{4,3,2,1,0:T(8,128)S(1)}, u32[]{:S(2)}, u32[]{:S(2)}) %collective-permute-start.12) | collective-permute-done | bytes 196640 | tf_op jit(solution)/shard_map/ppermute | solution.py:613
  46.4 1.6 %collective-permute-start.13 = (f32[6,16,128]{2,1,0:T(8,128)S(1)}, f32[6,16,128]{2,1,0:T(8,128)S(1)}, u32[]{:S(2)}, u32[]{:S(2)}) collective-permute-start(f32[6,16,128]{2,1,0:T(8,128)S(1)} %get-tuple-element.71), channel_id=1, source_target_pairs={{0,1},{1,0},{2,3},{3,2},{4,5},{5,4},{6,7},{7,6},{8,9},{9,8},{10,11... | collective-permute-start | bytes 147464 | tf_op jit(solution)/shard_map/ppermute | solution.py:106
  48.4 1.8 %shard_map.94.refs_1_ = f32[4,3,8,2,16,128]{5,4,3,2,1,0:T(8,128)S(1)} custom-call(f32[4,14,2,16,128]{4,3,2,1,0:T(8,128)S(1)} %get-tuple-element.51.refs_0_, f32[4,3,8,2,16,128]{5,4,3,2,1,0:T(8,128)S(1)} %get-tuple-element.70.refs_1_, f32[4,3,8,2,16,128]{5,4,3,2,1,0:T(8,128)S(1)} %get-tuple-element.63.refs_2_), custom_call_target="tpu_custom_call" | custom-call | flops 18000000 | bytes 1000000 | tf_op jit(solution)/shard_map/pallas_call | solution.py:33
  50.5 1.6 %collective-permute-done.14.refs_3_ = f32[6,16,128]{2,1,0:T(8,128)S(1)} collective-permute-done((f32[6,16,128]{2,1,0:T(8,128)S(1)}, f32[6,16,128]{2,1,0:T(8,128)S(1)}, u32[]{:S(2)}, u32[]{:S(2)}) %collective-permute-start.14) | collective-permute-done | bytes 49184 | tf_op jit(solution)/shard_map/ppermute | solution.py:107
  54.3 6.0 %collective-permute-done.17.refs_2_ = f32[4,3,2,16,128]{4,3,2,1,0:T(8,128)S(1)} collective-permute-done((f32[4,3,2,16,128]{4,3,2,1,0:T(8,128)S(1)}, f32[4,3,2,16,128]{4,3,2,1,0:T(8,128)S(1)}, u32[]{:S(2)}, u32[]{:S(2)}) %collective-permute-start.17) | collective-permute-done | bytes 196640 | tf_op jit(solution)/shard_map/ppermute | solution.py:613
  63.5 1.8 %shard_map.97.refs_1_ = f32[4,3,8,2,16,128]{5,4,3,2,1,0:T(8,128)S(1)} custom-call(f32[4,14,2,16,128]{4,3,2,1,0:T(8,128)S(1)} %get-tuple-element.51.refs_0_, f32[4,3,8,2,16,128]{5,4,3,2,1,0:T(8,128)S(1)} %get-tuple-element.77.refs_1_, f32[4,3,8,2,16,128]{5,4,3,2,1,0:T(8,128)S(1)} %get-tuple-element.63.refs_2_), custom_call_target="tpu_custom_call" | custom-call | flops 18000000 | bytes 1000000 | tf_op jit(solution)/shard_map/pallas_call | solution.py:33
  69.0 5.6 %collective-permute-done.22.refs_2_ = f32[4,3,2,16,128]{4,3,2,1,0:T(8,128)S(1)} collective-permute-done((f32[4,3,2,16,128]{4,3,2,1,0:T(8,128)S(1)}, f32[4,3,2,16,128]{4,3,2,1,0:T(8,128)S(1)}, u32[]{:S(2)}, u32[]{:S(2)}) %collective-permute-start.22) | collective-permute-done | bytes 196640 | tf_op jit(solution)/shard_map/ppermute | solution.py:613
  77.6 2.7 %collective-permute-start.23 = (f32[6,16,128]{2,1,0:T(8,128)S(1)}, f32[6,16,128]{2,1,0:T(8,128)S(1)}, u32[]{:S(2)}, u32[]{:S(2)}) collective-permute-start(f32[6,16,128]{2,1,0:T(8,128)S(1)} %get-tuple-element.85), channel_id=1, source_target_pairs={{0,1},{1,0},{2,3},{3,2},{4,5},{5,4},{6,7},{7,6},{8,9},{9,8},{10,11... | collective-permute-start | bytes 147464 | tf_op jit(solution)/shard_map/ppermute | solution.py:106
  80.4 1.8 %shard_map.100.refs_1_ = f32[4,3,8,2,16,128]{5,4,3,2,1,0:T(8,128)S(1)} custom-call(f32[4,14,2,16,128]{4,3,2,1,0:T(8,128)S(1)} %get-tuple-element.51.refs_0_, f32[4,3,8,2,16,128]{5,4,3,2,1,0:T(8,128)S(1)} %get-tuple-element.84.refs_1_, f32[4,3,8,2,16,128]{5,4,3,2,1,0:T(8,128)S(1)} %get-tuple-element.63.refs_2_), custom_call_target="tpu_custom_call" | custom-call | flops 18000000 | bytes 1000000 | tf_op jit(solution)/shard_map/pallas_call | solution.py:33
  82.4 2.4 %collective-permute-done.24.refs_3_ = f32[6,16,128]{2,1,0:T(8,128)S(1)} collective-permute-done((f32[6,16,128]{2,1,0:T(8,128)S(1)}, f32[6,16,128]{2,1,0:T(8,128)S(1)}, u32[]{:S(2)}, u32[]{:S(2)}) %collective-permute-start.24) | collective-permute-done | bytes 49184 | tf_op jit(solution)/shard_map/ppermute | solution.py:107
  86.8 6.7 %collective-permute-done.27.refs_2_.refs_3_ = f32[4,3,2,16,128]{4,3,2,1,0:T(8,128)S(1)} collective-permute-done((f32[4,3,2,16,128]{4,3,2,1,0:T(8,128)S(1)}, f32[4,3,2,16,128]{4,3,2,1,0:T(8,128)S(1)}, u32[]{:S(2)}, u32[]{:S(2)}) %collective-permute-start.27) | collective-permute-done | bytes 196640 | tf_op jit(solution)/shard_map/ppermute | solution.py:613
  95.3 1.9 %shard_map.103.refs_1_ = f32[4,3,8,2,16,128]{5,4,3,2,1,0:T(8,128)S(1)} custom-call(f32[4,14,2,16,128]{4,3,2,1,0:T(8,128)S(1)} %get-tuple-element.51.refs_0_, f32[4,3,8,2,16,128]{5,4,3,2,1,0:T(8,128)S(1)} %get-tuple-element.92.refs_1_.refs_2_, f32[4,3,8,2,16,128]{5,4,3,2,1,0:T(8,128)S(1)} %get-tuple-element.63.refs_2_, ...), custom_call_target="tpu_custom_call" | custom-call | flops 18000000 | bytes 1000000 | tf_op jit(solution)/shard_map/pallas_call | solution.py:33
  98.7 3.5 %collective-permute-start.28 = (f32[4,3,4,4096]{3,2,1,0:T(4,128)S(1)}, f32[4,3,4,4096]{3,2,1,0:T(4,128)S(1)}, u32[]{:S(2)}, u32[]{:S(2)}) collective-permute-start(f32[4,3,4,4096]{3,2,1,0:T(4,128)S(1)} %get-tuple-element.93), channel_id=1, source_target_pairs={{0,8},{8,0},{16,24},{24,16},{1,9},{9,1},{17,25},{25,17},{2,10},{10... | collective-permute-start | bytes 2359304 | tf_op jit(solution)/shard_map/ppermute | solution.py:113
  103.4 1.9 %shard_map.106.refs_1_ = f32[8,3,4,4096]{3,2,1,0:T(4,128)} custom-call(f32[4,14,2,16,128]{4,3,2,1,0:T(8,128)S(1)} %get-tuple-element.51.refs_0_, f32[4,3,8,2,16,128]{5,4,3,2,1,0:T(8,128)S(1)} %shard_map.103.refs_1_, f32[6,16,128]{2,1,0:T(8,128)S(1)} %collective-permute-done.29.refs_2_, f32[6,16,128]{2,1,0:T(8,128)S(1)} %collective-permute-done.30.refs_3_, ...), custom_call_target="tpu_custom_call" | custom-call | flops 6000000 | bytes 1000000 | tf_op jit(solution)/shard_map/pallas_call | solution.py:33
  106.2 2.0 %place.2 = f32[8,3,4,4096]{3,2,1,0:T(4,128)} custom-call(f32[4,3,4,4096]{3,2,1,0:T(4,128)} %copy-done.8, f32[8,3,4,4096]{3,2,1,0:T(4,128)} %get-tuple-element.94.refs_1_), custom_call_target="tpu_custom_call", output_to_operand_aliasing={{}: (1, {})} | custom-call | tf_op jit(solution)/shard_map/place/pallas_call | solution.py:671
  109.1 2.0 %place.3 = f32[8,3,4,4096]{3,2,1,0:T(4,128)} custom-call(f32[4,3,4,4096]{3,2,1,0:T(4,128)} %copy-done.9, f32[8,3,4,4096]{3,2,1,0:T(4,128)} %shard_map.106.refs_1_), custom_call_target="tpu_custom_call", output_to_operand_aliasing={{}: (1, {})} | custom-call | tf_op jit(solution)/shard_map/place/pallas_call | solution.py:671
  (87 shorter events, 36.1 us)
Async XLA Ops:
  1.2 13.0 %collective-permute-start.1 = (f32[8,3,4,4096]{3,2,1,0:T(4,128)}, f32[8,3,4,4096]{3,2,1,0:T(4,128)S(1)}, u32[]{:S(2)}, u32[]{:S(2)}) collective-permute-start(f32[8,3,4,4096]{3,2,1,0:T(4,128)} %bitcast.9), channel_id=1, source_target_pairs={{0,8},{8,0},{16,24},{24,16},{1,9},{9,1},{17,25},{25,17},{2,10},{10... | collective-permute-start | bytes 4718600 | tf_op jit(solution)/shard_map/ppermute | solution.py:113
  7.1 13.3 %collective-permute-start.2 = (f32[4,3,2,16,128]{4,3,2,1,0:T(8,128)S(1)}, f32[4,3,2,16,128]{4,3,2,1,0:T(8,128)S(1)}, u32[]{:S(2)}, u32[]{:S(2)}) collective-permute-start(f32[4,3,2,16,128]{4,3,2,1,0:T(8,128)S(1)} %get-tuple-element.54), channel_id=1, source_target_pairs={{0,16},{8,24},{1,17},{9,25},{2,18},{10,26},{3,19},{11,27},{4,20},{... | collective-permute-start | bytes 589832 | tf_op jit(solution)/shard_map/ppermute | solution.py:607
  11.8 8.5 %collective-permute-start.5 = (f32[6,2,16,128]{3,2,1,0:T(8,128)S(1)}, f32[6,2,16,128]{3,2,1,0:T(8,128)S(1)}, u32[]{:S(2)}, u32[]{:S(2)}) collective-permute-start(f32[6,2,16,128]{3,2,1,0:T(8,128)S(1)} %get-tuple-element.58), channel_id=1, source_target_pairs={{0,8},{8,0},{16,24},{24,16},{1,9},{9,1},{17,25},{25,17},{2,10},{10... | collective-permute-start | bytes 294920 | tf_op jit(solution)/shard_map/ppermute | solution.py:113
  11.9 8.5 %collective-permute-start.6 = (f32[6,2,16,128]{3,2,1,0:T(8,128)S(1)}, f32[6,2,16,128]{3,2,1,0:T(8,128)S(1)}, u32[]{:S(2)}, u32[]{:S(2)}) collective-permute-start(f32[6,2,16,128]{3,2,1,0:T(8,128)S(1)} %get-tuple-element.59), channel_id=1, source_target_pairs={{8,12},{9,13},{10,14},{11,15},{12,8},{13,9},{14,10},{15,11},{24,28... | collective-permute-start | bytes 294920 | tf_op jit(solution)/shard_map/ppermute | solution.py:103
  12.6 7.8 %collective-permute-start.3 = (f32[6,16,128]{2,1,0:T(8,128)S(1)}, f32[6,16,128]{2,1,0:T(8,128)S(1)}, u32[]{:S(2)}, u32[]{:S(2)}) collective-permute-start(f32[6,16,128]{2,1,0:T(8,128)S(1)} %get-tuple-element.56), channel_id=1, source_target_pairs={{0,1},{1,0},{2,3},{3,2},{4,5},{5,4},{6,7},{7,6},{8,9},{9,8},{10,11... | collective-permute-start | bytes 147464 | tf_op jit(solution)/shard_map/ppermute | solution.py:106
  14.2 6.2 %collective-permute-start.4 = (f32[6,16,128]{2,1,0:T(8,128)S(1)}, f32[6,16,128]{2,1,0:T(8,128)S(1)}, u32[]{:S(2)}, u32[]{:S(2)}) collective-permute-start(f32[6,16,128]{2,1,0:T(8,128)S(1)} %get-tuple-element.57), channel_id=1, source_target_pairs={{0,2},{1,3},{2,0},{3,1},{4,6},{5,7},{6,4},{7,5},{8,10},{9,11},{10,... | collective-permute-start | bytes 147464 | tf_op jit(solution)/shard_map/ppermute | solution.py:107
  21.7 5.7 %collective-permute-start.7 = (f32[4,3,2,16,128]{4,3,2,1,0:T(8,128)S(1)}, f32[4,3,2,16,128]{4,3,2,1,0:T(8,128)S(1)}, u32[]{:S(2)}, u32[]{:S(2)}) collective-permute-start(f32[4,3,2,16,128]{4,3,2,1,0:T(8,128)S(1)} %get-tuple-element.61.refs_3_), channel_id=1, source_target_pairs={{0,16},{8,24},{16,0},{24,8},{1,17},{9,25},{17,1},{25,9},{2,18},{10... | collective-permute-start | bytes 589832 | tf_op jit(solution)/shard_map/ppermute | solution.py:613
  28.2 7.7 %collective-permute-start.10 = (f32[6,2,16,128]{3,2,1,0:T(8,128)S(1)}, f32[6,2,16,128]{3,2,1,0:T(8,128)S(1)}, u32[]{:S(2)}, u32[]{:S(2)}) collective-permute-start(f32[6,2,16,128]{3,2,1,0:T(8,128)S(1)} %get-tuple-element.66), channel_id=1, source_target_pairs={{0,8},{8,0},{16,24},{24,16},{1,9},{9,1},{17,25},{25,17},{2,10},{10... | collective-permute-start | bytes 294920 | tf_op jit(solution)/shard_map/ppermute | solution.py:113
  30.6 5.3 %collective-permute-start.11 = (f32[6,2,16,128]{3,2,1,0:T(8,128)S(1)}, f32[6,2,16,128]{3,2,1,0:T(8,128)S(1)}, u32[]{:S(2)}, u32[]{:S(2)}) collective-permute-start(f32[6,2,16,128]{3,2,1,0:T(8,128)S(1)} %get-tuple-element.67), channel_id=1, source_target_pairs={{8,12},{9,13},{10,14},{11,15},{12,8},{13,9},{14,10},{15,11},{24,28... | collective-permute-start | bytes 294920 | tf_op jit(solution)/shard_map/ppermute | solution.py:103
  37.2 6.4 %collective-permute-start.12 = (f32[4,3,2,16,128]{4,3,2,1,0:T(8,128)S(1)}, f32[4,3,2,16,128]{4,3,2,1,0:T(8,128)S(1)}, u32[]{:S(2)}, u32[]{:S(2)}) collective-permute-start(f32[4,3,2,16,128]{4,3,2,1,0:T(8,128)S(1)} %get-tuple-element.69.refs_3_), channel_id=1, source_target_pairs={{0,16},{8,24},{16,0},{24,8},{1,17},{9,25},{17,1},{25,9},{2,18},{10... | collective-permute-start | bytes 589832 | tf_op jit(solution)/shard_map/ppermute | solution.py:613
  44.4 7.8 %collective-permute-start.15 = (f32[6,2,16,128]{3,2,1,0:T(8,128)S(1)}, f32[6,2,16,128]{3,2,1,0:T(8,128)S(1)}, u32[]{:S(2)}, u32[]{:S(2)}) collective-permute-start(f32[6,2,16,128]{3,2,1,0:T(8,128)S(1)} %get-tuple-element.73), channel_id=1, source_target_pairs={{0,8},{8,0},{16,24},{24,16},{1,9},{9,1},{17,25},{25,17},{2,10},{10... | collective-permute-start | bytes 294920 | tf_op jit(solution)/shard_map/ppermute | solution.py:113
  45.7 6.5 %collective-permute-start.16 = (f32[6,2,16,128]{3,2,1,0:T(8,128)S(1)}, f32[6,2,16,128]{3,2,1,0:T(8,128)S(1)}, u32[]{:S(2)}, u32[]{:S(2)}) collective-permute-start(f32[6,2,16,128]{3,2,1,0:T(8,128)S(1)} %get-tuple-element.74), channel_id=1, source_target_pairs={{8,12},{9,13},{10,14},{11,15},{12,8},{13,9},{14,10},{15,11},{24,28... | collective-permute-start | bytes 294920 | tf_op jit(solution)/shard_map/ppermute | solution.py:103
  53.4 6.8 %collective-permute-start.17 = (f32[4,3,2,16,128]{4,3,2,1,0:T(8,128)S(1)}, f32[4,3,2,16,128]{4,3,2,1,0:T(8,128)S(1)}, u32[]{:S(2)}, u32[]{:S(2)}) collective-permute-start(f32[4,3,2,16,128]{4,3,2,1,0:T(8,128)S(1)} %get-tuple-element.76.refs_3_), channel_id=1, source_target_pairs={{0,16},{8,24},{16,0},{24,8},{1,17},{9,25},{17,1},{25,9},{2,18},{10... | collective-permute-start | bytes 589832 | tf_op jit(solution)/shard_map/ppermute | solution.py:613
  61.1 6.1 %collective-permute-start.20 = (f32[6,2,16,128]{3,2,1,0:T(8,128)S(1)}, f32[6,2,16,128]{3,2,1,0:T(8,128)S(1)}, u32[]{:S(2)}, u32[]{:S(2)}) collective-permute-start(f32[6,2,16,128]{3,2,1,0:T(8,128)S(1)} %get-tuple-element.80), channel_id=1, source_target_pairs={{0,8},{8,0},{16,24},{24,16},{1,9},{9,1},{17,25},{25,17},{2,10},{10... | collective-permute-start | bytes 294920 | tf_op jit(solution)/shard_map/ppermute | solution.py:113
  62.0 5.2 %collective-permute-start.21 = (f32[6,2,16,128]{3,2,1,0:T(8,128)S(1)}, f32[6,2,16,128]{3,2,1,0:T(8,128)S(1)}, u32[]{:S(2)}, u32[]{:S(2)}) collective-permute-start(f32[6,2,16,128]{3,2,1,0:T(8,128)S(1)} %get-tuple-element.81), channel_id=1, source_target_pairs={{8,12},{9,13},{10,14},{11,15},{12,8},{13,9},{14,10},{15,11},{24,28... | collective-permute-start | bytes 294920 | tf_op jit(solution)/shard_map/ppermute | solution.py:103
  68.4 6.2 %collective-permute-start.22 = (f32[4,3,2,16,128]{4,3,2,1,0:T(8,128)S(1)}, f32[4,3,2,16,128]{4,3,2,1,0:T(8,128)S(1)}, u32[]{:S(2)}, u32[]{:S(2)}) collective-permute-start(f32[4,3,2,16,128]{4,3,2,1,0:T(8,128)S(1)} %get-tuple-element.83.refs_3_), channel_id=1, source_target_pairs={{0,16},{8,24},{16,0},{24,8},{1,17},{9,25},{17,1},{25,9},{2,18},{10... | collective-permute-start | bytes 589832 | tf_op jit(solution)/shard_map/ppermute | solution.py:613
  75.4 9.5 %collective-permute-start.25 = (f32[6,2,16,128]{3,2,1,0:T(8,128)S(1)}, f32[6,2,16,128]{3,2,1,0:T(8,128)S(1)}, u32[]{:S(2)}, u32[]{:S(2)}) collective-permute-start(f32[6,2,16,128]{3,2,1,0:T(8,128)S(1)} %get-tuple-element.87), channel_id=1, source_target_pairs={{0,8},{8,0},{16,24},{24,16},{1,9},{9,1},{17,25},{25,17},{2,10},{10... | collective-permute-start | bytes 294920 | tf_op jit(solution)/shard_map/ppermute | solution.py:113
  77.0 7.9 %collective-permute-start.26 = (f32[6,2,16,128]{3,2,1,0:T(8,128)S(1)}, f32[6,2,16,128]{3,2,1,0:T(8,128)S(1)}, u32[]{:S(2)}, u32[]{:S(2)}) collective-permute-start(f32[6,2,16,128]{3,2,1,0:T(8,128)S(1)} %get-tuple-element.88), channel_id=1, source_target_pairs={{8,12},{9,13},{10,14},{11,15},{12,8},{13,9},{14,10},{15,11},{24,28... | collective-permute-start | bytes 294920 | tf_op jit(solution)/shard_map/ppermute | solution.py:103
  86.1 7.4 %collective-permute-start.27 = (f32[4,3,2,16,128]{4,3,2,1,0:T(8,128)S(1)}, f32[4,3,2,16,128]{4,3,2,1,0:T(8,128)S(1)}, u32[]{:S(2)}, u32[]{:S(2)}) collective-permute-start(f32[4,3,2,16,128]{4,3,2,1,0:T(8,128)S(1)} %get-tuple-element.90.refs_3_.refs_4_), channel_id=1, source_target_pairs={{0,16},{8,24},{16,0},{24,8},{1,17},{9,25},{17,1},{25,9},{2,18},{10... | collective-permute-start | bytes 589832 | tf_op jit(solution)/shard_map/ppermute | solution.py:613
  94.4 7.8 %collective-permute-start.31 = (f32[6,2,16,128]{3,2,1,0:T(8,128)S(1)}, f32[6,2,16,128]{3,2,1,0:T(8,128)S(1)}, u32[]{:S(2)}, u32[]{:S(2)}) collective-permute-start(f32[6,2,16,128]{3,2,1,0:T(8,128)S(1)} %get-tuple-element.98), channel_id=1, source_target_pairs={{0,8},{8,0},{16,24},{24,16},{1,9},{9,1},{17,25},{25,17},{2,10},{10... | collective-permute-start | bytes 294920 | tf_op jit(solution)/shard_map/ppermute | solution.py:113
  94.4 7.8 %collective-permute-start.32 = (f32[6,2,16,128]{3,2,1,0:T(8,128)S(1)}, f32[6,2,16,128]{3,2,1,0:T(8,128)S(1)}, u32[]{:S(2)}, u32[]{:S(2)}) collective-permute-start(f32[6,2,16,128]{3,2,1,0:T(8,128)S(1)} %get-tuple-element.99), channel_id=1, source_target_pairs={{8,12},{9,13},{10,14},{11,15},{12,8},{13,9},{14,10},{15,11},{24,28... | collective-permute-start | bytes 294920 | tf_op jit(solution)/shard_map/ppermute | solution.py:103
  95.1 7.1 %collective-permute-start.29 = (f32[6,16,128]{2,1,0:T(8,128)S(1)}, f32[6,16,128]{2,1,0:T(8,128)S(1)}, u32[]{:S(2)}, u32[]{:S(2)}) collective-permute-start(f32[6,16,128]{2,1,0:T(8,128)S(1)} %get-tuple-element.96), channel_id=1, source_target_pairs={{0,1},{1,0},{2,3},{3,2},{4,5},{5,4},{6,7},{7,6},{8,9},{9,8},{10,11... | collective-permute-start | bytes 147464 | tf_op jit(solution)/shard_map/ppermute | solution.py:106
  95.2 7.0 %collective-permute-start.30 = (f32[6,16,128]{2,1,0:T(8,128)S(1)}, f32[6,16,128]{2,1,0:T(8,128)S(1)}, u32[]{:S(2)}, u32[]{:S(2)}) collective-permute-start(f32[6,16,128]{2,1,0:T(8,128)S(1)} %get-tuple-element.97), channel_id=1, source_target_pairs={{0,2},{1,3},{2,0},{3,1},{4,6},{5,7},{6,4},{7,5},{8,10},{9,11},{10,... | collective-permute-start | bytes 147464 | tf_op jit(solution)/shard_map/ppermute | solution.py:107
  98.7 6.6 %collective-permute-start.28 = (f32[4,3,4,4096]{3,2,1,0:T(4,128)S(1)}, f32[4,3,4,4096]{3,2,1,0:T(4,128)S(1)}, u32[]{:S(2)}, u32[]{:S(2)}) collective-permute-start(f32[4,3,4,4096]{3,2,1,0:T(4,128)S(1)} %get-tuple-element.93), channel_id=1, source_target_pairs={{0,8},{8,0},{16,24},{24,16},{1,9},{9,1},{17,25},{25,17},{2,10},{10... | collective-permute-start | bytes 2359304 | tf_op jit(solution)/shard_map/ppermute | solution.py:113
  (20 other events, 113.3 us)

commit v5 on v4

--- a/solution.py
+++ b/solution.py
@@ -16,6 +16,7 @@
 WORK = 6_000_000
 XP, XM, YP, YM, ZP, ZM, XG, YG, ZG, Q, INV, LIVE, K0 = range(13)
 FACES = 6
+GRANT = 67_043_328
 F32 = jnp.float32
 
 
@@ -27,18 +28,18 @@
     return lead + (2, EDGE, LANES)
 
 
-def call(kernel, tables, ins, outs, scratch=(), flops=2_000_000, in_hbm=None):
-    vmem = pl.BlockSpec(memory_space=pltpu.VMEM)
-    tables = tables or []
+def call(kernel, ins, outs, scratch=(), flops=2_000_000, far=(), far_outs=(), alias=None, grant=24 << 20):
+    vmem, hbm = pl.BlockSpec(memory_space=pltpu.VMEM), pl.BlockSpec(memory_space=pltpu.HBM)
     return pl.pallas_call(
         kernel,
-        in_specs=[pl.BlockSpec(memory_space=pltpu.SMEM)] * len(tables) + [vmem] * len(ins),
-        out_specs=[vmem if s != in_hbm else pl.BlockSpec(memory_space=pltpu.HBM) for s in outs],
+        in_specs=[hbm if i in far else vmem for i in range(len(ins))],
+        out_specs=[hbm if i in far_outs else vmem for i in range(len(outs))],
         out_shape=[jax.ShapeDtypeStruct(s, F32) for s in outs],
         scratch_shapes=list(scratch),
-        compiler_params=pltpu.CompilerParams(vmem_limit_bytes=24 * 1024 * 1024),
+        input_output_aliases=alias or {},
+        compiler_params=pltpu.CompilerParams(vmem_limit_bytes=grant),
         cost_estimate=pl.CostEstimate(flops=flops, bytes_accessed=1_000_000, transcendentals=0),
-    )(*tables, *ins)
+    )(*ins)
 
 
 class Shape:
@@ -273,7 +274,24 @@
     return jnp.where(holder[slot, face] >= 0, 1.0, 0.0).astype(F32)
 
 
-def coefficient_kernel(sh, holder, mask, viscosity, peclet, initial, coef, first, rows, tiles):
+def prepare_kernel(sh, *refs):
+    far, (coef, first, own), rest = refs[:6], refs[6:9], refs[9:]
+    near, (sems, rows, tiles, native_rows) = rest[:6], rest[6:]
+    mine = pl.ds(sh.upper() * sh.half, sh.half)
+    copies = [
+        pltpu.make_async_copy(a.at[mine] if i == 5 else a, b, sems.at[i])
+        for i, (a, b) in enumerate(zip(far, near))
+    ]
+    for copy in copies:
+        copy.start()
+    for copy in copies[:5]:
+        copy.wait()
+    coefficients(sh, *near[:5], coef, first, rows, tiles)
+    copies[5].wait()
+    unpack_half(sh, 0, near[5], own, 0, native_rows, 0)
+
+
+def coefficients(sh, holder, mask, viscosity, peclet, initial, coef, first, rows, tiles):
     chip = sh.chip()
     slots = sh.slots
 
@@ -351,29 +369,29 @@
     lax.fori_loop(0, sh.half, step, 0)
 
 
-def assemble(sh, whole, other, field, rows):
+def unpack_half(sh, which, source, field, first, rows, base=None):
+    def visit(j, comp):
+        slot = (sh.upper() * sh.half if base is None else base) + j
+
+        def read(c):
+            return source[slot, comp, :, c * LANES : (c + 1) * LANES]
+
+        def write(i, h, value):
+            field[j, comp, first + i, h] = value
+
+        rows_to_tiles(read, sh.local, rows.at[2 * j + which], write)
+
+    over_tiles(sh, visit)
+
+
+def gather_kernel(sh, own, other, field, last, *rest):
     core = sh.core()
+    unpack_half(sh, 1, other, field, (1 - core) * sh.local, rest[-1])
 
     def visit(j, comp):
-        slot = sh.upper() * sh.half + j
-        for part, source in enumerate((whole, other)):
-            first = (core if part == 0 else 1 - core) * sh.local
-
-            def read(c, source=source):
-                return source[slot, sh.base + comp, :, c * LANES : (c + 1) * LANES]
-
-            def write(i, h, value, first=first):
-                field[j, comp, first + i, h] = value
-
-            rows_to_tiles(read, sh.local, rows.at[2 * j + part], write)
-
-    over_tiles(sh, visit)
-
-
-def gather_kernel(sh, whole, other, field, last, *rest):
-    assemble(sh, whole, other, field, rest[-1])
-
-    def visit(j, comp):
+        for i in range(sh.local):
+            for h in range(2):
+                field[j, comp, core * sh.local + i, h] = own[j, comp, i, h]
         last[j, comp] = field[j, comp, sh.span - 1]
 
     over_tiles(sh, visit)
@@ -381,7 +399,9 @@
 
 
 def residual_inner_kernel(sh, coef, field, whole, other, inner, force, rows):
-    assemble(sh, whole, other, force, rows)
+    core = sh.core()
+    unpack_half(sh, 0, whole, force, core * sh.local, rows)
+    unpack_half(sh, 1, other, force, (1 - core) * sh.local, rows)
 
     def visit(j, comp):
         prior = None
@@ -474,7 +494,7 @@
     pack_faces(sh, tile, field, messages)
 
 
-def velocity_kernel(sh, whole, other, field, out, send, rows, kept, sem):
+def velocity_kernel(sh, whole, other, field, out, send, rows, kept, sems):
     core = sh.core()
     own, others = core * sh.local, (1 - core) * sh.local
 
@@ -494,18 +514,52 @@
             lambda i, h: field[j, comp, others + i, h], sh.local, rows.at[2 * j + 1], pass_on
         )
 
-    over_tiles(sh, visit)
-    put_half(sh, sh.upper(), kept, out, sem)
-
-
-def put_half(sh, which, source, out, sem):
-    copy = pltpu.make_async_copy(source, out.at[pl.ds(which * sh.half, sh.half)], sem)
-    copy.start()
-    copy.wait()
-
-
-def place_kernel(sh, half, partial, out, sem):
-    put_half(sh, 1 - sh.upper(), half, out, sem)
+    def component(comp):
+        for j in range(sh.half):
+            visit(j, comp)
+        put_copy(sh, comp, kept, out, sems).start()
+
+    over_components(sh, component)
+    wait_copies(sh, kept, out, sems)
+
+
+def put_copy(sh, comp, kept, out, sems):
+    slots = pl.ds(sh.upper() * sh.half, sh.half)
+    return pltpu.make_async_copy(kept.at[:, comp], out.at[slots, comp], sems.at[comp])
+
+
+def wait_copies(sh, kept, out, sems):
+    for comp in range(sh.comps):
+        put_copy(sh, comp, kept, out, sems).wait()
+
+
+def bounce_copies(sh, comp, half, out, buffer, sems):
+    slots = pl.ds((1 - sh.upper()) * sh.half, sh.half)
+    first = pltpu.make_async_copy(half.at[:, comp], buffer.at[:, comp], sems.at[0, comp])
+    if out is None:
+        return first, None
+    return first, pltpu.make_async_copy(
+        buffer.at[:, comp], out.at[slots, comp], sems.at[1, comp]
+    )
+
+
+def start_bounce(sh, half, buffer, sems):
+    for comp in range(sh.comps):
+        bounce_copies(sh, comp, half, None, buffer, sems)[0].start()
+
+
+def end_bounce(sh, half, out, buffer, sems):
+    for comp in range(sh.comps):
+        first, second = bounce_copies(sh, comp, half, out, buffer, sems)
+        first.wait()
+        second.start()
+    for comp in range(sh.comps):
+        bounce_copies(sh, comp, half, out, buffer, sems)[1].wait()
+
+
+def place_kernel(sh, half, partial, out, buffer, sems):
+    start_bounce(sh, half, buffer, sems)
+    end_bounce(sh, half, out, buffer, sems)
 
 
 def final_inner_kernel(sh, coef, field, scaled, *rest):
@@ -530,7 +584,12 @@
 
 def final_outer_kernel(sh, mine, coef, inner, *rest):
     faces = rest[: sh.x_count + 1]
-    inner_in, z_in, out, z_ghost, hold, rows, *kept = rest[sh.x_count + 1 :]
+    if mine:
+        inner_in, z_in, half, partial, out, placed, z_ghost, hold, rows, *kept = rest[sh.x_count + 1 :]
+        bounce = kept[2:]
+        start_bounce(sh, half, *bounce)
+    else:
+        inner_in, z_in, out, z_ghost, hold, rows = rest[sh.x_count + 1 :]
     target = kept[0] if mine else out
     place_z_ghost(sh, inner_in, z_in, z_ghost)
     core = sh.core()
@@ -550,12 +609,19 @@
 
             tiles_to_rows(lambda i, h: hold[j, i, h], sh.local, rows.at[j], write)
 
+        def component(comp, visit=visit):
+            for j in range(sh.half):
+                visit(j, comp)
+            if mine:
+                put_copy(sh, comp, kept[0], out, kept[1]).start()
+
         @pl.when(core == (number if mine else 1 - number))
-        def _(visit=visit):
-            over_tiles(sh, visit)
+        def _(component=component):
+            over_components(sh, component)
 
     if mine:
-        put_half(sh, sh.upper(), kept[0], out, kept[1])
+        end_bounce(sh, half, placed, *bounce)
+        wait_copies(sh, kept[0], out, kept[1])
 
 
 def bind(kernel, sh, *fixed):
@@ -588,23 +654,40 @@
 
     rows = pltpu.VMEM((2 * half, CHUNKS * local, LANES), F32)
 
-    coef, first = call(
-        bind(coefficient_kernel, sh),
-        [neighbour_holder, live_patch_mask],
-        [viscosity, peclet.transpose(1, 0, 2), initial_velocity.transpose(1, 0, 2)],
-        [tile_shape(half, K0 + sh.chips), tile_shape(half, COMPONENTS)],
-        [pltpu.VMEM((CHUNKS * slots, LANES), F32), pltpu.VMEM(tile_shape(7, slots), F32)],
+    native = (half, COMPONENTS, local, CHUNKS * LANES)
+    whole = (slots,) + native[1:]
+    params = [
+        neighbour_holder,
+        live_patch_mask,
+        viscosity,
+        peclet.transpose(1, 0, 2),
+        initial_velocity.transpose(1, 0, 2),
+    ]
+    near = [(pltpu.SMEM if i < 2 else pltpu.VMEM)(p.shape, p.dtype) for i, p in enumerate(params)]
+    sh = shapes[0]
+    coef, first, own = call(
+        bind(prepare_kernel, sh),
+        params + [velocity],
+        [tile_shape(half, K0 + sh.chips), tile_shape(half, COMPONENTS), tile_shape(half, COMPONENTS, local)],
+        near
+        + [
+            pltpu.VMEM(native, F32),
+            pltpu.SemaphoreType.DMA((6,)),
+            pltpu.VMEM((CHUNKS * slots, LANES), F32),
+            pltpu.VMEM(tile_shape(7, slots), F32),
+            rows,
+        ],
+        flops=WORK,
+        far=range(6),
+        grant=GRANT - velocity.size * 4 * 9 // 4,
     )
+    coef, first, own, arrived = lax.optimization_barrier((coef, first, own, velocity_other))
     fields, faces, befores = [], [], []
     for sh in shapes:
         field, last, *out = call(
-            bind(gather_kernel, sh),
-            None,
-            [velocity, velocity_other],
-            [sh.field, sh.slice] + sh.messages,
-            [rows],
+            bind(gather_kernel, sh), [own, arrived], [sh.field, sh.slice] + sh.messages, [rows]
         )
-        befores.append(lax.ppermute(last, "tm", [(a, a + 2) for a in range(n_time - 2)]))
+        befores.append(lax.ppermute(last, "tm", [(a, (a + 2) % n_time) for a in range(n_time)]))
         faces.append(exchange(sh, out, n_time, places))
         fields.append(field)
 
@@ -618,7 +701,6 @@
     for sh, field, before, face in zip(shapes, fields, befores, faces):
         inner, _ = call(
             bind(residual_inner_kernel, sh),
-            None,
             [coef, field, force, force_other],
             [sh.field, sh.field],
             [rows],
@@ -626,7 +708,6 @@
         )
         scaled, partial, last = call(
             bind(residual_outer_kernel, sh),
-            None,
             [coef, inner, before, first] + face,
             [sh.field, sh.field, sh.slice],
             [sh.z_ghost],
@@ -642,14 +723,12 @@
             if sweep > 0:
                 (inner,) = call(
                     bind(sweep_inner_kernel, sh),
-                    None,
                     [coef, corrections[number], scaleds[number]],
                     [sh.field],
                     flops=sh.comps * WORK,
                 )
                 partials[number], last = call(
                     bind(sweep_outer_kernel, sh),
-                    None,
                     [coef, inner] + faces[number],
                     [sh.field, sh.slice],
                     [sh.z_ghost],
@@ -658,69 +737,59 @@
                 ends[number] = chip_ends(sh, last)
             corrections[number], *out = call(
                 bind(close_kernel, sh),
-                None,
                 [coef, partials[number]] + ends[number],
                 [sh.field] + sh.messages,
                 flops=sh.comps * WORK,
             )
             faces[number] = exchange(sh, out, n_time, places)
-    native = (half, COMPONENTS, local, CHUNKS * LANES)
-    whole = (slots,) + native[1:]
-
-    def place(out, other):
-        placed = pl.pallas_call(
-            bind(place_kernel, sh),
-            in_specs=[
-                pl.BlockSpec(memory_space=pltpu.VMEM),
-                pl.BlockSpec(memory_space=pltpu.HBM),
-            ],
-            out_specs=pl.BlockSpec(memory_space=pltpu.HBM),
-            out_shape=jax.ShapeDtypeStruct(whole, F32),
-            scratch_shapes=[pltpu.SemaphoreType.DMA(())],
-            input_output_aliases={1: 0},
-            name="place",
-        )(other, out)
-        return placed.transpose(0, 2, 1, 3)
-
     sh = shapes[0]
     (inner,) = call(
         bind(final_inner_kernel, sh),
-        None,
         [coef, corrections[0], scaleds[0]] + ends[0],
         [sh.field],
         flops=sh.comps * WORK,
     )
     held_back, inner = lax.optimization_barrier((corrections[0], inner))
+    copied = [pltpu.VMEM(native, F32), pltpu.SemaphoreType.DMA((COMPONENTS,))]
+    bounce = [pltpu.VMEM(native, F32), pltpu.SemaphoreType.DMA((2, COMPONENTS))]
+    velocity_out, send = call(
+        bind(velocity_kernel, sh),
+        [velocity, velocity_other, held_back],
+        [whole, native],
+        [rows] + copied,
+        flops=WORK,
+        far_outs=(0,),
+    )
+    velocity_other = swap_cores(send, n_time)
     (send,) = call(
         bind(final_outer_kernel, sh, False),
-        None,
         [coef, inner] + faces[0],
         [native],
         [sh.z_ghost, pltpu.VMEM(tile_shape(half, local), F32), rows],
         flops=WORK,
     )
     residual_other = swap_cores(send, n_time)
-    copied = [pltpu.VMEM(native, F32), pltpu.SemaphoreType.DMA(())]
-    (residual_out,) = call(
+    ins = [coef, inner] + faces[0] + [velocity_other, velocity_out]
+    residual_out, corrected_velocity = call(
         bind(final_outer_kernel, sh, True),
-        None,
-        [coef, inner] + faces[0],
+        ins,
+        [whole, whole],
+        [sh.z_ghost, pltpu.VMEM(tile_shape(half, local), F32), rows] + copied + bounce,
+        flops=WORK,
+        far=(len(ins) - 2, len(ins) - 1),
+        far_outs=(0, 1),
+        alias={len(ins) - 1: 1},
+    )
+    (corrected_residual,) = call(
+        bind(place_kernel, sh),
+        [residual_other, residual_out],
         [whole],
-        [sh.z_ghost, pltpu.VMEM(tile_shape(half, local), F32), rows] + copied,
-        flops=WORK,
-        in_hbm=whole,
+        bounce,
+        far=(0, 1),
+        far_outs=(0,),
+        alias={1: 0},
     )
-    out, send = call(
-        bind(velocity_kernel, sh),
-        None,
-        [velocity, velocity_other, held_back],
-        [whole, native],
-        [rows] + copied,
-        flops=WORK,
-        in_hbm=whole,
-    )
-    corrected_velocity = place(out, swap_cores(send, n_time))
-    return corrected_velocity, place(residual_out, residual_other)
+    return corrected_velocity.transpose(0, 2, 1, 3), corrected_residual.transpose(0, 2, 1, 3)
 
 
 def solution(mesh):

time: 112 us -> 106 us (0.946)
  waiting for transfers between devices: 41.4 us -> 38.5 us
  local copies, waits for them, and re-layouts: 3.24 us -> 1.23 us
    ppermute x10, waiting for transfers between devices: 3.18 us -> 0.77 us  [swap_cores(): return lax.ppermute(value, 'tm', [(t, t ^ 1) for t in range(n_time)])]
    unnamed x20 -> x10, local copies, waits for them, and re-layouts: 3.24 us -> 1.23 us
    ppermute x1, starting transfers between devices: 4.76 us -> 2.95 us  [body(): lax.ppermute(last, 'tm', [(a, (a + 2) % n_time) for a in range(n_time)])]
    pallas_call x23 -> x22, Pallas kernels: 33.9 us -> 34.3 us  [call(): pl.pallas_call(kernel, in_specs=[hbm if i in far else vmem for i in range...]
  transfers between devices with their start and end apart: 34 -> 34, of which waited for: 14 -> 14; matrix products, arithmetic and copies ran while one was open for 0% -> 0% of each run, Pallas kernels for 19% -> 22%
where the time goes in v5:
time: 106 us; the launch traced here: 105 us
  waiting for transfers between devices  38.5 us (36%)
  Pallas kernels  34.3 us (32%)
  starting transfers between devices  30.5 us (29%)
  local copies, waits for them, and re-layouts  1.23 us (1%)
    pallas_call x22, Pallas kernels, call(): pl.pallas_call(kernel, in_specs=[hbm if i in far else vmem for i in range...  34.3 us
    ppermute x5, waiting for transfers between devices, chip_ends(): lax.ppermute(last, 'tm', [(a, (a + 2 * back) % n_time) for a in range(n_t...  29.4 us
    ppermute x10, starting transfers between devices, swap_cores(): return lax.ppermute(value, 'tm', [(t, t ^ 1) for t in range(n_time)])  10.6 us
    ppermute x6, starting transfers between devices, exchange(): x_in.append(lax.ppermute(x_out[i], axes, pairs(bit, sh.bits[0], False)))  7.03 us
    ppermute x6, waiting for transfers between devices, exchange(): y_in = lax.ppermute(y_out, axes, pairs(sh.bits[1][0], sh.bits[1], False))  5.14 us
    ppermute x6, starting transfers between devices, exchange(): z_in = lax.ppermute(z_out, axes, pairs(sh.bits[2][0], sh.bits[2], True))  3.94 us
    ppermute x6, waiting for transfers between devices, exchange(): x_in.append(lax.ppermute(x_out[i], axes, pairs(bit, sh.bits[0], False)))  3.17 us
    ppermute x5, starting transfers between devices, chip_ends(): lax.ppermute(last, 'tm', [(a, (a + 2 * back) % n_time) for a in range(n_t...  2.98 us
  transfers between devices with their start and end apart: 34, of which 14 were waited for; matrix products, arithmetic and copies ran while one was open for 0% of the time, Pallas kernels for 22%

profile of v5, /device:TPU:0, one launch (start us, length us, event | category | flops | bytes accessed | tf_op | source)
XLA Modules:
  0.0 105.5 jit_solution(15842418733706450575)
XLA Ops:
  1.3 3.3 %shard_map.86 = (f32[4,14,2,16,128]{4,3,2,1,0:T(8,128)}, f32[4,3,2,16,128]{4,3,2,1,0:T(8,128)}, f32[4,3,4,2,16,128]{5,4,3,2,1,0:T(8,128)}) custom-call(s32[8,6]{1,0:T(8,128)} %refs_0_.1, s32[8]{0:T(128)} %refs_1_.1, f32[8,4096]{1,0:T(8,128)} %refs_2_.1, f32[3,8,4096]{2,1,0:T(8,128)} %bitcast.13, f32[3,8,4096]{2,1,0:T(8,128)} %bitcast.14, ...), custom_call_target="tpu_custom_call" | custom-call | flops 6000000 | bytes 1000000 | tf_op jit(solution)/shard_map/pallas_call | solution.py:33
  6.8 3.0 %collective-permute-start.2 = (f32[4,3,2,16,128]{4,3,2,1,0:T(8,128)S(1)}, f32[4,3,2,16,128]{4,3,2,1,0:T(8,128)S(1)}, u32[]{:S(2)}, u32[]{:S(2)}) collective-permute-start(f32[4,3,2,16,128]{4,3,2,1,0:T(8,128)S(1)} %get-tuple-element.66), channel_id=1, source_target_pairs={{0,16},{8,24},{16,0},{24,8},{1,17},{9,25},{17,1},{25,9},{2,18},{10... | collective-permute-start | bytes 589832 | tf_op jit(solution)/shard_map/ppermute | solution.py:690
  10.5 1.6 %collective-permute-start.3 = (f32[6,16,128]{2,1,0:T(8,128)S(1)}, f32[6,16,128]{2,1,0:T(8,128)S(1)}, u32[]{:S(2)}, u32[]{:S(2)}) collective-permute-start(f32[6,16,128]{2,1,0:T(8,128)S(1)} %get-tuple-element.68), channel_id=1, source_target_pairs={{0,1},{1,0},{2,3},{3,2},{4,5},{5,4},{6,7},{7,6},{8,9},{9,8},{10,11... | collective-permute-start | bytes 147464 | tf_op jit(solution)/shard_map/ppermute | solution.py:107
  12.0 1.6 %collective-permute-start.4 = (f32[6,16,128]{2,1,0:T(8,128)S(1)}, f32[6,16,128]{2,1,0:T(8,128)S(1)}, u32[]{:S(2)}, u32[]{:S(2)}) collective-permute-start(f32[6,16,128]{2,1,0:T(8,128)S(1)} %get-tuple-element.69), channel_id=1, source_target_pairs={{0,2},{1,3},{2,0},{3,1},{4,6},{5,7},{6,4},{7,5},{8,10},{9,11},{10,... | collective-permute-start | bytes 147464 | tf_op jit(solution)/shard_map/ppermute | solution.py:108
  13.6 4.9 %shard_map.88 = (f32[4,3,8,2,16,128]{5,4,3,2,1,0:T(8,128)S(1)}, f32[4,3,8,2,16,128]{5,4,3,2,1,0:T(8,128)}) custom-call(f32[4,14,2,16,128]{4,3,2,1,0:T(8,128)S(1)} %copy-done, f32[4,3,8,2,16,128]{5,4,3,2,1,0:T(8,128)S(1)} %get-tuple-element.64.refs_1_, f32[8,3,4,4096]{3,2,1,0:T(4,128)S(1)} %bitcast.10, f32[8,3,4,4096]{3,2,1,0:T(4,128)} %collective-permute-done.1.refs_3_), custom_call_target="tpu_custom_call" | custom-call | flops 18000000 | bytes 1000000 | tf_op jit(solution)/shard_map/pallas_call | solution.py:33
  20.4 5.1 %collective-permute-done.7.refs_2_ = f32[4,3,2,16,128]{4,3,2,1,0:T(8,128)S(1)} collective-permute-done((f32[4,3,2,16,128]{4,3,2,1,0:T(8,128)S(1)}, f32[4,3,2,16,128]{4,3,2,1,0:T(8,128)S(1)}, u32[]{:S(2)}, u32[]{:S(2)}) %collective-permute-start.7) | collective-permute-done | bytes 196640 | tf_op jit(solution)/shard_map/ppermute | solution.py:696
  26.3 2.4 %collective-permute-start.10 = (f32[6,2,16,128]{3,2,1,0:T(8,128)S(1)}, f32[6,2,16,128]{3,2,1,0:T(8,128)S(1)}, u32[]{:S(2)}, u32[]{:S(2)}) collective-permute-start(f32[6,2,16,128]{3,2,1,0:T(8,128)S(1)} %get-tuple-element.78), channel_id=1, source_target_pairs={{0,8},{8,0},{16,24},{24,16},{1,9},{9,1},{17,25},{25,17},{2,10},{10... | collective-permute-start | bytes 294920 | tf_op jit(solution)/shard_map/ppermute | solution.py:114
  30.4 1.8 %shard_map.91.refs_1_ = f32[4,3,8,2,16,128]{5,4,3,2,1,0:T(8,128)S(1)} custom-call(f32[4,14,2,16,128]{4,3,2,1,0:T(8,128)S(1)} %copy-done, f32[4,3,8,2,16,128]{5,4,3,2,1,0:T(8,128)S(1)} %get-tuple-element.74.refs_1_, f32[4,3,8,2,16,128]{5,4,3,2,1,0:T(8,128)S(1)} %get-tuple-element.75.refs_2_), custom_call_target="tpu_custom_call" | custom-call | flops 18000000 | bytes 1000000 | tf_op jit(solution)/shard_map/pallas_call | solution.py:33
  35.9 5.8 %collective-permute-done.12.refs_2_ = f32[4,3,2,16,128]{4,3,2,1,0:T(8,128)S(1)} collective-permute-done((f32[4,3,2,16,128]{4,3,2,1,0:T(8,128)S(1)}, f32[4,3,2,16,128]{4,3,2,1,0:T(8,128)S(1)}, u32[]{:S(2)}, u32[]{:S(2)}) %collective-permute-start.12) | collective-permute-done | bytes 196640 | tf_op jit(solution)/shard_map/ppermute | solution.py:696
  44.5 1.6 %collective-permute-start.13 = (f32[6,16,128]{2,1,0:T(8,128)S(1)}, f32[6,16,128]{2,1,0:T(8,128)S(1)}, u32[]{:S(2)}, u32[]{:S(2)}) collective-permute-start(f32[6,16,128]{2,1,0:T(8,128)S(1)} %get-tuple-element.83), channel_id=1, source_target_pairs={{0,1},{1,0},{2,3},{3,2},{4,5},{5,4},{6,7},{7,6},{8,9},{9,8},{10,11... | collective-permute-start | bytes 147464 | tf_op jit(solution)/shard_map/ppermute | solution.py:107
  46.6 1.8 %shard_map.94.refs_1_ = f32[4,3,8,2,16,128]{5,4,3,2,1,0:T(8,128)S(1)} custom-call(f32[4,14,2,16,128]{4,3,2,1,0:T(8,128)S(1)} %copy-done, f32[4,3,8,2,16,128]{5,4,3,2,1,0:T(8,128)S(1)} %get-tuple-element.82.refs_1_, f32[4,3,8,2,16,128]{5,4,3,2,1,0:T(8,128)S(1)} %get-tuple-element.75.refs_2_), custom_call_target="tpu_custom_call" | custom-call | flops 18000000 | bytes 1000000 | tf_op jit(solution)/shard_map/pallas_call | solution.py:33
  48.7 1.6 %collective-permute-done.14.refs_3_ = f32[6,16,128]{2,1,0:T(8,128)S(1)} collective-permute-done((f32[6,16,128]{2,1,0:T(8,128)S(1)}, f32[6,16,128]{2,1,0:T(8,128)S(1)}, u32[]{:S(2)}, u32[]{:S(2)}) %collective-permute-start.14) | collective-permute-done | bytes 49184 | tf_op jit(solution)/shard_map/ppermute | solution.py:108
  52.2 6.2 %collective-permute-done.17.refs_2_ = f32[4,3,2,16,128]{4,3,2,1,0:T(8,128)S(1)} collective-permute-done((f32[4,3,2,16,128]{4,3,2,1,0:T(8,128)S(1)}, f32[4,3,2,16,128]{4,3,2,1,0:T(8,128)S(1)}, u32[]{:S(2)}, u32[]{:S(2)}) %collective-permute-start.17) | collective-permute-done | bytes 196640 | tf_op jit(solution)/shard_map/ppermute | solution.py:696
  61.7 1.8 %shard_map.97.refs_1_ = f32[4,3,8,2,16,128]{5,4,3,2,1,0:T(8,128)S(1)} custom-call(f32[4,14,2,16,128]{4,3,2,1,0:T(8,128)S(1)} %copy-done, f32[4,3,8,2,16,128]{5,4,3,2,1,0:T(8,128)S(1)} %get-tuple-element.89.refs_1_, f32[4,3,8,2,16,128]{5,4,3,2,1,0:T(8,128)S(1)} %get-tuple-element.75.refs_2_), custom_call_target="tpu_custom_call" | custom-call | flops 18000000 | bytes 1000000 | tf_op jit(solution)/shard_map/pallas_call | solution.py:33
  67.2 5.6 %collective-permute-done.22.refs_2_ = f32[4,3,2,16,128]{4,3,2,1,0:T(8,128)S(1)} collective-permute-done((f32[4,3,2,16,128]{4,3,2,1,0:T(8,128)S(1)}, f32[4,3,2,16,128]{4,3,2,1,0:T(8,128)S(1)}, u32[]{:S(2)}, u32[]{:S(2)}) %collective-permute-start.22) | collective-permute-done | bytes 196640 | tf_op jit(solution)/shard_map/ppermute | solution.py:696
  73.5 1.6 %collective-permute-start.25 = (f32[6,2,16,128]{3,2,1,0:T(8,128)S(1)}, f32[6,2,16,128]{3,2,1,0:T(8,128)S(1)}, u32[]{:S(2)}, u32[]{:S(2)}) collective-permute-start(f32[6,2,16,128]{3,2,1,0:T(8,128)S(1)} %get-tuple-element.99), channel_id=1, source_target_pairs={{0,8},{8,0},{16,24},{24,16},{1,9},{9,1},{17,25},{25,17},{2,10},{10... | collective-permute-start | bytes 294920 | tf_op jit(solution)/shard_map/ppermute | solution.py:114
  75.8 2.7 %collective-permute-start.23 = (f32[6,16,128]{2,1,0:T(8,128)S(1)}, f32[6,16,128]{2,1,0:T(8,128)S(1)}, u32[]{:S(2)}, u32[]{:S(2)}) collective-permute-start(f32[6,16,128]{2,1,0:T(8,128)S(1)} %get-tuple-element.97), channel_id=1, source_target_pairs={{0,1},{1,0},{2,3},{3,2},{4,5},{5,4},{6,7},{7,6},{8,9},{9,8},{10,11... | collective-permute-start | bytes 147464 | tf_op jit(solution)/shard_map/ppermute | solution.py:107
  78.5 1.8 %shard_map.100.refs_1_ = f32[4,3,8,2,16,128]{5,4,3,2,1,0:T(8,128)S(1)} custom-call(f32[4,14,2,16,128]{4,3,2,1,0:T(8,128)S(1)} %copy-done, f32[4,3,8,2,16,128]{5,4,3,2,1,0:T(8,128)S(1)} %get-tuple-element.96.refs_1_, f32[4,3,8,2,16,128]{5,4,3,2,1,0:T(8,128)S(1)} %get-tuple-element.75.refs_2_), custom_call_target="tpu_custom_call" | custom-call | flops 18000000 | bytes 1000000 | tf_op jit(solution)/shard_map/pallas_call | solution.py:33
  80.5 2.6 %collective-permute-done.24.refs_3_ = f32[6,16,128]{2,1,0:T(8,128)S(1)} collective-permute-done((f32[6,16,128]{2,1,0:T(8,128)S(1)}, f32[6,16,128]{2,1,0:T(8,128)S(1)}, u32[]{:S(2)}, u32[]{:S(2)}) %collective-permute-start.24) | collective-permute-done | bytes 49184 | tf_op jit(solution)/shard_map/ppermute | solution.py:108
  85.0 6.8 %collective-permute-done.27.refs_2_.refs_3_ = f32[4,3,2,16,128]{4,3,2,1,0:T(8,128)S(1)} collective-permute-done((f32[4,3,2,16,128]{4,3,2,1,0:T(8,128)S(1)}, f32[4,3,2,16,128]{4,3,2,1,0:T(8,128)S(1)}, u32[]{:S(2)}, u32[]{:S(2)}) %collective-permute-start.27) | collective-permute-done | bytes 196640 | tf_op jit(solution)/shard_map/ppermute | solution.py:696
  93.5 1.9 %shard_map.103.refs_1_ = f32[4,3,8,2,16,128]{5,4,3,2,1,0:T(8,128)S(1)} custom-call(f32[4,14,2,16,128]{4,3,2,1,0:T(8,128)S(1)} %copy-done, f32[4,3,8,2,16,128]{5,4,3,2,1,0:T(8,128)S(1)} %get-tuple-element.109.refs_1_.refs_2_, f32[4,3,8,2,16,128]{5,4,3,2,1,0:T(8,128)S(1)} %get-tuple-element.75.refs_2_, ...), custom_call_target="tpu_custom_call" | custom-call | flops 18000000 | bytes 1000000 | tf_op jit(solution)/shard_map/pallas_call | solution.py:33
  95.4 1.4 %shard_map.104 = (f32[8,3,4,4096]{3,2,1,0:T(4,128)}, f32[4,3,4,4096]{3,2,1,0:T(4,128)S(1)}) custom-call(f32[8,3,4,4096]{3,2,1,0:T(4,128)S(1)} %bitcast.8, f32[8,3,4,4096]{3,2,1,0:T(4,128)S(1)} %collective-permute-done.refs_1_, f32[4,3,8,2,16,128]{5,4,3,2,1,0:T(8,128)S(1)} %get-tuple-element.109.refs_1_.refs_2_), custom_call_target="tpu_custom_call" | custom-call | flops 6000000 | bytes 1000000 | tf_op jit(solution)/shard_map/pallas_call | solution.py:33
  96.8 3.6 %collective-permute-start.32 = (f32[4,3,4,4096]{3,2,1,0:T(4,128)S(1)}, f32[4,3,4,4096]{3,2,1,0:T(4,128)S(1)}, u32[]{:S(2)}, u32[]{:S(2)}) collective-permute-start(f32[4,3,4,4096]{3,2,1,0:T(4,128)S(1)} %get-tuple-element.110), channel_id=1, source_target_pairs={{0,8},{8,0},{16,24},{24,16},{1,9},{9,1},{17,25},{25,17},{2,10},{10... | collective-permute-start | bytes 2359304 | tf_op jit(solution)/shard_map/ppermute | solution.py:114
  102.3 2.1 %shard_map.105 = (f32[8,3,4,4096]{3,2,1,0:T(4,128)}, f32[8,3,4,4096]{3,2,1,0:T(4,128)}) custom-call(f32[4,14,2,16,128]{4,3,2,1,0:T(8,128)S(1)} %copy-done, f32[4,3,8,2,16,128]{5,4,3,2,1,0:T(8,128)S(1)} %shard_map.103.refs_1_, f32[6,16,128]{2,1,0:T(8,128)S(1)} %collective-permute-done.28.refs_2_, ...), custom_call_target="tpu_custom_call", output_to_operand_aliasing={{1}: (7, {})} | custom-call | flops 6000000 | bytes 1000000 | tf_op jit(solution)/shard_map/pallas_call | solution.py:33
  (76 shorter events, 31.9 us)
Async XLA Ops:
  1.2 10.9 %collective-permute-start.1 = (f32[8,3,4,4096]{3,2,1,0:T(4,128)}, f32[8,3,4,4096]{3,2,1,0:T(4,128)}, u32[]{:S(2)}, u32[]{:S(2)}) collective-permute-start(f32[8,3,4,4096]{3,2,1,0:T(4,128)} %bitcast.9), channel_id=1, source_target_pairs={{0,8},{8,0},{16,24},{24,16},{1,9},{9,1},{17,25},{25,17},{2,10},{10... | collective-permute-start | bytes 4718600 | tf_op jit(solution)/shard_map/ppermute | solution.py:114
  6.8 11.7 %collective-permute-start.2 = (f32[4,3,2,16,128]{4,3,2,1,0:T(8,128)S(1)}, f32[4,3,2,16,128]{4,3,2,1,0:T(8,128)S(1)}, u32[]{:S(2)}, u32[]{:S(2)}) collective-permute-start(f32[4,3,2,16,128]{4,3,2,1,0:T(8,128)S(1)} %get-tuple-element.66), channel_id=1, source_target_pairs={{0,16},{8,24},{16,0},{24,8},{1,17},{9,25},{17,1},{25,9},{2,18},{10... | collective-permute-start | bytes 589832 | tf_op jit(solution)/shard_map/ppermute | solution.py:690
  9.8 8.7 %collective-permute-start.5 = (f32[6,2,16,128]{3,2,1,0:T(8,128)S(1)}, f32[6,2,16,128]{3,2,1,0:T(8,128)S(1)}, u32[]{:S(2)}, u32[]{:S(2)}) collective-permute-start(f32[6,2,16,128]{3,2,1,0:T(8,128)S(1)} %get-tuple-element.70), channel_id=1, source_target_pairs={{0,8},{8,0},{16,24},{24,16},{1,9},{9,1},{17,25},{25,17},{2,10},{10... | collective-permute-start | bytes 294920 | tf_op jit(solution)/shard_map/ppermute | solution.py:114
  9.8 8.7 %collective-permute-start.6 = (f32[6,2,16,128]{3,2,1,0:T(8,128)S(1)}, f32[6,2,16,128]{3,2,1,0:T(8,128)S(1)}, u32[]{:S(2)}, u32[]{:S(2)}) collective-permute-start(f32[6,2,16,128]{3,2,1,0:T(8,128)S(1)} %get-tuple-element.71), channel_id=1, source_target_pairs={{8,12},{9,13},{10,14},{11,15},{12,8},{13,9},{14,10},{15,11},{24,28... | collective-permute-start | bytes 294920 | tf_op jit(solution)/shard_map/ppermute | solution.py:104
  10.5 8.0 %collective-permute-start.3 = (f32[6,16,128]{2,1,0:T(8,128)S(1)}, f32[6,16,128]{2,1,0:T(8,128)S(1)}, u32[]{:S(2)}, u32[]{:S(2)}) collective-permute-start(f32[6,16,128]{2,1,0:T(8,128)S(1)} %get-tuple-element.68), channel_id=1, source_target_pairs={{0,1},{1,0},{2,3},{3,2},{4,5},{5,4},{6,7},{7,6},{8,9},{9,8},{10,11... | collective-permute-start | bytes 147464 | tf_op jit(solution)/shard_map/ppermute | solution.py:107
  12.0 6.4 %collective-permute-start.4 = (f32[6,16,128]{2,1,0:T(8,128)S(1)}, f32[6,16,128]{2,1,0:T(8,128)S(1)}, u32[]{:S(2)}, u32[]{:S(2)}) collective-permute-start(f32[6,16,128]{2,1,0:T(8,128)S(1)} %get-tuple-element.69), channel_id=1, source_target_pairs={{0,2},{1,3},{2,0},{3,1},{4,6},{5,7},{6,4},{7,5},{8,10},{9,11},{10,... | collective-permute-start | bytes 147464 | tf_op jit(solution)/shard_map/ppermute | solution.py:108
  19.8 5.7 %collective-permute-start.7 = (f32[4,3,2,16,128]{4,3,2,1,0:T(8,128)S(1)}, f32[4,3,2,16,128]{4,3,2,1,0:T(8,128)S(1)}, u32[]{:S(2)}, u32[]{:S(2)}) collective-permute-start(f32[4,3,2,16,128]{4,3,2,1,0:T(8,128)S(1)} %get-tuple-element.73.refs_3_), channel_id=1, source_target_pairs={{0,16},{8,24},{16,0},{24,8},{1,17},{9,25},{17,1},{25,9},{2,18},{10... | collective-permute-start | bytes 589832 | tf_op jit(solution)/shard_map/ppermute | solution.py:696
  26.3 7.7 %collective-permute-start.10 = (f32[6,2,16,128]{3,2,1,0:T(8,128)S(1)}, f32[6,2,16,128]{3,2,1,0:T(8,128)S(1)}, u32[]{:S(2)}, u32[]{:S(2)}) collective-permute-start(f32[6,2,16,128]{3,2,1,0:T(8,128)S(1)} %get-tuple-element.78), channel_id=1, source_target_pairs={{0,8},{8,0},{16,24},{24,16},{1,9},{9,1},{17,25},{25,17},{2,10},{10... | collective-permute-start | bytes 294920 | tf_op jit(solution)/shard_map/ppermute | solution.py:114
  28.7 5.3 %collective-permute-start.11 = (f32[6,2,16,128]{3,2,1,0:T(8,128)S(1)}, f32[6,2,16,128]{3,2,1,0:T(8,128)S(1)}, u32[]{:S(2)}, u32[]{:S(2)}) collective-permute-start(f32[6,2,16,128]{3,2,1,0:T(8,128)S(1)} %get-tuple-element.79), channel_id=1, source_target_pairs={{8,12},{9,13},{10,14},{11,15},{12,8},{13,9},{14,10},{15,11},{24,28... | collective-permute-start | bytes 294920 | tf_op jit(solution)/shard_map/ppermute | solution.py:104
  35.3 6.4 %collective-permute-start.12 = (f32[4,3,2,16,128]{4,3,2,1,0:T(8,128)S(1)}, f32[4,3,2,16,128]{4,3,2,1,0:T(8,128)S(1)}, u32[]{:S(2)}, u32[]{:S(2)}) collective-permute-start(f32[4,3,2,16,128]{4,3,2,1,0:T(8,128)S(1)} %get-tuple-element.81.refs_3_), channel_id=1, source_target_pairs={{0,16},{8,24},{16,0},{24,8},{1,17},{9,25},{17,1},{25,9},{2,18},{10... | collective-permute-start | bytes 589832 | tf_op jit(solution)/shard_map/ppermute | solution.py:696
  42.5 7.8 %collective-permute-start.15 = (f32[6,2,16,128]{3,2,1,0:T(8,128)S(1)}, f32[6,2,16,128]{3,2,1,0:T(8,128)S(1)}, u32[]{:S(2)}, u32[]{:S(2)}) collective-permute-start(f32[6,2,16,128]{3,2,1,0:T(8,128)S(1)} %get-tuple-element.85), channel_id=1, source_target_pairs={{0,8},{8,0},{16,24},{24,16},{1,9},{9,1},{17,25},{25,17},{2,10},{10... | collective-permute-start | bytes 294920 | tf_op jit(solution)/shard_map/ppermute | solution.py:114
  43.9 6.5 %collective-permute-start.16 = (f32[6,2,16,128]{3,2,1,0:T(8,128)S(1)}, f32[6,2,16,128]{3,2,1,0:T(8,128)S(1)}, u32[]{:S(2)}, u32[]{:S(2)}) collective-permute-start(f32[6,2,16,128]{3,2,1,0:T(8,128)S(1)} %get-tuple-element.86), channel_id=1, source_target_pairs={{8,12},{9,13},{10,14},{11,15},{12,8},{13,9},{14,10},{15,11},{24,28... | collective-permute-start | bytes 294920 | tf_op jit(solution)/shard_map/ppermute | solution.py:104
  51.6 6.8 %collective-permute-start.17 = (f32[4,3,2,16,128]{4,3,2,1,0:T(8,128)S(1)}, f32[4,3,2,16,128]{4,3,2,1,0:T(8,128)S(1)}, u32[]{:S(2)}, u32[]{:S(2)}) collective-permute-start(f32[4,3,2,16,128]{4,3,2,1,0:T(8,128)S(1)} %get-tuple-element.88.refs_3_), channel_id=1, source_target_pairs={{0,16},{8,24},{16,0},{24,8},{1,17},{9,25},{17,1},{25,9},{2,18},{10... | collective-permute-start | bytes 589832 | tf_op jit(solution)/shard_map/ppermute | solution.py:696
  59.1 6.2 %collective-permute-start.20 = (f32[6,2,16,128]{3,2,1,0:T(8,128)S(1)}, f32[6,2,16,128]{3,2,1,0:T(8,128)S(1)}, u32[]{:S(2)}, u32[]{:S(2)}) collective-permute-start(f32[6,2,16,128]{3,2,1,0:T(8,128)S(1)} %get-tuple-element.92), channel_id=1, source_target_pairs={{0,8},{8,0},{16,24},{24,16},{1,9},{9,1},{17,25},{25,17},{2,10},{10... | collective-permute-start | bytes 294920 | tf_op jit(solution)/shard_map/ppermute | solution.py:114
  60.1 5.2 %collective-permute-start.21 = (f32[6,2,16,128]{3,2,1,0:T(8,128)S(1)}, f32[6,2,16,128]{3,2,1,0:T(8,128)S(1)}, u32[]{:S(2)}, u32[]{:S(2)}) collective-permute-start(f32[6,2,16,128]{3,2,1,0:T(8,128)S(1)} %get-tuple-element.93), channel_id=1, source_target_pairs={{8,12},{9,13},{10,14},{11,15},{12,8},{13,9},{14,10},{15,11},{24,28... | collective-permute-start | bytes 294920 | tf_op jit(solution)/shard_map/ppermute | solution.py:104
  66.6 6.2 %collective-permute-start.22 = (f32[4,3,2,16,128]{4,3,2,1,0:T(8,128)S(1)}, f32[4,3,2,16,128]{4,3,2,1,0:T(8,128)S(1)}, u32[]{:S(2)}, u32[]{:S(2)}) collective-permute-start(f32[4,3,2,16,128]{4,3,2,1,0:T(8,128)S(1)} %get-tuple-element.95.refs_3_), channel_id=1, source_target_pairs={{0,16},{8,24},{16,0},{24,8},{1,17},{9,25},{17,1},{25,9},{2,18},{10... | collective-permute-start | bytes 589832 | tf_op jit(solution)/shard_map/ppermute | solution.py:696
  73.5 9.6 %collective-permute-start.25 = (f32[6,2,16,128]{3,2,1,0:T(8,128)S(1)}, f32[6,2,16,128]{3,2,1,0:T(8,128)S(1)}, u32[]{:S(2)}, u32[]{:S(2)}) collective-permute-start(f32[6,2,16,128]{3,2,1,0:T(8,128)S(1)} %get-tuple-element.99), channel_id=1, source_target_pairs={{0,8},{8,0},{16,24},{24,16},{1,9},{9,1},{17,25},{25,17},{2,10},{10... | collective-permute-start | bytes 294920 | tf_op jit(solution)/shard_map/ppermute | solution.py:114
  75.1 8.1 %collective-permute-start.26 = (f32[6,2,16,128]{3,2,1,0:T(8,128)S(1)}, f32[6,2,16,128]{3,2,1,0:T(8,128)S(1)}, u32[]{:S(2)}, u32[]{:S(2)}) collective-permute-start(f32[6,2,16,128]{3,2,1,0:T(8,128)S(1)} %get-tuple-element.100), channel_id=1, source_target_pairs={{8,12},{9,13},{10,14},{11,15},{12,8},{13,9},{14,10},{15,11},{24,28... | collective-permute-start | bytes 294920 | tf_op jit(solution)/shard_map/ppermute | solution.py:104
  84.4 7.4 %collective-permute-start.27 = (f32[4,3,2,16,128]{4,3,2,1,0:T(8,128)S(1)}, f32[4,3,2,16,128]{4,3,2,1,0:T(8,128)S(1)}, u32[]{:S(2)}, u32[]{:S(2)}) collective-permute-start(f32[4,3,2,16,128]{4,3,2,1,0:T(8,128)S(1)} %get-tuple-element.102.refs_3_.refs_4_), channel_id=1, source_target_pairs={{0,16},{8,24},{16,0},{24,8},{1,17},{9,25},{17,1},{25,9},{2,18},{10... | collective-permute-start | bytes 589832 | tf_op jit(solution)/shard_map/ppermute | solution.py:696
  92.6 7.8 %collective-permute-start.30 = (f32[6,2,16,128]{3,2,1,0:T(8,128)S(1)}, f32[6,2,16,128]{3,2,1,0:T(8,128)S(1)}, u32[]{:S(2)}, u32[]{:S(2)}) collective-permute-start(f32[6,2,16,128]{3,2,1,0:T(8,128)S(1)} %get-tuple-element.107), channel_id=1, source_target_pairs={{0,8},{8,0},{16,24},{24,16},{1,9},{9,1},{17,25},{25,17},{2,10},{10... | collective-permute-start | bytes 294920 | tf_op jit(solution)/shard_map/ppermute | solution.py:114
  92.7 7.8 %collective-permute-start.31 = (f32[6,2,16,128]{3,2,1,0:T(8,128)S(1)}, f32[6,2,16,128]{3,2,1,0:T(8,128)S(1)}, u32[]{:S(2)}, u32[]{:S(2)}) collective-permute-start(f32[6,2,16,128]{3,2,1,0:T(8,128)S(1)} %get-tuple-element.108), channel_id=1, source_target_pairs={{8,12},{9,13},{10,14},{11,15},{12,8},{13,9},{14,10},{15,11},{24,28... | collective-permute-start | bytes 294920 | tf_op jit(solution)/shard_map/ppermute | solution.py:104
  93.3 7.1 %collective-permute-start.28 = (f32[6,16,128]{2,1,0:T(8,128)S(1)}, f32[6,16,128]{2,1,0:T(8,128)S(1)}, u32[]{:S(2)}, u32[]{:S(2)}) collective-permute-start(f32[6,16,128]{2,1,0:T(8,128)S(1)} %get-tuple-element.105), channel_id=1, source_target_pairs={{0,1},{1,0},{2,3},{3,2},{4,5},{5,4},{6,7},{7,6},{8,9},{9,8},{10,11... | collective-permute-start | bytes 147464 | tf_op jit(solution)/shard_map/ppermute | solution.py:107
  93.4 7.0 %collective-permute-start.29 = (f32[6,16,128]{2,1,0:T(8,128)S(1)}, f32[6,16,128]{2,1,0:T(8,128)S(1)}, u32[]{:S(2)}, u32[]{:S(2)}) collective-permute-start(f32[6,16,128]{2,1,0:T(8,128)S(1)} %get-tuple-element.106), channel_id=1, source_target_pairs={{0,2},{1,3},{2,0},{3,1},{4,6},{5,7},{6,4},{7,5},{8,10},{9,11},{10,... | collective-permute-start | bytes 147464 | tf_op jit(solution)/shard_map/ppermute | solution.py:108
  96.8 5.5 %collective-permute-start.32 = (f32[4,3,4,4096]{3,2,1,0:T(4,128)S(1)}, f32[4,3,4,4096]{3,2,1,0:T(4,128)S(1)}, u32[]{:S(2)}, u32[]{:S(2)}) collective-permute-start(f32[4,3,4,4096]{3,2,1,0:T(4,128)S(1)} %get-tuple-element.110), channel_id=1, source_target_pairs={{0,8},{8,0},{16,24},{24,16},{1,9},{9,1},{17,25},{25,17},{2,10},{10... | collective-permute-start | bytes 2359304 | tf_op jit(solution)/shard_map/ppermute | solution.py:114
  (15 other events, 70.6 us)

commit v6 on v5

--- a/solution.py
+++ b/solution.py
@@ -398,10 +398,15 @@
     pack_faces(sh, lambda j, c, l, h: field[j, c, l, h], field, rest[:-1])
 
 
-def residual_inner_kernel(sh, coef, field, whole, other, inner, force, rows):
+def residual_inner_kernel(sh, coef, field, whole, other, inner, own_rows, other_rows, force, rows, sems):
     core = sh.core()
-    unpack_half(sh, 0, whole, force, core * sh.local, rows)
-    unpack_half(sh, 1, other, force, (1 - core) * sh.local, rows)
+    mine = pl.ds(sh.upper() * sh.half, sh.half)
+    copies = [
+        pltpu.make_async_copy(source.at[mine], near, sems.at[i])
+        for i, (source, near) in enumerate(((whole, own_rows), (other, other_rows)))
+    ]
+    for copy in copies:
+        copy.start()
 
     def visit(j, comp):
         prior = None
@@ -409,12 +414,22 @@
             total = inner_sum(coef, field, j, comp, l)
             now = [field[j, comp, l, h] for h in range(2)]
             for h in range(2):
-                q = coef[j, Q, h]
-                value = total[h] + (0.5 * q) * force[j, comp, l, h] - now[h]
-                inner[j, comp, l, h] = value if prior is None else value + q * prior[h]
+                value = total[h] - now[h]
+                inner[j, comp, l, h] = value if prior is None else value + coef[j, Q, h] * prior[h]
             prior = now
 
     over_tiles(sh, visit)
+    for copy in copies:
+        copy.wait()
+    unpack_half(sh, 0, own_rows, force, core * sh.local, rows, 0)
+    unpack_half(sh, 1, other_rows, force, (1 - core) * sh.local, rows, 0)
+
+    def add(j, comp):
+        for l in range(sh.span):
+            for h in range(2):
+                inner[j, comp, l, h] += (0.5 * coef[j, Q, h]) * force[j, comp, l, h]
+
+    over_tiles(sh, add)
 
 
 def residual_outer_kernel(sh, coef, inner, before, first, *rest):
@@ -699,12 +714,14 @@
 
     scaleds, partials, ends = [], [], []
     for sh, field, before, face in zip(shapes, fields, befores, faces):
-        inner, _ = call(
+        (inner,) = call(
             bind(residual_inner_kernel, sh),
             [coef, field, force, force_other],
-            [sh.field, sh.field],
-            [rows],
+            [sh.field],
+            [pltpu.VMEM(native, F32)] * 2
+            + [pltpu.VMEM(sh.field, F32), rows, pltpu.SemaphoreType.DMA((2,))],
             flops=sh.comps * WORK,
+            far=(2, 3),
         )
         scaled, partial, last = call(
             bind(residual_outer_kernel, sh),

time: 106 us -> 104 us (0.981)
  starting transfers between devices: 30.5 us -> 38.4 us
  waiting for transfers between devices: 38.5 us -> 31.7 us
  Pallas kernels: 34.3 us -> 31.9 us
    ppermute x5, waiting for transfers between devices: 29.4 us -> 24.6 us  [chip_ends(): lax.ppermute(last, 'tm', [(a, (a + 2 * back) % n_time) for a in range(n_t...]
    ppermute x6, starting transfers between devices: 2.94 us -> 6.59 us  [exchange(): y_in = lax.ppermute(y_out, axes, pairs(sh.bits[1][0], sh.bits[1], False))]
    ppermute x5, starting transfers between devices: 2.98 us -> 6.45 us  [chip_ends(): lax.ppermute(last, 'tm', [(a, (a + 2 * back) % n_time) for a in range(n_t...]
    pallas_call x22, Pallas kernels: 34.3 us -> 31.9 us  [call(): pl.pallas_call(kernel, in_specs=[hbm if i in far else vmem for i in range...]
    ppermute x10, starting transfers between devices: 10.6 us -> 12.4 us  [swap_cores(): return lax.ppermute(value, 'tm', [(t, t ^ 1) for t in range(n_time)])]
    ppermute x6, waiting for transfers between devices: 5.14 us -> 3.93 us  [exchange(): y_in = lax.ppermute(y_out, axes, pairs(sh.bits[1][0], sh.bits[1], False))]
  transfers between devices with their start and end apart: 34 -> 34, of which waited for: 14 -> 13; matrix products, arithmetic and copies ran while one was open for 0% -> 0% of each run, Pallas kernels for 22% -> 20%
where the time goes in v6:
time: 104 us
  starting transfers between devices  38.4 us (37%)
  Pallas kernels  31.9 us (31%)
  waiting for transfers between devices  31.7 us (30%)
  local copies, waits for them, and re-layouts  1.22 us (1%)
    pallas_call x22, Pallas kernels, call(): pl.pallas_call(kernel, in_specs=[hbm if i in far else vmem for i in range...  31.9 us
    ppermute x5, waiting for transfers between devices, chip_ends(): lax.ppermute(last, 'tm', [(a, (a + 2 * back) % n_time) for a in range(n_t...  24.6 us
    ppermute x10, starting transfers between devices, swap_cores(): return lax.ppermute(value, 'tm', [(t, t ^ 1) for t in range(n_time)])  12.4 us
    ppermute x6, starting transfers between devices, exchange(): y_in = lax.ppermute(y_out, axes, pairs(sh.bits[1][0], sh.bits[1], False))  6.59 us
    ppermute x5, starting transfers between devices, chip_ends(): lax.ppermute(last, 'tm', [(a, (a + 2 * back) % n_time) for a in range(n_t...  6.45 us
    ppermute x6, starting transfers between devices, exchange(): x_in.append(lax.ppermute(x_out[i], axes, pairs(bit, sh.bits[0], False)))  6.11 us
    ppermute x6, waiting for transfers between devices, exchange(): y_in = lax.ppermute(y_out, axes, pairs(sh.bits[1][0], sh.bits[1], False))  3.93 us
    ppermute x6, starting transfers between devices, exchange(): z_in = lax.ppermute(z_out, axes, pairs(sh.bits[2][0], sh.bits[2], True))  3.93 us
  transfers between devices with their start and end apart: 34, of which 13 were waited for; matrix products, arithmetic and copies ran while one was open for 0% of the time, Pallas kernels for 20%

profile of v6, /device:TPU:0, one launch (start us, length us, event | category | flops | bytes accessed | tf_op | source)
XLA Modules:
  0.0 104.2 jit_solution(11850509042923395623)
XLA Ops:
  1.3 3.3 %shard_map.86 = (f32[4,14,2,16,128]{4,3,2,1,0:T(8,128)}, f32[4,3,2,16,128]{4,3,2,1,0:T(8,128)}, f32[4,3,4,2,16,128]{5,4,3,2,1,0:T(8,128)}) custom-call(s32[8,6]{1,0:T(8,128)} %refs_0_.1, s32[8]{0:T(128)} %refs_1_.1, f32[8,4096]{1,0:T(8,128)} %refs_2_.1, f32[3,8,4096]{2,1,0:T(8,128)} %bitcast.13, f32[3,8,4096]{2,1,0:T(8,128)} %bitcast.14, ...), custom_call_target="tpu_custom_call" | custom-call | flops 6000000 | bytes 1000000 | tf_op jit(solution)/shard_map/pallas_call | solution.py:33
  6.8 3.0 %collective-permute-start.2 = (f32[4,3,2,16,128]{4,3,2,1,0:T(8,128)S(1)}, f32[4,3,2,16,128]{4,3,2,1,0:T(8,128)S(1)}, u32[]{:S(2)}, u32[]{:S(2)}) collective-permute-start(f32[4,3,2,16,128]{4,3,2,1,0:T(8,128)S(1)} %get-tuple-element.64), channel_id=1, source_target_pairs={{0,16},{8,24},{16,0},{24,8},{1,17},{9,25},{17,1},{25,9},{2,18},{10... | collective-permute-start | bytes 589832 | tf_op jit(solution)/shard_map/ppermute | solution.py:705
  10.5 1.6 %collective-permute-start.3 = (f32[6,16,128]{2,1,0:T(8,128)S(1)}, f32[6,16,128]{2,1,0:T(8,128)S(1)}, u32[]{:S(2)}, u32[]{:S(2)}) collective-permute-start(f32[6,16,128]{2,1,0:T(8,128)S(1)} %get-tuple-element.66), channel_id=1, source_target_pairs={{0,1},{1,0},{2,3},{3,2},{4,5},{5,4},{6,7},{7,6},{8,9},{9,8},{10,11... | collective-permute-start | bytes 147464 | tf_op jit(solution)/shard_map/ppermute | solution.py:107
  12.0 1.6 %collective-permute-start.4 = (f32[6,16,128]{2,1,0:T(8,128)S(1)}, f32[6,16,128]{2,1,0:T(8,128)S(1)}, u32[]{:S(2)}, u32[]{:S(2)}) collective-permute-start(f32[6,16,128]{2,1,0:T(8,128)S(1)} %get-tuple-element.67), channel_id=1, source_target_pairs={{0,2},{1,3},{2,0},{3,1},{4,6},{5,7},{6,4},{7,5},{8,10},{9,11},{10,... | collective-permute-start | bytes 147464 | tf_op jit(solution)/shard_map/ppermute | solution.py:108
  13.6 2.5 %shard_map.88.refs_1_ = f32[4,3,8,2,16,128]{5,4,3,2,1,0:T(8,128)S(1)} custom-call(f32[4,14,2,16,128]{4,3,2,1,0:T(8,128)S(1)} %copy-done, f32[4,3,8,2,16,128]{5,4,3,2,1,0:T(8,128)S(1)} %get-tuple-element.63.refs_1_, f32[8,3,4,4096]{3,2,1,0:T(4,128)S(1)} %bitcast.10, f32[8,3,4,4096]{3,2,1,0:T(4,128)} %collective-permute-done.1.refs_3_), custom_call_target="tpu_custom_call" | custom-call | flops 18000000 | bytes 1000000 | tf_op jit(solution)/shard_map/pallas_call | solution.py:33
  19.1 5.7 %collective-permute-done.7.refs_2_ = f32[4,3,2,16,128]{4,3,2,1,0:T(8,128)S(1)} collective-permute-done((f32[4,3,2,16,128]{4,3,2,1,0:T(8,128)S(1)}, f32[4,3,2,16,128]{4,3,2,1,0:T(8,128)S(1)}, u32[]{:S(2)}, u32[]{:S(2)}) %collective-permute-start.7) | collective-permute-done | bytes 196640 | tf_op jit(solution)/shard_map/ppermute | solution.py:711
  28.8 1.8 %shard_map.91.refs_1_ = f32[4,3,8,2,16,128]{5,4,3,2,1,0:T(8,128)S(1)} custom-call(f32[4,14,2,16,128]{4,3,2,1,0:T(8,128)S(1)} %copy-done, f32[4,3,8,2,16,128]{5,4,3,2,1,0:T(8,128)S(1)} %get-tuple-element.72.refs_1_, f32[4,3,8,2,16,128]{5,4,3,2,1,0:T(8,128)S(1)} %get-tuple-element.73.refs_2_), custom_call_target="tpu_custom_call" | custom-call | flops 18000000 | bytes 1000000 | tf_op jit(solution)/shard_map/pallas_call | solution.py:33
  34.2 5.1 %collective-permute-done.12.refs_2_ = f32[4,3,2,16,128]{4,3,2,1,0:T(8,128)S(1)} collective-permute-done((f32[4,3,2,16,128]{4,3,2,1,0:T(8,128)S(1)}, f32[4,3,2,16,128]{4,3,2,1,0:T(8,128)S(1)}, u32[]{:S(2)}, u32[]{:S(2)}) %collective-permute-start.12) | collective-permute-done | bytes 196640 | tf_op jit(solution)/shard_map/ppermute | solution.py:711
  40.1 1.6 %collective-permute-start.15 = (f32[6,2,16,128]{3,2,1,0:T(8,128)S(1)}, f32[6,2,16,128]{3,2,1,0:T(8,128)S(1)}, u32[]{:S(2)}, u32[]{:S(2)}) collective-permute-start(f32[6,2,16,128]{3,2,1,0:T(8,128)S(1)} %get-tuple-element.83), channel_id=1, source_target_pairs={{0,8},{8,0},{16,24},{24,16},{1,9},{9,1},{17,25},{25,17},{2,10},{10... | collective-permute-start | bytes 294920 | tf_op jit(solution)/shard_map/ppermute | solution.py:114
  42.4 2.0 %collective-permute-start.13 = (f32[6,16,128]{2,1,0:T(8,128)S(1)}, f32[6,16,128]{2,1,0:T(8,128)S(1)}, u32[]{:S(2)}, u32[]{:S(2)}) collective-permute-start(f32[6,16,128]{2,1,0:T(8,128)S(1)} %get-tuple-element.81), channel_id=1, source_target_pairs={{0,1},{1,0},{2,3},{3,2},{4,5},{5,4},{6,7},{7,6},{8,9},{9,8},{10,11... | collective-permute-start | bytes 147464 | tf_op jit(solution)/shard_map/ppermute | solution.py:107
  45.4 1.8 %shard_map.94.refs_1_ = f32[4,3,8,2,16,128]{5,4,3,2,1,0:T(8,128)S(1)} custom-call(f32[4,14,2,16,128]{4,3,2,1,0:T(8,128)S(1)} %copy-done, f32[4,3,8,2,16,128]{5,4,3,2,1,0:T(8,128)S(1)} %get-tuple-element.80.refs_1_, f32[4,3,8,2,16,128]{5,4,3,2,1,0:T(8,128)S(1)} %get-tuple-element.73.refs_2_), custom_call_target="tpu_custom_call" | custom-call | flops 18000000 | bytes 1000000 | tf_op jit(solution)/shard_map/pallas_call | solution.py:33
  49.8 1.5 %collective-permute-start.17 = (f32[4,3,2,16,128]{4,3,2,1,0:T(8,128)S(1)}, f32[4,3,2,16,128]{4,3,2,1,0:T(8,128)S(1)}, u32[]{:S(2)}, u32[]{:S(2)}) collective-permute-start(f32[4,3,2,16,128]{4,3,2,1,0:T(8,128)S(1)} %get-tuple-element.86.refs_3_), channel_id=1, source_target_pairs={{0,16},{8,24},{16,0},{24,8},{1,17},{9,25},{17,1},{25,9},{2,18},{10... | collective-permute-start | bytes 589832 | tf_op jit(solution)/shard_map/ppermute | solution.py:711
  51.2 5.2 %collective-permute-done.17.refs_2_ = f32[4,3,2,16,128]{4,3,2,1,0:T(8,128)S(1)} collective-permute-done((f32[4,3,2,16,128]{4,3,2,1,0:T(8,128)S(1)}, f32[4,3,2,16,128]{4,3,2,1,0:T(8,128)S(1)}, u32[]{:S(2)}, u32[]{:S(2)}) %collective-permute-start.17) | collective-permute-done | bytes 196640 | tf_op jit(solution)/shard_map/ppermute | solution.py:711
  60.1 1.8 %shard_map.97.refs_1_ = f32[4,3,8,2,16,128]{5,4,3,2,1,0:T(8,128)S(1)} custom-call(f32[4,14,2,16,128]{4,3,2,1,0:T(8,128)S(1)} %copy-done, f32[4,3,8,2,16,128]{5,4,3,2,1,0:T(8,128)S(1)} %get-tuple-element.87.refs_1_, f32[4,3,8,2,16,128]{5,4,3,2,1,0:T(8,128)S(1)} %get-tuple-element.73.refs_2_), custom_call_target="tpu_custom_call" | custom-call | flops 18000000 | bytes 1000000 | tf_op jit(solution)/shard_map/pallas_call | solution.py:33
  65.9 4.5 %collective-permute-done.22.refs_2_ = f32[4,3,2,16,128]{4,3,2,1,0:T(8,128)S(1)} collective-permute-done((f32[4,3,2,16,128]{4,3,2,1,0:T(8,128)S(1)}, f32[4,3,2,16,128]{4,3,2,1,0:T(8,128)S(1)}, u32[]{:S(2)}, u32[]{:S(2)}) %collective-permute-start.22) | collective-permute-done | bytes 196640 | tf_op jit(solution)/shard_map/ppermute | solution.py:711
  71.2 1.9 %collective-permute-start.25 = (f32[6,2,16,128]{3,2,1,0:T(8,128)S(1)}, f32[6,2,16,128]{3,2,1,0:T(8,128)S(1)}, u32[]{:S(2)}, u32[]{:S(2)}) collective-permute-start(f32[6,2,16,128]{3,2,1,0:T(8,128)S(1)} %get-tuple-element.97), channel_id=1, source_target_pairs={{0,8},{8,0},{16,24},{24,16},{1,9},{9,1},{17,25},{25,17},{2,10},{10... | collective-permute-start | bytes 294920 | tf_op jit(solution)/shard_map/ppermute | solution.py:114
  73.8 1.9 %collective-permute-start.23 = (f32[6,16,128]{2,1,0:T(8,128)S(1)}, f32[6,16,128]{2,1,0:T(8,128)S(1)}, u32[]{:S(2)}, u32[]{:S(2)}) collective-permute-start(f32[6,16,128]{2,1,0:T(8,128)S(1)} %get-tuple-element.95), channel_id=1, source_target_pairs={{0,1},{1,0},{2,3},{3,2},{4,5},{5,4},{6,7},{7,6},{8,9},{9,8},{10,11... | collective-permute-start | bytes 147464 | tf_op jit(solution)/shard_map/ppermute | solution.py:107
  76.6 1.8 %shard_map.100.refs_1_ = f32[4,3,8,2,16,128]{5,4,3,2,1,0:T(8,128)S(1)} custom-call(f32[4,14,2,16,128]{4,3,2,1,0:T(8,128)S(1)} %copy-done, f32[4,3,8,2,16,128]{5,4,3,2,1,0:T(8,128)S(1)} %get-tuple-element.94.refs_1_, f32[4,3,8,2,16,128]{5,4,3,2,1,0:T(8,128)S(1)} %get-tuple-element.73.refs_2_), custom_call_target="tpu_custom_call" | custom-call | flops 18000000 | bytes 1000000 | tf_op jit(solution)/shard_map/pallas_call | solution.py:33
  81.1 2.0 %collective-permute-start.27 = (f32[4,3,2,16,128]{4,3,2,1,0:T(8,128)S(1)}, f32[4,3,2,16,128]{4,3,2,1,0:T(8,128)S(1)}, u32[]{:S(2)}, u32[]{:S(2)}) collective-permute-start(f32[4,3,2,16,128]{4,3,2,1,0:T(8,128)S(1)} %get-tuple-element.100.refs_3_.refs_4_), channel_id=1, source_target_pairs={{0,16},{8,24},{16,0},{24,8},{1,17},{9,25},{17,1},{25,9},{2,18},{10... | collective-permute-start | bytes 589832 | tf_op jit(solution)/shard_map/ppermute | solution.py:711
  83.1 4.1 %collective-permute-done.27.refs_2_.refs_3_ = f32[4,3,2,16,128]{4,3,2,1,0:T(8,128)S(1)} collective-permute-done((f32[4,3,2,16,128]{4,3,2,1,0:T(8,128)S(1)}, f32[4,3,2,16,128]{4,3,2,1,0:T(8,128)S(1)}, u32[]{:S(2)}, u32[]{:S(2)}) %collective-permute-start.27) | collective-permute-done | bytes 196640 | tf_op jit(solution)/shard_map/ppermute | solution.py:711
  88.0 1.6 %collective-permute-start.30 = (f32[6,2,16,128]{3,2,1,0:T(8,128)S(1)}, f32[6,2,16,128]{3,2,1,0:T(8,128)S(1)}, u32[]{:S(2)}, u32[]{:S(2)}) collective-permute-start(f32[6,2,16,128]{3,2,1,0:T(8,128)S(1)} %get-tuple-element.105), channel_id=1, source_target_pairs={{0,8},{8,0},{16,24},{24,16},{1,9},{9,1},{17,25},{25,17},{2,10},{10... | collective-permute-start | bytes 294920 | tf_op jit(solution)/shard_map/ppermute | solution.py:114
  91.7 1.8 %shard_map.103.refs_1_ = f32[4,3,8,2,16,128]{5,4,3,2,1,0:T(8,128)S(1)} custom-call(f32[4,14,2,16,128]{4,3,2,1,0:T(8,128)S(1)} %copy-done, f32[4,3,8,2,16,128]{5,4,3,2,1,0:T(8,128)S(1)} %get-tuple-element.107.refs_1_.refs_2_, f32[4,3,8,2,16,128]{5,4,3,2,1,0:T(8,128)S(1)} %get-tuple-element.73.refs_2_, ...), custom_call_target="tpu_custom_call" | custom-call | flops 18000000 | bytes 1000000 | tf_op jit(solution)/shard_map/pallas_call | solution.py:33
  94.9 4.2 %collective-permute-start.32 = (f32[4,3,4,4096]{3,2,1,0:T(4,128)S(1)}, f32[4,3,4,4096]{3,2,1,0:T(4,128)S(1)}, u32[]{:S(2)}, u32[]{:S(2)}) collective-permute-start(f32[4,3,4,4096]{3,2,1,0:T(4,128)S(1)} %get-tuple-element.108), channel_id=1, source_target_pairs={{0,8},{8,0},{16,24},{24,16},{1,9},{9,1},{17,25},{25,17},{2,10},{10... | collective-permute-start | bytes 2359304 | tf_op jit(solution)/shard_map/ppermute | solution.py:114
  101.1 2.1 %shard_map.105 = (f32[8,3,4,4096]{3,2,1,0:T(4,128)}, f32[8,3,4,4096]{3,2,1,0:T(4,128)}) custom-call(f32[4,14,2,16,128]{4,3,2,1,0:T(8,128)S(1)} %copy-done, f32[4,3,8,2,16,128]{5,4,3,2,1,0:T(8,128)S(1)} %shard_map.103.refs_1_, f32[6,16,128]{2,1,0:T(8,128)S(1)} %collective-permute-done.28.refs_2_, ...), custom_call_target="tpu_custom_call", output_to_operand_aliasing={{1}: (7, {})} | custom-call | flops 6000000 | bytes 1000000 | tf_op jit(solution)/shard_map/pallas_call | solution.py:33
  (76 shorter events, 38.7 us)
Async XLA Ops:
  1.2 10.9 %collective-permute-start.1 = (f32[8,3,4,4096]{3,2,1,0:T(4,128)}, f32[8,3,4,4096]{3,2,1,0:T(4,128)}, u32[]{:S(2)}, u32[]{:S(2)}) collective-permute-start(f32[8,3,4,4096]{3,2,1,0:T(4,128)} %bitcast.9), channel_id=1, source_target_pairs={{0,8},{8,0},{16,24},{24,16},{1,9},{9,1},{17,25},{25,17},{2,10},{10... | collective-permute-start | bytes 4718600 | tf_op jit(solution)/shard_map/ppermute | solution.py:114
  6.8 10.4 %collective-permute-start.2 = (f32[4,3,2,16,128]{4,3,2,1,0:T(8,128)S(1)}, f32[4,3,2,16,128]{4,3,2,1,0:T(8,128)S(1)}, u32[]{:S(2)}, u32[]{:S(2)}) collective-permute-start(f32[4,3,2,16,128]{4,3,2,1,0:T(8,128)S(1)} %get-tuple-element.64), channel_id=1, source_target_pairs={{0,16},{8,24},{16,0},{24,8},{1,17},{9,25},{17,1},{25,9},{2,18},{10... | collective-permute-start | bytes 589832 | tf_op jit(solution)/shard_map/ppermute | solution.py:705
  9.8 7.4 %collective-permute-start.5 = (f32[6,2,16,128]{3,2,1,0:T(8,128)S(1)}, f32[6,2,16,128]{3,2,1,0:T(8,128)S(1)}, u32[]{:S(2)}, u32[]{:S(2)}) collective-permute-start(f32[6,2,16,128]{3,2,1,0:T(8,128)S(1)} %get-tuple-element.68), channel_id=1, source_target_pairs={{0,8},{8,0},{16,24},{24,16},{1,9},{9,1},{17,25},{25,17},{2,10},{10... | collective-permute-start | bytes 294920 | tf_op jit(solution)/shard_map/ppermute | solution.py:114
  9.8 7.4 %collective-permute-start.6 = (f32[6,2,16,128]{3,2,1,0:T(8,128)S(1)}, f32[6,2,16,128]{3,2,1,0:T(8,128)S(1)}, u32[]{:S(2)}, u32[]{:S(2)}) collective-permute-start(f32[6,2,16,128]{3,2,1,0:T(8,128)S(1)} %get-tuple-element.69), channel_id=1, source_target_pairs={{8,12},{9,13},{10,14},{11,15},{12,8},{13,9},{14,10},{15,11},{24,28... | collective-permute-start | bytes 294920 | tf_op jit(solution)/shard_map/ppermute | solution.py:104
  10.5 5.7 %collective-permute-start.3 = (f32[6,16,128]{2,1,0:T(8,128)S(1)}, f32[6,16,128]{2,1,0:T(8,128)S(1)}, u32[]{:S(2)}, u32[]{:S(2)}) collective-permute-start(f32[6,16,128]{2,1,0:T(8,128)S(1)} %get-tuple-element.66), channel_id=1, source_target_pairs={{0,1},{1,0},{2,3},{3,2},{4,5},{5,4},{6,7},{7,6},{8,9},{9,8},{10,11... | collective-permute-start | bytes 147464 | tf_op jit(solution)/shard_map/ppermute | solution.py:107
  12.0 5.1 %collective-permute-start.4 = (f32[6,16,128]{2,1,0:T(8,128)S(1)}, f32[6,16,128]{2,1,0:T(8,128)S(1)}, u32[]{:S(2)}, u32[]{:S(2)}) collective-permute-start(f32[6,16,128]{2,1,0:T(8,128)S(1)} %get-tuple-element.67), channel_id=1, source_target_pairs={{0,2},{1,3},{2,0},{3,1},{4,6},{5,7},{6,4},{7,5},{8,10},{9,11},{10,... | collective-permute-start | bytes 147464 | tf_op jit(solution)/shard_map/ppermute | solution.py:108
  18.5 6.3 %collective-permute-start.7 = (f32[4,3,2,16,128]{4,3,2,1,0:T(8,128)S(1)}, f32[4,3,2,16,128]{4,3,2,1,0:T(8,128)S(1)}, u32[]{:S(2)}, u32[]{:S(2)}) collective-permute-start(f32[4,3,2,16,128]{4,3,2,1,0:T(8,128)S(1)} %get-tuple-element.71.refs_3_), channel_id=1, source_target_pairs={{0,16},{8,24},{16,0},{24,8},{1,17},{9,25},{17,1},{25,9},{2,18},{10... | collective-permute-start | bytes 589832 | tf_op jit(solution)/shard_map/ppermute | solution.py:711
  25.6 6.3 %collective-permute-start.10 = (f32[6,2,16,128]{3,2,1,0:T(8,128)S(1)}, f32[6,2,16,128]{3,2,1,0:T(8,128)S(1)}, u32[]{:S(2)}, u32[]{:S(2)}) collective-permute-start(f32[6,2,16,128]{3,2,1,0:T(8,128)S(1)} %get-tuple-element.76), channel_id=1, source_target_pairs={{0,8},{8,0},{16,24},{24,16},{1,9},{9,1},{17,25},{25,17},{2,10},{10... | collective-permute-start | bytes 294920 | tf_op jit(solution)/shard_map/ppermute | solution.py:114
  27.0 4.9 %collective-permute-start.11 = (f32[6,2,16,128]{3,2,1,0:T(8,128)S(1)}, f32[6,2,16,128]{3,2,1,0:T(8,128)S(1)}, u32[]{:S(2)}, u32[]{:S(2)}) collective-permute-start(f32[6,2,16,128]{3,2,1,0:T(8,128)S(1)} %get-tuple-element.77), channel_id=1, source_target_pairs={{8,12},{9,13},{10,14},{11,15},{12,8},{13,9},{14,10},{15,11},{24,28... | collective-permute-start | bytes 294920 | tf_op jit(solution)/shard_map/ppermute | solution.py:104
  33.2 6.1 %collective-permute-start.12 = (f32[4,3,2,16,128]{4,3,2,1,0:T(8,128)S(1)}, f32[4,3,2,16,128]{4,3,2,1,0:T(8,128)S(1)}, u32[]{:S(2)}, u32[]{:S(2)}) collective-permute-start(f32[4,3,2,16,128]{4,3,2,1,0:T(8,128)S(1)} %get-tuple-element.79.refs_3_), channel_id=1, source_target_pairs={{0,16},{8,24},{16,0},{24,8},{1,17},{9,25},{17,1},{25,9},{2,18},{10... | collective-permute-start | bytes 589832 | tf_op jit(solution)/shard_map/ppermute | solution.py:711
  40.1 8.4 %collective-permute-start.15 = (f32[6,2,16,128]{3,2,1,0:T(8,128)S(1)}, f32[6,2,16,128]{3,2,1,0:T(8,128)S(1)}, u32[]{:S(2)}, u32[]{:S(2)}) collective-permute-start(f32[6,2,16,128]{3,2,1,0:T(8,128)S(1)} %get-tuple-element.83), channel_id=1, source_target_pairs={{0,8},{8,0},{16,24},{24,16},{1,9},{9,1},{17,25},{25,17},{2,10},{10... | collective-permute-start | bytes 294920 | tf_op jit(solution)/shard_map/ppermute | solution.py:114
  41.7 6.8 %collective-permute-start.16 = (f32[6,2,16,128]{3,2,1,0:T(8,128)S(1)}, f32[6,2,16,128]{3,2,1,0:T(8,128)S(1)}, u32[]{:S(2)}, u32[]{:S(2)}) collective-permute-start(f32[6,2,16,128]{3,2,1,0:T(8,128)S(1)} %get-tuple-element.84), channel_id=1, source_target_pairs={{8,12},{9,13},{10,14},{11,15},{12,8},{13,9},{14,10},{15,11},{24,28... | collective-permute-start | bytes 294920 | tf_op jit(solution)/shard_map/ppermute | solution.py:104
  49.8 6.7 %collective-permute-start.17 = (f32[4,3,2,16,128]{4,3,2,1,0:T(8,128)S(1)}, f32[4,3,2,16,128]{4,3,2,1,0:T(8,128)S(1)}, u32[]{:S(2)}, u32[]{:S(2)}) collective-permute-start(f32[4,3,2,16,128]{4,3,2,1,0:T(8,128)S(1)} %get-tuple-element.86.refs_3_), channel_id=1, source_target_pairs={{0,16},{8,24},{16,0},{24,8},{1,17},{9,25},{17,1},{25,9},{2,18},{10... | collective-permute-start | bytes 589832 | tf_op jit(solution)/shard_map/ppermute | solution.py:711
  57.3 6.0 %collective-permute-start.20 = (f32[6,2,16,128]{3,2,1,0:T(8,128)S(1)}, f32[6,2,16,128]{3,2,1,0:T(8,128)S(1)}, u32[]{:S(2)}, u32[]{:S(2)}) collective-permute-start(f32[6,2,16,128]{3,2,1,0:T(8,128)S(1)} %get-tuple-element.90), channel_id=1, source_target_pairs={{0,8},{8,0},{16,24},{24,16},{1,9},{9,1},{17,25},{25,17},{2,10},{10... | collective-permute-start | bytes 294920 | tf_op jit(solution)/shard_map/ppermute | solution.py:114
  58.3 5.0 %collective-permute-start.21 = (f32[6,2,16,128]{3,2,1,0:T(8,128)S(1)}, f32[6,2,16,128]{3,2,1,0:T(8,128)S(1)}, u32[]{:S(2)}, u32[]{:S(2)}) collective-permute-start(f32[6,2,16,128]{3,2,1,0:T(8,128)S(1)} %get-tuple-element.91), channel_id=1, source_target_pairs={{8,12},{9,13},{10,14},{11,15},{12,8},{13,9},{14,10},{15,11},{24,28... | collective-permute-start | bytes 294920 | tf_op jit(solution)/shard_map/ppermute | solution.py:104
  64.6 5.8 %collective-permute-start.22 = (f32[4,3,2,16,128]{4,3,2,1,0:T(8,128)S(1)}, f32[4,3,2,16,128]{4,3,2,1,0:T(8,128)S(1)}, u32[]{:S(2)}, u32[]{:S(2)}) collective-permute-start(f32[4,3,2,16,128]{4,3,2,1,0:T(8,128)S(1)} %get-tuple-element.93.refs_3_), channel_id=1, source_target_pairs={{0,16},{8,24},{16,0},{24,8},{1,17},{9,25},{17,1},{25,9},{2,18},{10... | collective-permute-start | bytes 589832 | tf_op jit(solution)/shard_map/ppermute | solution.py:711
  71.2 8.6 %collective-permute-start.25 = (f32[6,2,16,128]{3,2,1,0:T(8,128)S(1)}, f32[6,2,16,128]{3,2,1,0:T(8,128)S(1)}, u32[]{:S(2)}, u32[]{:S(2)}) collective-permute-start(f32[6,2,16,128]{3,2,1,0:T(8,128)S(1)} %get-tuple-element.97), channel_id=1, source_target_pairs={{0,8},{8,0},{16,24},{24,16},{1,9},{9,1},{17,25},{25,17},{2,10},{10... | collective-permute-start | bytes 294920 | tf_op jit(solution)/shard_map/ppermute | solution.py:114
  73.1 6.7 %collective-permute-start.26 = (f32[6,2,16,128]{3,2,1,0:T(8,128)S(1)}, f32[6,2,16,128]{3,2,1,0:T(8,128)S(1)}, u32[]{:S(2)}, u32[]{:S(2)}) collective-permute-start(f32[6,2,16,128]{3,2,1,0:T(8,128)S(1)} %get-tuple-element.98), channel_id=1, source_target_pairs={{8,12},{9,13},{10,14},{11,15},{12,8},{13,9},{14,10},{15,11},{24,28... | collective-permute-start | bytes 294920 | tf_op jit(solution)/shard_map/ppermute | solution.py:104
  81.1 6.1 %collective-permute-start.27 = (f32[4,3,2,16,128]{4,3,2,1,0:T(8,128)S(1)}, f32[4,3,2,16,128]{4,3,2,1,0:T(8,128)S(1)}, u32[]{:S(2)}, u32[]{:S(2)}) collective-permute-start(f32[4,3,2,16,128]{4,3,2,1,0:T(8,128)S(1)} %get-tuple-element.100.refs_3_.refs_4_), channel_id=1, source_target_pairs={{0,16},{8,24},{16,0},{24,8},{1,17},{9,25},{17,1},{25,9},{2,18},{10... | collective-permute-start | bytes 589832 | tf_op jit(solution)/shard_map/ppermute | solution.py:711
  88.0 11.1 %collective-permute-start.30 = (f32[6,2,16,128]{3,2,1,0:T(8,128)S(1)}, f32[6,2,16,128]{3,2,1,0:T(8,128)S(1)}, u32[]{:S(2)}, u32[]{:S(2)}) collective-permute-start(f32[6,2,16,128]{3,2,1,0:T(8,128)S(1)} %get-tuple-element.105), channel_id=1, source_target_pairs={{0,8},{8,0},{16,24},{24,16},{1,9},{9,1},{17,25},{25,17},{2,10},{10... | collective-permute-start | bytes 294920 | tf_op jit(solution)/shard_map/ppermute | solution.py:114
  89.6 9.6 %collective-permute-start.31 = (f32[6,2,16,128]{3,2,1,0:T(8,128)S(1)}, f32[6,2,16,128]{3,2,1,0:T(8,128)S(1)}, u32[]{:S(2)}, u32[]{:S(2)}) collective-permute-start(f32[6,2,16,128]{3,2,1,0:T(8,128)S(1)} %get-tuple-element.106), channel_id=1, source_target_pairs={{8,12},{9,13},{10,14},{11,15},{12,8},{13,9},{14,10},{15,11},{24,28... | collective-permute-start | bytes 294920 | tf_op jit(solution)/shard_map/ppermute | solution.py:104
  90.3 8.9 %collective-permute-start.28 = (f32[6,16,128]{2,1,0:T(8,128)S(1)}, f32[6,16,128]{2,1,0:T(8,128)S(1)}, u32[]{:S(2)}, u32[]{:S(2)}) collective-permute-start(f32[6,16,128]{2,1,0:T(8,128)S(1)} %get-tuple-element.103), channel_id=1, source_target_pairs={{0,1},{1,0},{2,3},{3,2},{4,5},{5,4},{6,7},{7,6},{8,9},{9,8},{10,11... | collective-permute-start | bytes 147464 | tf_op jit(solution)/shard_map/ppermute | solution.py:107
  90.5 8.7 %collective-permute-start.29 = (f32[6,16,128]{2,1,0:T(8,128)S(1)}, f32[6,16,128]{2,1,0:T(8,128)S(1)}, u32[]{:S(2)}, u32[]{:S(2)}) collective-permute-start(f32[6,16,128]{2,1,0:T(8,128)S(1)} %get-tuple-element.104), channel_id=1, source_target_pairs={{0,2},{1,3},{2,0},{3,1},{4,6},{5,7},{6,4},{7,5},{8,10},{9,11},{10,... | collective-permute-start | bytes 147464 | tf_op jit(solution)/shard_map/ppermute | solution.py:108
  94.9 6.1 %collective-permute-start.32 = (f32[4,3,4,4096]{3,2,1,0:T(4,128)S(1)}, f32[4,3,4,4096]{3,2,1,0:T(4,128)S(1)}, u32[]{:S(2)}, u32[]{:S(2)}) collective-permute-start(f32[4,3,4,4096]{3,2,1,0:T(4,128)S(1)} %get-tuple-element.108), channel_id=1, source_target_pairs={{0,8},{8,0},{16,24},{24,16},{1,9},{9,1},{17,25},{25,17},{2,10},{10... | collective-permute-start | bytes 2359304 | tf_op jit(solution)/shard_map/ppermute | solution.py:114
  (15 other events, 69.3 us)
